TPU v7x, 512 devices: a 4x2x32 block of a 4x8x32 slice. The times are simulated.
512 devices in a mesh: grp: 2 (over y), freq: 32 (over z), beam: 4 (over x), dm: 2 (over core).
Axes of the slice: x: 4, y: 2, z: 32, core: 2. Of those that a mesh axis runs over, the one named last changes fastest.
The devices are a block of a 4x8x32 slice.
Arguments:
- voltages: bfloat16 [32, 256, 16, 2, 1024], P(None, ('freq', 'beam'), ('grp', 'dm')), parts along dimension 2, may hold values from -6 to 6
- grid_feed: int32 [1024], replicated, may hold values from 0 to 1023, each once
- delays: int32 [32, 256, 256], P('freq', None, 'dm'), may hold values from 0 to 4
Outputs:
- dedispersed: float32 [32, 256, 8, 1024], P('freq', 'dm', 'grp', 'beam'), parts along dimension 2
There are 2 independent parts, one for each index of `grp`. A program takes and returns all parts, laid end to end along the dimension named above; an argument that names none is the same for every part. Nothing has to cross between parts.
Inputs may be any that keep to these rules, and one draw needn't show every extreme that they name: `grid_feed`: each feed appears once.
All inputs are finite; a program needn't handle non-finite values.
Results may differ from a plain program's by a relative error of at most 0.0034.
Values may be sent and summed in bfloat16 or wider, within the bound.
No kernel may reach another device: no remote copies, remote signals or barrier semaphores. Data moves between devices by JAX's collectives and lax.ppermute only.
A program may use at most 64 MiB of HBM per device.

v0:
```python
import math

import jax
import jax.numpy as jnp
from jax import lax
from jax.sharding import PartitionSpec as P

GX = 4
GY = 256
FREQS = 8192


def laid_out(tiles, dim):
    shape = list(tiles.shape[1:])
    shape[dim] *= tiles.shape[0]
    return jnp.moveaxis(tiles, 0, dim).reshape(shape)


def from_everyone(shard, axis):
    copies = jnp.broadcast_to(shard, (lax.axis_size(axis), *shard.shape))
    return lax.all_to_all(copies, axis, split_axis=0, concat_axis=0, tiled=True)


def gathered_copies(shard, axis, dim):
    return laid_out(from_everyone(shard, axis), dim)


def steering_table(length, factor):
    position = jnp.arange(length, dtype=jnp.int32)
    phase_step = position[:, None] * position[None, :] % length
    phase_angle = phase_step.astype(jnp.float32) * (2.0 * math.pi / length)
    cosine = jnp.cos(phase_angle) * factor
    sine_part = jnp.sin(phase_angle) * factor
    upper_half = jnp.concatenate([cosine, -sine_part], axis=1)
    lower_half = jnp.concatenate([sine_part, cosine], axis=1)
    return jnp.concatenate([upper_half, lower_half], axis=0).astype(jnp.bfloat16)


def quarter_table():
    position = jnp.arange(GX, dtype=jnp.int32)
    phase_step = position[:, None] * position[None, :] % GX
    cosine = jnp.where(phase_step == 0, 1.0, jnp.where(phase_step == 2, -1.0, 0.0)) * 0.5
    sine_part = jnp.where(phase_step == 1, 1.0, jnp.where(phase_step == 3, -1.0, 0.0)) * 0.5
    real_in = jnp.stack([cosine, -sine_part], axis=2)
    imag_in = jnp.stack([sine_part, cosine], axis=2)
    return jnp.stack([real_in, imag_in], axis=1).astype(jnp.float32)


def form_power(voltages, grid_feed):
    row_count = voltages.shape[0] * voltages.shape[1] * voltages.shape[2]
    feed_count = voltages.shape[4]
    gridded = jnp.take(voltages.reshape(row_count, 2, feed_count), grid_feed, axis=2)
    gridded = jnp.transpose(gridded.reshape(row_count, 2, GX, GY), (0, 2, 1, 3)).reshape(
        row_count * GX, 2 * GY
    )
    along_y = jnp.dot(
        gridded, steering_table(GY, 1.0 / math.sqrt(GY)), preferred_element_type=jnp.float32
    ).astype(jnp.bfloat16)
    along_y = along_y.reshape(row_count, GX, 2, GY).astype(jnp.float32)
    formed = jnp.einsum("rgpy,gpbq->rbqy", along_y, quarter_table())
    intensity = 0.5 * (formed[:, :, 0, :] ** 2 + formed[:, :, 1, :] ** 2)
    return intensity.astype(jnp.bfloat16).reshape(row_count, feed_count)


def body(voltages, grid_feed, delays):
    band_count, sub_local, time_local = (voltages.shape[0], voltages.shape[1], voltages.shape[2])
    feed_count = voltages.shape[4]
    columns = lax.axis_size("beam")
    col_width = feed_count // columns
    intensity = form_power(voltages, grid_feed).reshape(
        band_count, sub_local, time_local, columns, col_width
    )
    regrouped = jnp.transpose(intensity, (0, 3, 1, 2, 4)).reshape(
        band_count * columns, sub_local, time_local, col_width
    )
    turned = lax.all_to_all(regrouped, ("freq", "beam"), split_axis=0, concat_axis=1, tiled=True)
    turned = turned.reshape(-1, time_local, col_width)
    full_time = gathered_copies(turned, "dm", 1)
    sub_count, total_time = (full_time.shape[0], full_time.shape[1])
    levels = full_time.astype(jnp.float32)
    centered = (levels - jnp.mean(levels, axis=1, keepdims=True)).astype(jnp.bfloat16)
    flattened = centered.reshape(sub_count * total_time, col_width)
    out_time = total_time // 2
    offsets = jnp.arange(out_time, dtype=jnp.int32)
    sample_ids = jnp.arange(total_time, dtype=jnp.int32)
    dm_local = delays.shape[2]
    dm_block = 32
    lag_blocks = jnp.transpose(delays[0]).reshape(dm_local // dm_block, dm_block, sub_count)

    def dedisperse(lag_rows):
        shifted = offsets[None, :, None] + lag_rows[:, None, :]
        selector = (shifted[:, :, :, None] == sample_ids[None, None, None, :]).astype(jnp.bfloat16)
        summed = jnp.dot(
            selector.reshape(dm_block * out_time, sub_count * total_time),
            flattened,
            preferred_element_type=jnp.float32,
        )
        return summed.reshape(dm_block, out_time, col_width)

    partial_sum = lax.map(dedisperse, lag_blocks).reshape(dm_local, out_time, col_width)
    cumulative = lax.all_to_all(
        jnp.cumsum(
            lax.all_to_all(partial_sum[None], "freq", split_axis=1, concat_axis=0, tiled=True),
            axis=0,
        ),
        "freq",
        split_axis=0,
        concat_axis=1,
        tiled=True,
    )
    return cumulative * (1.0 / math.sqrt(FREQS))


def solution(mesh):
    in_specs = (P(None, ("freq", "beam"), ("grp", "dm"), None, None), P(), P("freq", None, "dm"))
    out_specs = P("freq", "dm", "grp", "beam")
    return jax.shard_map(body, mesh=mesh, in_specs=in_specs, out_specs=out_specs, check_vma=False)
```

profile of v0, /device:TPU:40, one launch (start us, length us, event | category | flops | bytes accessed | tf_op | source)
XLA Modules:
  0.0 293.6 jit_solution(16959458648239387791)
XLA Ops:
  1.4 1.0 fusion.29
  2.4 1.1 negate_convert_fusion
  3.8 4.3 %copy.43 = bf16[256,2,1024]{0,1,2:T(2,128)(2,1)S(1)} copy(bf16[256,2,1024]{2,1,0:T(2,128)(2,1)} %bitcast.77) | data formatting | bytes 2097152 | tf_op jit(solution)/shard_map/reshape | solution.py:52
  8.1 4.2 %gather_fusion = bf16[1024,256,2]{1,2,0:T(2,128)(2,1)S(1)} fusion(bf16[256,2,1024]{0,1,2:T(2,128)(2,1)S(1)} %copy.43, s32[1024]{0:T(1024)S(1)} %fusion.32), kind=kCustom, calls=%fused_computation | custom fusion | bytes 2101248 | tf_op jit(solution)/shard_map/jit(_take)/gather | solution.py:52
  12.3 2.1 copy.44
  14.4 0.9 broadcast_select_fusion
  15.6 0.7 convolution_convert_fusion
  16.6 1.1 convolution_bitcast_fusion
  18.0 1.0 copy.46
  19.1 53.2 %all-to-all-start = ((bf16[128,2,4,256]{3,2,1,0:T(4,128)(2,1)}), bf16[128,2,4,256]{3,2,1,0:T(4,128)(2,1)S(1)}, u32[]{:S(2)}, u32[]{:S(2)}) async-start(bf16[128,2,4,256]{3,2,1,0:T(4,128)(2,1)} %bitcast.18), calls=%async_computation | async-start | bytes 1048576 | tf_op jit(solution)/shard_map/all_to_all | solution.py:76
  72.4 56.4 %all-to-all-done = bf16[128,2,4,256]{3,2,1,0:T(4,128)(2,1)S(1)} async-done(((bf16[128,2,4,256]{3,2,1,0:T(4,128)(2,1)}), bf16[128,2,4,256]{3,2,1,0:T(4,128)(2,1)S(1)}, u32[]{:S(2)}, u32[]{:S(2)}) %all-to-all-start) | async-done | bytes 524320 | tf_op jit(solution)/shard_map/all_to_all | solution.py:76
  129.0 4.6 %all_to_all.35 = bf16[2,256,4,256]{3,2,1,0:T(4,128)(2,1)S(1)} all-to-all(bf16[2,256,4,256]{3,2,1,0:T(4,128)(2,1)S(1)} %broadcast_in_dim.54), channel_id=1, replica_groups=mesh['grp'=2,'freq'=32,'beam'=4,'dm'=2] {'dm'}, dimensions={0} | all-to-all | bytes 2097152 | tf_op jit(solution)/shard_map/all_to_all | solution.py:21
  133.6 0.8 convert_reduce_fusion
  134.8 1.7 copy.47
  136.5 2.0 reshape.194
  138.8 9.9 %while.11 = (s32[]{:T(128)}, f32[4,32,4,256]{3,1,0,2:T(8,128)}, s32[4,32,256]{2,1,0:T(8,128)S(1)}, bf16[2048,256]{1,0:T(8,128)(2,1)S(1)}, s32[]{:T(128)}) while((s32[]{:T(128)}, f32[4,32,4,256]{3,1,0,2:T(8,128)}, s32[4,32,256]{2,1,0:T(8,128)S(1)}, bf16[2048,256]{1,0:T(8,128)(2,1)S(1)}, s32[]{:T(128)}) %tuple.30), condition=%wide.region_2.3_spmd.clone, body=%wide.region_1.2_spmd.clone.sunk | while | flops 134512640 | bytes 1638477 | solution.py:100
  139.1 2.2 fusion.43
  141.6 2.2 fusion.43
  144.0 2.2 fusion.43
  146.5 2.2 fusion.43
  148.7 1.4 copy.50
  150.1 74.6 %all_to_all.36 = f32[1,128,4,256]{3,2,0,1:T(4,128)S(1)} all-to-all(f32[1,128,4,256]{3,2,0,1:T(4,128)S(1)} %copy.50), channel_id=1, replica_groups=mesh['grp'=2,'freq'=32,'beam'=4,'dm'=2] {'freq'}, dimensions={1} | all-to-all | bytes 1048576 | tf_op jit(solution)/shard_map/all_to_all | solution.py:103
  224.7 67.9 %all_to_all.37 = f32[32,4,4,256]{3,2,1,0:T(4,128)S(1)} all-to-all(f32[32,4,4,256]{3,2,1,0:T(4,128)S(1)} %fusion.37), channel_id=1, replica_groups=mesh['grp'=2,'freq'=32,'beam'=4,'dm'=2] {'freq'}, dimensions={0} | all-to-all | bytes 1048576 | tf_op jit(solution)/shard_map/all_to_all | solution.py:101
  292.7 0.9 broadcast_multiply_fusion
  (40 shorter events, 4.6 us)
Async XLA Ops:
  17.7 54.6 %copy-start = (s32[1,256,128]{2,1,0:T(8,128)S(1)}, s32[1,256,128]{2,1,0:T(8,128)}, u32[]{:S(2)}) copy-start(s32[1,256,128]{2,1,0:T(8,128)} %param.7) | copy-start | bytes 393220
  19.1 109.7 %all-to-all-start = ((bf16[128,2,4,256]{3,2,1,0:T(4,128)(2,1)}), bf16[128,2,4,256]{3,2,1,0:T(4,128)(2,1)S(1)}, u32[]{:S(2)}, u32[]{:S(2)}) async-start(bf16[128,2,4,256]{3,2,1,0:T(4,128)(2,1)} %bitcast.18), calls=%async_computation | async-start | bytes 1048576 | tf_op jit(solution)/shard_map/all_to_all | solution.py:76
where the time goes:
time: 294 us
  blocking collectives  147 us (50%)
  waiting for transfers between devices  56.4 us (19%)
  starting transfers between devices  53.2 us (18%)
  local copies, waits for them, and re-layouts  18.8 us (6%)
  matrix products  10.6 us (4%)
  other arithmetic  7.38 us (3%)
    all_to_all x1, blocking collectives, body(): lax.all_to_all(partial_sum[None], 'freq', split_axis=1, concat_axis=0, ti...  74.6 us
    all_to_all x1, blocking collectives, body(): lax.all_to_all(jnp.cumsum(lax.all_to_all(partial_sum[None], 'freq', split...  67.9 us
    all_to_all x1, waiting for transfers between devices, body(): lax.all_to_all(regrouped, ('freq', 'beam'), split_axis=0, concat_axis=1,...  56.4 us
    all_to_all x1, starting transfers between devices, body(): lax.all_to_all(regrouped, ('freq', 'beam'), split_axis=0, concat_axis=1,...  53.2 us
    dot_general x4, matrix products, dedisperse(): jnp.dot(selector.reshape(dm_block * out_time, sub_count * total_time), fl...  8.82 us
    gather x2, local copies, waits for them, and re-layouts, form_power(): jnp.take(voltages.reshape(row_count, 2, feed_count), grid_feed, axis=2)  6.28 us
  transfers between devices with their start and end apart: 1, of which 1 were waited for; matrix products, arithmetic and copies ran while one was open for 0% of the time, Pallas kernels for 0%

commit v1 on v0

--- a/solution.py
+++ b/solution.py
@@ -98,17 +98,11 @@
         return summed.reshape(dm_block, out_time, col_width)
 
     partial_sum = lax.map(dedisperse, lag_blocks).reshape(dm_local, out_time, col_width)
-    cumulative = lax.all_to_all(
-        jnp.cumsum(
-            lax.all_to_all(partial_sum[None], "freq", split_axis=1, concat_axis=0, tiled=True),
-            axis=0,
-        ),
-        "freq",
-        split_axis=0,
-        concat_axis=1,
-        tiled=True,
-    )
-    return cumulative * (1.0 / math.sqrt(FREQS))
+    sent = partial_sum.astype(jnp.bfloat16)
+    bands = lax.all_to_all(sent[None], "freq", split_axis=1, concat_axis=0, tiled=True)
+    sums = jnp.cumsum(bands.astype(jnp.float32), axis=0).astype(jnp.bfloat16)
+    cumulative = lax.all_to_all(sums, "freq", split_axis=0, concat_axis=1, tiled=True)
+    return cumulative.astype(jnp.float32) * (1.0 / math.sqrt(FREQS))
 
 
 def solution(mesh):

time: 294 us -> 249 us (0.85)
  blocking collectives: 147 us -> 102 us
    all_to_all x2, blocking collectives: 142 us -> 97.4 us  [the longest x1 52.1 us: body(): lax.all_to_all(sent[None], 'freq', split_axis=1, concat_axis=0, tiled=True)]
where the time goes in v1:
time: 249 us; the launch traced here: 248 us
  blocking collectives  102 us (41%)
  waiting for transfers between devices  56.4 us (23%)
  starting transfers between devices  53.2 us (21%)
  local copies, waits for them, and re-layouts  18.5 us (7%)
  matrix products  10.5 us (4%)
  other arithmetic  7.4 us (3%)
    all_to_all x1, waiting for transfers between devices, body(): lax.all_to_all(regrouped, ('freq', 'beam'), split_axis=0, concat_axis=1,...  56.4 us
    all_to_all x1, starting transfers between devices, body(): lax.all_to_all(regrouped, ('freq', 'beam'), split_axis=0, concat_axis=1,...  53.2 us
    all_to_all x1, blocking collectives, body(): lax.all_to_all(sent[None], 'freq', split_axis=1, concat_axis=0, tiled=True)  52.1 us
    all_to_all x1, blocking collectives, body(): lax.all_to_all(sums, 'freq', split_axis=0, concat_axis=1, tiled=True)  45.3 us
    dot_general x4, matrix products, dedisperse(): jnp.dot(selector.reshape(dm_block * out_time, sub_count * total_time), fl...  8.72 us
    gather x2, local copies, waits for them, and re-layouts, form_power(): jnp.take(voltages.reshape(row_count, 2, feed_count), grid_feed, axis=2)  6.28 us
  transfers between devices with their start and end apart: 1, of which 1 were waited for; matrix products, arithmetic and copies ran while one was open for 0% of the time, Pallas kernels for 0%

profile of v1, /device:TPU:40, one launch (start us, length us, event | category | flops | bytes accessed | tf_op | source)
XLA Modules:
  0.0 248.2 jit_solution(14296487391771209717)
XLA Ops:
  1.4 1.0 fusion.31
  2.4 1.1 negate_convert_fusion
  3.8 4.3 %copy.43 = bf16[256,2,1024]{0,1,2:T(2,128)(2,1)S(1)} copy(bf16[256,2,1024]{2,1,0:T(2,128)(2,1)} %bitcast.76) | data formatting | bytes 2097152 | tf_op jit(solution)/shard_map/reshape | solution.py:52
  8.1 4.2 %gather_fusion = bf16[1024,256,2]{1,2,0:T(2,128)(2,1)S(1)} fusion(bf16[256,2,1024]{0,1,2:T(2,128)(2,1)S(1)} %copy.43, s32[1024]{0:T(1024)S(1)} %fusion.34), kind=kCustom, calls=%fused_computation | custom fusion | bytes 2101248 | tf_op jit(solution)/shard_map/jit(_take)/gather | solution.py:52
  12.3 2.1 copy.44
  14.4 0.9 broadcast_select_fusion
  15.6 0.7 convolution_convert_fusion
  16.6 1.1 convolution_bitcast_fusion
  18.0 1.1 copy.46
  19.1 53.2 %all-to-all-start = ((bf16[128,2,4,256]{3,2,1,0:T(4,128)(2,1)}), bf16[128,2,4,256]{3,2,1,0:T(4,128)(2,1)S(1)}, u32[]{:S(2)}, u32[]{:S(2)}) async-start(bf16[128,2,4,256]{3,2,1,0:T(4,128)(2,1)} %bitcast.18), calls=%async_computation | async-start | bytes 1048576 | tf_op jit(solution)/shard_map/all_to_all | solution.py:76
  72.4 56.4 %all-to-all-done = bf16[128,2,4,256]{3,2,1,0:T(4,128)(2,1)S(1)} async-done(((bf16[128,2,4,256]{3,2,1,0:T(4,128)(2,1)}), bf16[128,2,4,256]{3,2,1,0:T(4,128)(2,1)S(1)}, u32[]{:S(2)}, u32[]{:S(2)}) %all-to-all-start) | async-done | bytes 524320 | tf_op jit(solution)/shard_map/all_to_all | solution.py:76
  129.1 4.6 %all_to_all.32 = bf16[2,256,4,256]{3,2,1,0:T(4,128)(2,1)S(1)} all-to-all(bf16[2,256,4,256]{3,2,1,0:T(4,128)(2,1)S(1)} %broadcast_in_dim.55), channel_id=1, replica_groups=mesh['grp'=2,'freq'=32,'beam'=4,'dm'=2] {'dm'}, dimensions={0} | all-to-all | bytes 2097152 | tf_op jit(solution)/shard_map/all_to_all | solution.py:21
  133.7 0.8 convert_reduce_fusion
  134.8 1.7 copy.47
  136.5 2.0 reshape.213
  138.8 9.8 %while.11 = (s32[]{:T(128)}, bf16[4,32,4,256]{3,1,0,2:T(8,128)(2,1)}, s32[4,32,256]{2,1,0:T(8,128)S(1)}, bf16[2048,256]{1,0:T(8,128)(2,1)S(1)}, s32[]{:T(128)}) while((s32[]{:T(128)}, bf16[4,32,4,256]{3,1,0,2:T(8,128)(2,1)}, s32[4,32,256]{2,1,0:T(8,128)S(1)}, bf16[2048,256]{1,0:T(8,128)(2,1)S(1)}, s32[]{:T(128)}) %tuple.30), condition=%wide.region_2.3_spmd.clone, body=%wide.region_1.2_spmd.clone.sunk | while | flops 134512640 | bytes 1638477 | solution.py:100
  139.1 2.2 fusion.43
  141.5 2.2 fusion.43
  144.0 2.2 fusion.43
  146.5 2.2 fusion.43
  148.6 1.2 copy.50
  149.8 52.1 %all_to_all.33 = bf16[1,128,4,256]{3,2,0,1:T(4,128)(2,1)S(1)} all-to-all(bf16[1,128,4,256]{3,2,0,1:T(4,128)(2,1)S(1)} %copy.50), channel_id=1, replica_groups=mesh['grp'=2,'freq'=32,'beam'=4,'dm'=2] {'freq'}, dimensions={1} | all-to-all | bytes 524288 | tf_op jit(solution)/shard_map/all_to_all | solution.py:102
  202.0 45.3 %all_to_all.34 = bf16[32,4,4,256]{3,2,1,0:T(4,128)(2,1)S(1)} all-to-all(bf16[32,4,4,256]{3,2,1,0:T(4,128)(2,1)S(1)} %fusion.23), channel_id=1, replica_groups=mesh['grp'=2,'freq'=32,'beam'=4,'dm'=2] {'freq'}, dimensions={0} | all-to-all | bytes 524288 | tf_op jit(solution)/shard_map/all_to_all | solution.py:104
  247.3 0.9 convert_multiply_fusion
  (40 shorter events, 4.7 us)
Async XLA Ops:
  17.7 54.6 %copy-start = (s32[1,256,128]{2,1,0:T(8,128)S(1)}, s32[1,256,128]{2,1,0:T(8,128)}, u32[]{:S(2)}) copy-start(s32[1,256,128]{2,1,0:T(8,128)} %param.7) | copy-start | bytes 393220
  19.1 109.7 %all-to-all-start = ((bf16[128,2,4,256]{3,2,1,0:T(4,128)(2,1)}), bf16[128,2,4,256]{3,2,1,0:T(4,128)(2,1)S(1)}, u32[]{:S(2)}, u32[]{:S(2)}) async-start(bf16[128,2,4,256]{3,2,1,0:T(4,128)(2,1)} %bitcast.18), calls=%async_computation | async-start | bytes 1048576 | tf_op jit(solution)/shard_map/all_to_all | solution.py:76

commit v2 on v1

v2 whole, which is shorter than its diff:
```python
import functools
import math

import jax
import jax.numpy as jnp
import numpy as np
from jax import lax
from jax.experimental import pallas as pl
from jax.experimental.pallas import tpu as pltpu
from jax.sharding import Mesh
from jax.sharding import PartitionSpec as P


GX = 4
GY = 256
FREQS = 8192
LAGS = 5
LANES = 128
BF16 = jnp.bfloat16
F32 = jnp.float32


def steering_table(length):
    position = np.arange(length)
    angle = (position[:, None] * position[None, :] % length) * (2.0 * math.pi / length)
    cosine = np.cos(angle) / math.sqrt(length)
    sine = np.sin(angle) / math.sqrt(length)
    upper = np.concatenate([cosine, -sine], axis=1)
    lower = np.concatenate([sine, cosine], axis=1)
    return np.concatenate([upper, lower], axis=0).astype(BF16)


def iota(shape, dim):
    return lax.broadcasted_iota(jnp.int32, shape, dim)


def lane_blocks(arrays, width, shift):
    count = len(arrays)
    block = iota(arrays[0].shape, 1) // width
    result = None
    for i, array in enumerate(arrays):
        amount = (i - shift) % count * width
        moved = pltpu.roll(array, amount, 1) if amount else array
        result = moved if result is None else jnp.where(block == i, moved, result)
    return result


def front_kernel(times, blocks, near, beams, volt_ref, feed_ref, table_ref, out_ref, along_ref):
    rows, feeds = volt_ref.shape
    half = rows // 2
    chans = half // times
    tall = chans // blocks
    i = iota((rows, rows), 0)
    source = i % chans * (2 * times) + i // chans % times * 2 + i // half
    order = jnp.where(iota((rows, rows), 1) == source, 1.0, 0.0).astype(BF16)
    planes = jnp.dot(order, volt_ref[...], preferred_element_type=F32).astype(BF16)
    pick = jnp.where(iota((feeds, feeds), 0) == feed_ref[...], 1.0, 0.0).astype(BF16)
    grid = jnp.dot(planes, pick, preferred_element_type=F32).astype(BF16)
    for gx in range(GX):
        cells = slice(gx * GY, (gx + 1) * GY)
        paired = jnp.concatenate([grid[:half, cells], grid[half:, cells]], axis=1)
        along = jnp.dot(paired, table_ref[...], preferred_element_type=F32)
        along_ref[gx] = along.astype(BF16)
    per_tile = LANES // beams
    for block in range(blocks):
        for tile in range(GY // LANES):
            power = [[] for _ in range(GX)]
            for t in range(times):
                r = pl.ds(t * chans + block * tall, tall)
                re = [along_ref[gx, r, pl.ds(tile * LANES, LANES)].astype(F32) for gx in range(GX)]
                im = [along_ref[gx, r, pl.ds(GY + tile * LANES, LANES)].astype(F32) for gx in range(GX)]
                er, ei, orr, oi = re[0] + re[2], im[0] + im[2], re[1] + re[3], im[1] + im[3]
                dr, di, ur, ui = re[0] - re[2], im[0] - im[2], re[1] - re[3], im[1] - im[3]
                formed = [(er + orr, ei + oi), (dr + ui, di - ur), (er - orr, ei - oi), (dr - ui, di + ur)]
                for bx, (fr, fi) in enumerate(formed):
                    fr, fi = 0.5 * fr, 0.5 * fi
                    power[bx].append(0.5 * (fr * fr + fi * fi))
            for bx in range(GX):
                for part in range(per_tile):
                    peer = (block * near + tile * per_tile + part) * GX + bx
                    out_ref[peer] = lane_blocks(power[bx], beams, part).astype(BF16)


def dedisperse_kernel(beams, core_ref, own_ref, other_ref, lag_ref, out_ref, level_ref):
    sources, tall, width = own_ref.shape
    bands = out_ref.shape[0]
    subs = tall // bands
    chunk = 8
    low = core_ref[0] == 0

    def center(i, carry):
        mine = own_ref[pl.ds(i * chunk, chunk)].astype(F32).reshape(chunk * tall, width)
        theirs = other_ref[pl.ds(i * chunk, chunk)].astype(F32).reshape(chunk * tall, width)
        early = jnp.where(low, mine, theirs)
        late = jnp.where(low, theirs, mine)
        total = early + late
        amount = width // 2
        while amount >= beams:
            total = total + pltpu.roll(total, amount, 1)
            amount //= 2
        mean = total * (0.5 * beams / width)
        r = pl.ds(pl.multiple_of(i * (chunk * tall), chunk * tall), chunk * tall)
        level_ref[0, r, :] = early - mean
        level_ref[1, r, :] = late - mean
        return carry

    lax.fori_loop(0, sources // chunk, center, 0)
    lane = iota((out_ref.shape[1], width), 1)
    running = None
    for b in range(bands):
        rows = []
        for s in range(subs):
            r = pl.ds(b * subs + s, sources, stride=tall)
            rows.append(jnp.concatenate([level_ref[0, r, :].astype(BF16), level_ref[1, r, :].astype(BF16)], axis=1))
        data = jnp.concatenate(rows, axis=0)
        lags = lag_ref[b].astype(F32)
        chosen = [jnp.where(lags == float(v), 1.0, 0.0).astype(BF16) for v in range(LAGS)]
        for v in range(LAGS):
            picked = jnp.dot(chosen[v], data, preferred_element_type=F32)
            first, second = picked[:, :width], picked[:, width:]
            offset = v * beams
            if offset == 0:
                part = first
            elif offset == width:
                part = second
            else:
                back = width - offset
                part = jnp.where(lane < back, pltpu.roll(first, back, 1), pltpu.roll(second, back, 1))
            running = part if running is None else running + part
        out_ref[b] = running


def spread_kernel(beams, scale, in_ref, out_ref):
    slabs, trials, width = in_ref.shape
    count = width // beams
    for tile in range(slabs // count):
        parts = [in_ref[tile * count + i].astype(F32) * scale for i in range(count)]
        for t in range(count):
            out_ref[pl.ds(tile * count + t, trials, stride=slabs), :] = lane_blocks(parts, beams, t)


def search(voltages, grid_feed, delays):
    bands, sub_local, times = voltages.shape[:3]
    feeds = voltages.shape[4]
    blocks, near, columns = lax.axis_size("far"), lax.axis_size("near"), lax.axis_size("beam")
    peers = blocks * near * columns
    beams = feeds // columns // near
    trials = delays.shape[2]
    subs = delays.shape[1]
    tall = bands // blocks * sub_local
    rows = bands * sub_local * times * 2
    vmem = pl.BlockSpec(memory_space=pltpu.VMEM)

    lag_rows = delays[0].astype(BF16).reshape(peers, sub_local, trials)
    lag_rows = jnp.transpose(lag_rows, (2, 1, 0)).reshape(columns, trials // columns, subs)
    lag_part = lax.dynamic_index_in_dim(lag_rows, lax.axis_index("beam"), 0, keepdims=False)

    sent = pl.pallas_call(
        functools.partial(front_kernel, times, blocks, near, beams),
        out_shape=jax.ShapeDtypeStruct((peers, tall, times * beams), BF16),
        in_specs=[vmem] * 3,
        out_specs=vmem,
        scratch_shapes=[pltpu.VMEM((GX, rows // 2, 2 * GY), BF16)],
        cost_estimate=pl.CostEstimate(flops=2 * 10**9, bytes_accessed=4 * 10**6, transcendentals=0),
        name="front",
    )(voltages.reshape(rows, feeds), grid_feed.reshape(1, feeds), jnp.asarray(steering_table(GY)))
    own = lax.all_to_all(sent, ("far", "near", "beam"), split_axis=0, concat_axis=0, tiled=True)
    lag_near = lax.all_gather(lag_part, "near")
    lags = lax.all_gather(lag_near, "beam")
    lags = jnp.transpose(lags, (1, 0, 2, 3)).reshape(near, trials, subs)
    other = lax.ppermute(own, "dm", [(0, 1), (1, 0)])
    core = lax.axis_index("dm").astype(jnp.int32).reshape(1)
    local = pl.pallas_call(
        functools.partial(dedisperse_kernel, beams),
        out_shape=jax.ShapeDtypeStruct((bands // blocks, trials, times * beams), F32),
        in_specs=[pl.BlockSpec(memory_space=pltpu.SMEM)] + [vmem] * 3,
        out_specs=vmem,
        scratch_shapes=[pltpu.VMEM((2, peers * tall, times * beams), F32)],
        cost_estimate=pl.CostEstimate(flops=2 * 10**9, bytes_accessed=4 * 10**6, transcendentals=0),
        name="dedisperse",
    )(core, own, other, lags)
    total = local[-1]
    base = jnp.zeros_like(total)
    for k in range(blocks - 1):
        message = (base + total).astype(BF16)
        base = base + lax.ppermute(message, "far", [(k, k + 1)]).astype(F32)
    cumulative = (local + base).astype(BF16)
    slabs = lax.all_to_all(cumulative, "near", split_axis=0, concat_axis=0, tiled=True)
    spread = pl.pallas_call(
        functools.partial(spread_kernel, beams, 1.0 / math.sqrt(FREQS)),
        out_shape=jax.ShapeDtypeStruct((trials * near, LANES), F32),
        in_specs=[vmem],
        out_specs=vmem,
        name="spread",
    )(slabs)
    spread = jnp.transpose(spread.reshape(trials, near // times, times, LANES), (0, 2, 1, 3))
    return spread.reshape(1, trials, times, near * beams)


def solution(mesh):
    near = 8
    sizes = mesh.shape
    devices = mesh.devices.reshape(sizes["grp"], sizes["freq"] // near, near, sizes["beam"], sizes["dm"])
    split = Mesh(devices, ("grp", "far", "near", "beam", "dm"))
    freq = ("far", "near")
    in_specs = (P(None, (*freq, "beam"), ("grp", "dm"), None, None), P(), P(freq, None, "dm"))
    out_specs = P(freq, "dm", "grp", "beam")
    return jax.shard_map(search, mesh=split, in_specs=in_specs, out_specs=out_specs, check_vma=False)
```

time: 249 us -> 220 us (0.88)
  blocking collectives: 102 us -> 188 us
  waiting for transfers between devices: 56.4 us -> 1.77 us
  starting transfers between devices: 53.2 us -> 7.81 us
  Pallas kernels: 0 us -> 14.1 us
  local copies, waits for them, and re-layouts: 18.5 us -> 4.92 us
  matrix products: 10.5 us -> 0 us
  other arithmetic: 7.4 us -> 2.82 us
    all_gather x0 -> x2, blocking collectives: none -> 62.3 us  [the longest x1 46.4 us: search(): lag_near = lax.all_gather(lag_part, 'near')]
    all_to_all x1 -> x0, waiting for transfers between devices: 56.4 us -> none  [body(): lax.all_to_all(regrouped, ('freq', 'beam'), split_axis=0, concat_axis=1,...]
    all_to_all x1 -> x0, starting transfers between devices: 53.2 us -> none  [body(): lax.all_to_all(regrouped, ('freq', 'beam'), split_axis=0, concat_axis=1,...]
    all_to_all x3 -> x2, blocking collectives: 102 us -> 126 us  [the longest x1 110 us: search(): lax.all_to_all(sent, ('far', 'near', 'beam'), split_axis=0, concat_axis=0...]
    pallas_call x0 -> x3, Pallas kernels: none -> 14.1 us  [the longest x1 6.67 us: search(): pl.pallas_call(functools.partial(dedisperse_kernel, beams), out_shape=jax...]
    dot_general x6 -> x0, matrix products: 10.5 us -> none  [the longest x4 8.72 us: dedisperse(): jnp.dot(selector.reshape(dm_block * out_time, sub_count * total_time), fl...]
    ppermute x0 -> x4, starting transfers between devices: none -> 7.81 us  [the longest x3 5.87 us: search(): base = base + lax.ppermute(message, 'far', [(k, k + 1)]).astype(F32)]
    gather x2 -> x0, local copies, waits for them, and re-layouts: 6.28 us -> none  [form_power(): jnp.take(voltages.reshape(row_count, 2, feed_count), grid_feed, axis=2)]
  transfers between devices with their start and end apart: 1 -> 4, of which waited for: 1 -> 1; matrix products, arithmetic and copies ran while one was open for 0% -> 0% of each run, Pallas kernels for 0% -> 0%
where the time goes in v2:
time: 220 us
  blocking collectives  188 us (85%)
  Pallas kernels  14.1 us (6%)
  starting transfers between devices  7.81 us (4%)
  local copies, waits for them, and re-layouts  4.92 us (2%)
  other arithmetic  2.82 us (1%)
    all_to_all x1, blocking collectives, search(): lax.all_to_all(sent, ('far', 'near', 'beam'), split_axis=0, concat_axis=0...  110 us
    all_gather x1, blocking collectives, search(): lag_near = lax.all_gather(lag_part, 'near')  46.4 us
    all_to_all x1, blocking collectives, search(): lax.all_to_all(cumulative, 'near', split_axis=0, concat_axis=0, tiled=True)  16.2 us
    all_gather x1, blocking collectives, search(): lags = lax.all_gather(lag_near, 'beam')  15.9 us
    pallas_call x1, Pallas kernels, search(): pl.pallas_call(functools.partial(dedisperse_kernel, beams), out_shape=jax...  6.67 us
    ppermute x3, starting transfers between devices, search(): base = base + lax.ppermute(message, 'far', [(k, k + 1)]).astype(F32)  5.87 us
    pallas_call x1, Pallas kernels, search(): pl.pallas_call(functools.partial(front_kernel, times, blocks, near, beams...  5.16 us
  transfers between devices with their start and end apart: 4, of which 1 were waited for; matrix products, arithmetic and copies ran while one was open for 0% of the time, Pallas kernels for 0%

profile of v2, /device:TPU:40, one launch (start us, length us, event | category | flops | bytes accessed | tf_op | source)
XLA Modules:
  0.0 219.8 jit_solution(14893423928747135686)
XLA Ops:
  0.0 2.2 %reshape.26.volt_ref = bf16[512,1024]{1,0:T(8,128)(2,1)} reshape(bf16[32,2,4,2,1024]{4,3,2,1,0:T(2,128)(2,1)} %param.4) | data formatting | bytes 2097152 | tf_op jit(solution)/shard_map/reshape | solution.py:166
  2.3 5.2 %front.1 = bf16[128,16,128]{2,1,0:T(8,128)(2,1)} custom-call(bf16[512,1024]{1,0:T(8,128)(2,1)} %reshape.26.volt_ref, s32[1,1024]{1,0:T(1,128)} %bitcast.25, bf16[512,512]{1,0:T(8,128)(2,1)} %constant.16.clone.table_ref), custom_call_target="tpu_custom_call" | custom-call | flops 2000000000 | bytes 4000000 | tf_op jit(solution)/shard_map/front/pallas_call | solution.py:158
  7.4 109.8 %all_to_all.10.own_ref = bf16[128,16,128]{2,1,0:T(8,128)(2,1)S(1)} all-to-all(bf16[128,16,128]{2,1,0:T(8,128)(2,1)} %front.1), channel_id=1, replica_groups=mesh['grp'=2,'far'=4,'near'=8,'beam'=4,'dm'=2] {'far','near','beam'}, dimensions={0} | all-to-all | bytes 1048576 | tf_op jit(solution)/shard_map/all_to_all | solution.py:167
  117.2 1.9 collective-permute-start
  119.2 0.0 copy-done.1
  119.2 0.1 copy.9
  119.4 46.4 %all_gather.10 = bf16[8,32,256]{2,1,0:T(8,128)(2,1)S(1)} all-gather(bf16[1,32,256]{2,1,0:T(8,128)(2,1)S(1)} %constant_dynamic-slice_fusion), channel_id=1, replica_groups=mesh['grp'=2,'far'=4,'near'=8,'beam'=4,'dm'=2] {'near'}, dimensions={0}, use_global_device_ids=true | all-gather | bytes 147456 | tf_op jit(solution)/shard_map/all_gather | solution.py:168
  165.8 15.9 %all-gather = bf16[32,32,256]{2,1,0:T(8,128)(2,1)S(1)} all-gather(bf16[8,32,256]{2,1,0:T(8,128)(2,1)S(1)} %all_gather.10), channel_id=2, replica_groups=mesh['grp'=2,'far'=4,'near'=8,'beam'=4,'dm'=2] {'beam'}, dimensions={0}, use_global_device_ids=true | all-gather | bytes 655360 | tf_op jit(solution)/shard_map/all_gather | solution.py:169
  181.7 0.8 copy.10
  182.5 0.0 collective-permute-done.other_ref
  182.5 0.8 copy-done.2
  183.3 6.7 %dedisperse.1 = f32[8,128,128]{2,1,0:T(8,128)} custom-call(s32[1]{0:T(128)} %bitcast.core_ref, bf16[128,16,128]{2,1,0:T(8,128)(2,1)} %copy-done, bf16[128,16,128]{2,1,0:T(8,128)(2,1)} %copy-done.2, bf16[8,128,256]{2,1,0:T(8,128)(2,1)} %bitcast.22), custom_call_target="tpu_custom_call" | custom-call | flops 2000000000 | bytes 4000000 | tf_op jit(solution)/shard_map/dedisperse/pallas_call | solution.py:173
  190.0 0.8 fusion.1
  190.8 4.5 %collective-permute-start.1 = (bf16[128,128]{1,0:T(8,128)(2,1)S(1)}, bf16[128,128]{1,0:T(8,128)(2,1)S(1)}, u32[]{:S(2)}, u32[]{:S(2)}) collective-permute-start(bf16[128,128]{1,0:T(8,128)(2,1)S(1)} %fusion.1), channel_id=1, source_target_pairs={{0,64},{1,65},{2,66},{3,67},{4,68},{5,69},{6,70},{7,71},{8,72},{9,... | collective-permute-start | bytes 98312 | tf_op jit(solution)/shard_map/ppermute | solution.py:186
  195.4 1.8 collective-permute-done.1
  197.1 0.8 fusion
  198.0 0.7 collective-permute-start.2
  198.7 0.0 collective-permute-done.2
  198.7 0.9 add_convert_fusion.1
  199.5 0.7 collective-permute-start.3
  200.2 0.0 collective-permute-done.3
  200.2 1.1 add_convert_fusion
  201.3 16.2 %all_to_all.11.in_ref = bf16[8,128,128]{2,1,0:T(8,128)(2,1)} all-to-all(bf16[8,128,128]{2,1,0:T(8,128)(2,1)S(1)} %add_convert_fusion), channel_id=1, replica_groups=mesh['grp'=2,'far'=4,'near'=8,'beam'=4,'dm'=2] {'near'}, dimensions={0} | all-to-all | bytes 524288 | tf_op jit(solution)/shard_map/all_to_all | solution.py:188
  217.6 2.2 %spread.1 = f32[1024,128]{1,0:T(8,128)} custom-call(bf16[8,128,128]{2,1,0:T(8,128)(2,1)} %all_to_all.11.in_ref), custom_call_target="tpu_custom_call" | custom-call | tf_op jit(solution)/shard_map/spread/pallas_call | solution.py:189
  (8 shorter events, 0.1 us)
Async XLA Ops:
  7.4 111.8 %copy-start.1 = (s32[1,256,128]{2,1,0:T(8,128)S(1)}, s32[1,256,128]{2,1,0:T(8,128)}, u32[]{:S(2)}) copy-start(s32[1,256,128]{2,1,0:T(8,128)} %param.6) | copy-start | bytes 393220
  117.2 64.5 %copy-start = (bf16[128,16,128]{2,1,0:T(8,128)(2,1)}, bf16[128,16,128]{2,1,0:T(8,128)(2,1)S(1)}, u32[]{:S(2)}) copy-start(bf16[128,16,128]{2,1,0:T(8,128)(2,1)S(1)} %all_to_all.10.own_ref) | copy-start | bytes 1572868
  117.2 65.3 %collective-permute-start = (bf16[128,16,128]{2,1,0:T(8,128)(2,1)S(1)}, bf16[128,16,128]{2,1,0:T(8,128)(2,1)S(1)}, u32[]{:S(2)}, u32[]{:S(2)}) collective-permute-start(bf16[128,16,128]{2,1,0:T(8,128)(2,1)S(1)} %all_to_all.10.own_ref), channel_id=1, source_target_pairs={{0,1},{1,0},{2,3},{3,2},{4,5},{5,4},{6,7},{7,6},{8,9},{9,8},{10,11... | collective-permute-start | bytes 1572872 | tf_op jit(solution)/shard_map/ppermute | solution.py:171
  182.5 0.8 copy-start.2
  190.8 6.3 %collective-permute-start.1 = (bf16[128,128]{1,0:T(8,128)(2,1)S(1)}, bf16[128,128]{1,0:T(8,128)(2,1)S(1)}, u32[]{:S(2)}, u32[]{:S(2)}) collective-permute-start(bf16[128,128]{1,0:T(8,128)(2,1)S(1)} %fusion.1), channel_id=1, source_target_pairs={{0,64},{1,65},{2,66},{3,67},{4,68},{5,69},{6,70},{7,71},{8,72},{9,... | collective-permute-start | bytes 98312 | tf_op jit(solution)/shard_map/ppermute | solution.py:186
  198.0 0.7 collective-permute-start.2
  199.5 0.7 collective-permute-start.3

commit v3 on v2

--- a/solution.py
+++ b/solution.py
@@ -46,14 +46,14 @@
 
 
 def front_kernel(times, blocks, near, beams, volt_ref, feed_ref, table_ref, out_ref, along_ref):
-    rows, feeds = volt_ref.shape
+    rows, feeds = 2 * volt_ref.shape[0], volt_ref.shape[2]
     half = rows // 2
     chans = half // times
     tall = chans // blocks
     i = iota((rows, rows), 0)
     source = i % chans * (2 * times) + i // chans % times * 2 + i // half
     order = jnp.where(iota((rows, rows), 1) == source, 1.0, 0.0).astype(BF16)
-    planes = jnp.dot(order, volt_ref[...], preferred_element_type=F32).astype(BF16)
+    planes = jnp.dot(order, volt_ref[...].reshape(rows, feeds), preferred_element_type=F32).astype(BF16)
     pick = jnp.where(iota((feeds, feeds), 0) == feed_ref[...], 1.0, 0.0).astype(BF16)
     grid = jnp.dot(planes, pick, preferred_element_type=F32).astype(BF16)
     for gx in range(GX):
@@ -81,12 +81,18 @@
                     out_ref[peer] = lane_blocks(power[bx], beams, part).astype(BF16)
 
 
-def dedisperse_kernel(beams, core_ref, own_ref, other_ref, lag_ref, out_ref, level_ref):
+def dedisperse_kernel(beams, place_ref, own_any, other_any, lag_any, out_ref, total_ref, own_ref, other_ref, lag_ref, level_ref, sems):
+    pairs = ((own_any, own_ref), (other_any, other_ref), (lag_any, lag_ref))
+    copies = [pltpu.make_async_copy(a, b, sems.at[i]) for i, (a, b) in enumerate(pairs)]
+    for copy in copies:
+        copy.start()
+    for copy in copies:
+        copy.wait()
     sources, tall, width = own_ref.shape
     bands = out_ref.shape[0]
     subs = tall // bands
     chunk = 8
-    low = core_ref[0] == 0
+    low = place_ref[0] == 0
 
     def center(i, carry):
         mine = own_ref[pl.ds(i * chunk, chunk)].astype(F32).reshape(chunk * tall, width)
@@ -113,7 +119,7 @@
             r = pl.ds(b * subs + s, sources, stride=tall)
             rows.append(jnp.concatenate([level_ref[0, r, :].astype(BF16), level_ref[1, r, :].astype(BF16)], axis=1))
         data = jnp.concatenate(rows, axis=0)
-        lags = lag_ref[b].astype(F32)
+        lags = lag_ref[lax.rem(b + bands - place_ref[1], bands)].astype(F32)
         chosen = [jnp.where(lags == float(v), 1.0, 0.0).astype(BF16) for v in range(LAGS)]
         for v in range(LAGS):
             picked = jnp.dot(chosen[v], data, preferred_element_type=F32)
@@ -128,6 +134,7 @@
                 part = jnp.where(lane < back, pltpu.roll(first, back, 1), pltpu.roll(second, back, 1))
             running = part if running is None else running + part
         out_ref[b] = running
+    total_ref[...] = running
 
 
 def spread_kernel(beams, scale, in_ref, out_ref):
@@ -152,8 +159,7 @@
     vmem = pl.BlockSpec(memory_space=pltpu.VMEM)
 
     lag_rows = delays[0].astype(BF16).reshape(peers, sub_local, trials)
-    lag_rows = jnp.transpose(lag_rows, (2, 1, 0)).reshape(columns, trials // columns, subs)
-    lag_part = lax.dynamic_index_in_dim(lag_rows, lax.axis_index("beam"), 0, keepdims=False)
+    lag_rows = jnp.transpose(lag_rows, (2, 1, 0)).reshape(trials, subs)
 
     sent = pl.pallas_call(
         functools.partial(front_kernel, times, blocks, near, beams),
@@ -163,23 +169,37 @@
         scratch_shapes=[pltpu.VMEM((GX, rows // 2, 2 * GY), BF16)],
         cost_estimate=pl.CostEstimate(flops=2 * 10**9, bytes_accessed=4 * 10**6, transcendentals=0),
         name="front",
-    )(voltages.reshape(rows, feeds), grid_feed.reshape(1, feeds), jnp.asarray(steering_table(GY)))
+    )(voltages.reshape(rows // 2, 2, feeds), grid_feed.reshape(1, feeds), jnp.asarray(steering_table(GY)))
     own = lax.all_to_all(sent, ("far", "near", "beam"), split_axis=0, concat_axis=0, tiled=True)
-    lag_near = lax.all_gather(lag_part, "near")
-    lags = lax.all_gather(lag_near, "beam")
-    lags = jnp.transpose(lags, (1, 0, 2, 3)).reshape(near, trials, subs)
+    share = near // columns
+    fetched = []
+    for j in range(share):
+        steps = [(n, x, (n + x * share + j) % near) for n in range(near) for x in range(columns)]
+        pairs = [(source * columns + x, n * columns + x) for n, x, source in steps]
+        fetched.append(lax.ppermute(lag_rows, ("near", "beam"), pairs))
+    lags = lax.all_gather(jnp.stack(fetched), "beam").reshape(near, trials, subs)
     other = lax.ppermute(own, "dm", [(0, 1), (1, 0)])
-    core = lax.axis_index("dm").astype(jnp.int32).reshape(1)
-    local = pl.pallas_call(
+    place = jnp.stack([lax.axis_index("dm"), lax.axis_index("near")]).astype(jnp.int32)
+    anywhere = pl.BlockSpec(memory_space=pl.ANY)
+    local, total = pl.pallas_call(
         functools.partial(dedisperse_kernel, beams),
-        out_shape=jax.ShapeDtypeStruct((bands // blocks, trials, times * beams), F32),
-        in_specs=[pl.BlockSpec(memory_space=pltpu.SMEM)] + [vmem] * 3,
-        out_specs=vmem,
-        scratch_shapes=[pltpu.VMEM((2, peers * tall, times * beams), F32)],
+        out_shape=(
+            jax.ShapeDtypeStruct((bands // blocks, trials, times * beams), F32),
+            jax.ShapeDtypeStruct((trials, times * beams), F32),
+        ),
+        in_specs=[pl.BlockSpec(memory_space=pltpu.SMEM)] + [anywhere] * 3,
+        out_specs=(vmem, vmem),
+        scratch_shapes=[
+            pltpu.VMEM(own.shape, BF16),
+            pltpu.VMEM(own.shape, BF16),
+            pltpu.VMEM(lags.shape, BF16),
+            pltpu.VMEM((2, peers * tall, times * beams), F32),
+            pltpu.SemaphoreType.DMA((3,)),
+        ],
+        compiler_params=pltpu.CompilerParams(vmem_limit_bytes=24 * 2**20),
         cost_estimate=pl.CostEstimate(flops=2 * 10**9, bytes_accessed=4 * 10**6, transcendentals=0),
         name="dedisperse",
-    )(core, own, other, lags)
-    total = local[-1]
+    )(place, own, other, lags)
     base = jnp.zeros_like(total)
     for k in range(blocks - 1):
         message = (base + total).astype(BF16)

time: 220 us -> 185 us (0.84)
  blocking collectives: 188 us -> 153 us
  starting transfers between devices: 7.81 us -> 15.3 us
  local copies, waits for them, and re-layouts: 4.92 us -> 0.14 us
  other arithmetic: 2.82 us -> 0.19 us
    all_gather x2 -> x1, blocking collectives: 62.3 us -> 26.4 us  [search(): lax.all_gather(jnp.stack(fetched), 'beam').reshape(near, trials, subs)]
    ppermute x0 -> x2, starting transfers between devices: none -> 7.75 us  [search(): fetched.append(lax.ppermute(lag_rows, ('near', 'beam'), pairs))]
    reshape x2 -> x0, local copies, waits for them, and re-layouts: 2.3 us -> none  [the longest x1 2.25 us: search(): voltages.reshape(rows, feeds)]
  transfers between devices with their start and end apart: 4 -> 6, of which waited for: 1 -> 2; matrix products, arithmetic and copies ran while one was open for 0% -> 0% of each run, Pallas kernels for 0% -> 0%
where the time goes in v3:
time: 185 us
  blocking collectives  153 us (83%)
  starting transfers between devices  15.3 us (8%)
  Pallas kernels  12.6 us (7%)
  waiting for transfers between devices  3.15 us (2%)
    all_to_all x1, blocking collectives, search(): lax.all_to_all(sent, ('far', 'near', 'beam'), split_axis=0, concat_axis=0...  110 us
    all_gather x1, blocking collectives, search(): lax.all_gather(jnp.stack(fetched), 'beam').reshape(near, trials, subs)  26.4 us
    all_to_all x1, blocking collectives, search(): lax.all_to_all(cumulative, 'near', split_axis=0, concat_axis=0, tiled=True)  17.1 us
    ppermute x2, starting transfers between devices, search(): fetched.append(lax.ppermute(lag_rows, ('near', 'beam'), pairs))  7.75 us
    ppermute x3, starting transfers between devices, search(): base = base + lax.ppermute(message, 'far', [(k, k + 1)]).astype(F32)  5.66 us
    pallas_call x1, Pallas kernels, search(): pl.pallas_call(functools.partial(front_kernel, times, blocks, near, beams...  5.22 us
    pallas_call x1, Pallas kernels, search(): pl.pallas_call(functools.partial(dedisperse_kernel, beams), out_shape=(ja...  5.19 us
  transfers between devices with their start and end apart: 6, of which 2 were waited for; matrix products, arithmetic and copies ran while one was open for 0% of the time, Pallas kernels for 0%

profile of v3, /device:TPU:40, one launch (start us, length us, event | category | flops | bytes accessed | tf_op | source)
XLA Modules:
  0.0 185.0 jit_solution(10423284235531323135)
XLA Ops:
  0.0 5.2 %front.1 = bf16[128,16,128]{2,1,0:T(8,128)(2,1)} custom-call(bf16[256,2,1024]{2,1,0:T(2,128)(2,1)} %bitcast.23, s32[1,1024]{1,0:T(1,128)} %bitcast.24, bf16[512,512]{1,0:T(8,128)(2,1)} %constant.11.clone.table_ref), custom_call_target="tpu_custom_call" | custom-call | flops 2000000000 | bytes 4000000 | tf_op jit(solution)/shard_map/front/pallas_call | solution.py:164
  5.2 0.0 copy-start
  5.2 109.8 %all_to_all.10.own_any = bf16[128,16,128]{2,1,0:T(8,128)(2,1)S(1)} all-to-all(bf16[128,16,128]{2,1,0:T(8,128)(2,1)} %front.1), channel_id=1, replica_groups=mesh['grp'=2,'far'=4,'near'=8,'beam'=4,'dm'=2] {'far','near','beam'}, dimensions={0} | all-to-all | bytes 1048576 | tf_op jit(solution)/shard_map/all_to_all | solution.py:173
  115.0 1.9 %collective-permute-start = (bf16[128,16,128]{2,1,0:T(8,128)(2,1)S(1)}, bf16[128,16,128]{2,1,0:T(8,128)(2,1)S(1)}, u32[]{:S(2)}, u32[]{:S(2)}) collective-permute-start(bf16[128,16,128]{2,1,0:T(8,128)(2,1)S(1)} %all_to_all.10.own_any), channel_id=1, source_target_pairs={{0,1},{1,0},{2,3},{3,2},{4,5},{5,4},{6,7},{7,6},{8,9},{9,8},{10,11... | collective-permute-start | bytes 1572872 | tf_op jit(solution)/shard_map/ppermute | solution.py:181
  117.0 0.0 copy-done
  117.0 0.1 copy.7
  117.1 7.1 %collective-permute-start.2 = (bf16[128,256]{1,0:T(8,128)(2,1)S(1)}, bf16[128,256]{1,0:T(8,128)(2,1)S(1)}, u32[]{:S(2)}, u32[]{:S(2)}) collective-permute-start(bf16[128,256]{1,0:T(8,128)(2,1)S(1)} %bitcast.19), channel_id=1, source_target_pairs={{8,0},{26,2},{44,4},{62,6},{16,8},{34,10},{52,12},{6,14},{24,16},{... | collective-permute-start | bytes 196616 | tf_op jit(solution)/shard_map/ppermute | solution.py:179
  124.2 0.7 collective-permute-start.1
  124.9 0.1 pad_add_fusion.place_ref
  125.0 1.6 collective-permute-done.2
  126.5 0.0 collective-permute-done.1
  126.6 26.4 %all-gather.lag_any = bf16[8,128,256]{2,1,0:T(8,128)(2,1)S(1)} all-gather(bf16[2,128,256]{2,1,0:T(8,128)(2,1)S(1)} %pad_maximum_fusion), channel_id=2, replica_groups=mesh['grp'=2,'far'=4,'near'=8,'beam'=4,'dm'=2] {'beam'}, dimensions={0}, use_global_device_ids=true | all-gather | bytes 655360 | tf_op jit(solution)/shard_map/all_gather | solution.py:180
  153.0 0.0 collective-permute-done.other_any
  153.0 5.2 %dedisperse.1 = (f32[8,128,128]{2,1,0:T(8,128)S(1)}, f32[128,128]{1,0:T(8,128)S(1)}) custom-call(s32[2]{0:T(128)S(1)} %pad_add_fusion.place_ref, bf16[128,16,128]{2,1,0:T(8,128)(2,1)S(1)} %all_to_all.10.own_any, bf16[128,16,128]{2,1,0:T(8,128)(2,1)S(1)} %collective-permute-done.other_any, bf16[8,128,256]{2,1,0:T(8,128)(2,1)S(1)} %all-gather.lag_any), custom_call_target="tpu_custom_call" | custom-call | flops 2000000000 | bytes 4000000 | tf_op jit(solution)/shard_map/dedisperse/pallas_call | solution.py:184
  158.2 4.3 %collective-permute-start.3 = (bf16[128,128]{1,0:T(8,128)(2,1)S(1)}, bf16[128,128]{1,0:T(8,128)(2,1)S(1)}, u32[]{:S(2)}, u32[]{:S(2)}) collective-permute-start(bf16[128,128]{1,0:T(8,128)(2,1)S(1)} %convert_element_type.30), channel_id=1, source_target_pairs={{0,64},{1,65},{2,66},{3,67},{4,68},{5,69},{6,70},{7,71},{8,72},{9,... | collective-permute-start | bytes 98312 | tf_op jit(solution)/shard_map/ppermute | solution.py:206
  162.6 1.6 collective-permute-done.3
  164.2 0.7 collective-permute-start.4
  164.8 0.0 collective-permute-done.4
  164.9 0.7 collective-permute-start.5
  165.5 0.0 collective-permute-done.5
  165.6 17.1 %all_to_all.11.in_ref = bf16[8,128,128]{2,1,0:T(8,128)(2,1)} all-to-all(bf16[8,128,128]{2,1,0:T(8,128)(2,1)S(1)} %add_convert_fusion), channel_id=1, replica_groups=mesh['grp'=2,'far'=4,'near'=8,'beam'=4,'dm'=2] {'near'}, dimensions={0} | all-to-all | bytes 524288 | tf_op jit(solution)/shard_map/all_to_all | solution.py:208
  182.8 2.2 %spread.1 = f32[1024,128]{1,0:T(8,128)} custom-call(bf16[8,128,128]{2,1,0:T(8,128)(2,1)} %all_to_all.11.in_ref), custom_call_target="tpu_custom_call" | custom-call | tf_op jit(solution)/shard_map/spread/pallas_call | solution.py:209
  (8 shorter events, 0.1 us)
Async XLA Ops:
  5.2 111.8 %copy-start = (s32[1,256,128]{2,1,0:T(8,128)S(1)}, s32[1,256,128]{2,1,0:T(8,128)}, u32[]{:S(2)}) copy-start(s32[1,256,128]{2,1,0:T(8,128)} %param.6) | copy-start | bytes 393220
  115.0 38.0 %collective-permute-start = (bf16[128,16,128]{2,1,0:T(8,128)(2,1)S(1)}, bf16[128,16,128]{2,1,0:T(8,128)(2,1)S(1)}, u32[]{:S(2)}, u32[]{:S(2)}) collective-permute-start(bf16[128,16,128]{2,1,0:T(8,128)(2,1)S(1)} %all_to_all.10.own_any), channel_id=1, source_target_pairs={{0,1},{1,0},{2,3},{3,2},{4,5},{5,4},{6,7},{7,6},{8,9},{9,8},{10,11... | collective-permute-start | bytes 1572872 | tf_op jit(solution)/shard_map/ppermute | solution.py:181
  117.1 9.4 %collective-permute-start.2 = (bf16[128,256]{1,0:T(8,128)(2,1)S(1)}, bf16[128,256]{1,0:T(8,128)(2,1)S(1)}, u32[]{:S(2)}, u32[]{:S(2)}) collective-permute-start(bf16[128,256]{1,0:T(8,128)(2,1)S(1)} %bitcast.19), channel_id=1, source_target_pairs={{8,0},{26,2},{44,4},{62,6},{16,8},{34,10},{52,12},{6,14},{24,16},{... | collective-permute-start | bytes 196616 | tf_op jit(solution)/shard_map/ppermute | solution.py:179
  124.2 2.3 %collective-permute-start.1 = (bf16[128,256]{1,0:T(8,128)(2,1)S(1)}, bf16[128,256]{1,0:T(8,128)(2,1)S(1)}, u32[]{:S(2)}, u32[]{:S(2)}) collective-permute-start(bf16[128,256]{1,0:T(8,128)(2,1)S(1)} %bitcast.20), channel_id=1, source_target_pairs={{0,0},{18,2},{36,4},{54,6},{8,8},{26,10},{44,12},{62,14},{16,16},{... | collective-permute-start | bytes 196616 | tf_op jit(solution)/shard_map/ppermute | solution.py:179
  158.2 5.9 %collective-permute-start.3 = (bf16[128,128]{1,0:T(8,128)(2,1)S(1)}, bf16[128,128]{1,0:T(8,128)(2,1)S(1)}, u32[]{:S(2)}, u32[]{:S(2)}) collective-permute-start(bf16[128,128]{1,0:T(8,128)(2,1)S(1)} %convert_element_type.30), channel_id=1, source_target_pairs={{0,64},{1,65},{2,66},{3,67},{4,68},{5,69},{6,70},{7,71},{8,72},{9,... | collective-permute-start | bytes 98312 | tf_op jit(solution)/shard_map/ppermute | solution.py:206
  164.2 0.7 collective-permute-start.4
  164.9 0.7 collective-permute-start.5

commit v4 on v3

--- a/solution.py
+++ b/solution.py
@@ -45,7 +45,11 @@
     return result
 
 
-def front_kernel(times, blocks, near, beams, volt_ref, feed_ref, table_ref, out_ref, along_ref):
+def front_kernel(times, blocks, near, beams, volt_any, feed_ref, table_any, out_ref, volt_ref, table_ref, along_ref, sems):
+    load = pltpu.make_async_copy(volt_any, volt_ref, sems.at[0])
+    load_table = pltpu.make_async_copy(table_any, table_ref, sems.at[1])
+    load.start()
+    load_table.start()
     rows, feeds = 2 * volt_ref.shape[0], volt_ref.shape[2]
     half = rows // 2
     chans = half // times
@@ -53,8 +57,10 @@
     i = iota((rows, rows), 0)
     source = i % chans * (2 * times) + i // chans % times * 2 + i // half
     order = jnp.where(iota((rows, rows), 1) == source, 1.0, 0.0).astype(BF16)
+    pick = jnp.where(iota((feeds, feeds), 0) == feed_ref[...], 1.0, 0.0).astype(BF16)
+    load.wait()
+    load_table.wait()
     planes = jnp.dot(order, volt_ref[...].reshape(rows, feeds), preferred_element_type=F32).astype(BF16)
-    pick = jnp.where(iota((feeds, feeds), 0) == feed_ref[...], 1.0, 0.0).astype(BF16)
     grid = jnp.dot(planes, pick, preferred_element_type=F32).astype(BF16)
     for gx in range(GX):
         cells = slice(gx * GY, (gx + 1) * GY)
@@ -137,7 +143,10 @@
     total_ref[...] = running
 
 
-def spread_kernel(beams, scale, in_ref, out_ref):
+def spread_kernel(beams, scale, in_any, out_ref, in_ref, sem):
+    copy = pltpu.make_async_copy(in_any, in_ref, sem)
+    copy.start()
+    copy.wait()
     slabs, trials, width = in_ref.shape
     count = width // beams
     for tile in range(slabs // count):
@@ -157,6 +166,7 @@
     tall = bands // blocks * sub_local
     rows = bands * sub_local * times * 2
     vmem = pl.BlockSpec(memory_space=pltpu.VMEM)
+    anywhere = pl.BlockSpec(memory_space=pl.ANY)
 
     lag_rows = delays[0].astype(BF16).reshape(peers, sub_local, trials)
     lag_rows = jnp.transpose(lag_rows, (2, 1, 0)).reshape(trials, subs)
@@ -164,9 +174,14 @@
     sent = pl.pallas_call(
         functools.partial(front_kernel, times, blocks, near, beams),
         out_shape=jax.ShapeDtypeStruct((peers, tall, times * beams), BF16),
-        in_specs=[vmem] * 3,
+        in_specs=[anywhere, vmem, anywhere],
         out_specs=vmem,
-        scratch_shapes=[pltpu.VMEM((GX, rows // 2, 2 * GY), BF16)],
+        scratch_shapes=[
+            pltpu.VMEM((rows // 2, 2, feeds), BF16),
+            pltpu.VMEM((2 * GY, 2 * GY), BF16),
+            pltpu.VMEM((GX, rows // 2, 2 * GY), BF16),
+            pltpu.SemaphoreType.DMA((2,)),
+        ],
         cost_estimate=pl.CostEstimate(flops=2 * 10**9, bytes_accessed=4 * 10**6, transcendentals=0),
         name="front",
     )(voltages.reshape(rows // 2, 2, feeds), grid_feed.reshape(1, feeds), jnp.asarray(steering_table(GY)))
@@ -180,7 +195,6 @@
     lags = lax.all_gather(jnp.stack(fetched), "beam").reshape(near, trials, subs)
     other = lax.ppermute(own, "dm", [(0, 1), (1, 0)])
     place = jnp.stack([lax.axis_index("dm"), lax.axis_index("near")]).astype(jnp.int32)
-    anywhere = pl.BlockSpec(memory_space=pl.ANY)
     local, total = pl.pallas_call(
         functools.partial(dedisperse_kernel, beams),
         out_shape=(
@@ -209,8 +223,10 @@
     spread = pl.pallas_call(
         functools.partial(spread_kernel, beams, 1.0 / math.sqrt(FREQS)),
         out_shape=jax.ShapeDtypeStruct((trials * near, LANES), F32),
-        in_specs=[vmem],
+        in_specs=[anywhere],
         out_specs=vmem,
+        scratch_shapes=[pltpu.VMEM(slabs.shape, BF16), pltpu.SemaphoreType.DMA],
+        compiler_params=pltpu.CompilerParams(vmem_limit_bytes=24 * 2**20),
         name="spread",
     )(slabs)
     spread = jnp.transpose(spread.reshape(trials, near // times, times, LANES), (0, 2, 1, 3))

time: 185 us -> 185 us (level)
  no operation moved by 1% of the time
where the time goes in v4:
time: 185 us
  blocking collectives  153 us (83%)
  starting transfers between devices  15.3 us (8%)
  Pallas kernels  12.3 us (7%)
  waiting for transfers between devices  3.15 us (2%)
    all_to_all x1, blocking collectives, search(): lax.all_to_all(sent, ('far', 'near', 'beam'), split_axis=0, concat_axis=0...  110 us
    all_gather x1, blocking collectives, search(): lax.all_gather(jnp.stack(fetched), 'beam').reshape(near, trials, subs)  26.4 us
    all_to_all x1, blocking collectives, search(): lax.all_to_all(cumulative, 'near', split_axis=0, concat_axis=0, tiled=True)  17 us
    ppermute x2, starting transfers between devices, search(): fetched.append(lax.ppermute(lag_rows, ('near', 'beam'), pairs))  7.75 us
    pallas_call x1, Pallas kernels, search(): pl.pallas_call(functools.partial(front_kernel, times, blocks, near, beams...  5.83 us
    ppermute x3, starting transfers between devices, search(): base = base + lax.ppermute(message, 'far', [(k, k + 1)]).astype(F32)  5.65 us
    pallas_call x1, Pallas kernels, search(): pl.pallas_call(functools.partial(dedisperse_kernel, beams), out_shape=(ja...  5.19 us
  transfers between devices with their start and end apart: 6, of which 2 were waited for; matrix products, arithmetic and copies ran while one was open for 0% of the time, Pallas kernels for 0%

profile of v4, /device:TPU:40, one launch (start us, length us, event | category | flops | bytes accessed | tf_op | source)
XLA Modules:
  0.0 184.6 jit_solution(5100470465821125887)
XLA Ops:
  0.0 5.8 %front.1 = bf16[128,16,128]{2,1,0:T(8,128)(2,1)} custom-call(bf16[256,2,1024]{2,1,0:T(2,128)(2,1)} %bitcast.23, s32[1,1024]{1,0:T(1,128)} %bitcast.24, bf16[512,512]{1,0:T(8,128)(2,1)} %constant.11.clone.table_any), custom_call_target="tpu_custom_call" | custom-call | flops 2000000000 | bytes 4000000 | tf_op jit(solution)/shard_map/front/pallas_call | solution.py:174
  5.8 0.0 copy-start
  5.8 109.8 %all_to_all.10.own_any = bf16[128,16,128]{2,1,0:T(8,128)(2,1)S(1)} all-to-all(bf16[128,16,128]{2,1,0:T(8,128)(2,1)} %front.1), channel_id=1, replica_groups=mesh['grp'=2,'far'=4,'near'=8,'beam'=4,'dm'=2] {'far','near','beam'}, dimensions={0} | all-to-all | bytes 1048576 | tf_op jit(solution)/shard_map/all_to_all | solution.py:188
  115.7 1.9 %collective-permute-start = (bf16[128,16,128]{2,1,0:T(8,128)(2,1)S(1)}, bf16[128,16,128]{2,1,0:T(8,128)(2,1)S(1)}, u32[]{:S(2)}, u32[]{:S(2)}) collective-permute-start(bf16[128,16,128]{2,1,0:T(8,128)(2,1)S(1)} %all_to_all.10.own_any), channel_id=1, source_target_pairs={{0,1},{1,0},{2,3},{3,2},{4,5},{5,4},{6,7},{7,6},{8,9},{9,8},{10,11... | collective-permute-start | bytes 1572872 | tf_op jit(solution)/shard_map/ppermute | solution.py:196
  117.6 0.0 copy-done
  117.6 0.1 copy.7
  117.8 7.1 %collective-permute-start.2 = (bf16[128,256]{1,0:T(8,128)(2,1)S(1)}, bf16[128,256]{1,0:T(8,128)(2,1)S(1)}, u32[]{:S(2)}, u32[]{:S(2)}) collective-permute-start(bf16[128,256]{1,0:T(8,128)(2,1)S(1)} %bitcast.19), channel_id=1, source_target_pairs={{8,0},{26,2},{44,4},{62,6},{16,8},{34,10},{52,12},{6,14},{24,16},{... | collective-permute-start | bytes 196616 | tf_op jit(solution)/shard_map/ppermute | solution.py:194
  124.9 0.7 collective-permute-start.1
  125.6 0.1 pad_add_fusion.place_ref
  125.6 1.6 collective-permute-done.2
  127.2 0.0 collective-permute-done.1
  127.2 26.4 %all-gather.lag_any = bf16[8,128,256]{2,1,0:T(8,128)(2,1)S(1)} all-gather(bf16[2,128,256]{2,1,0:T(8,128)(2,1)S(1)} %pad_maximum_fusion), channel_id=2, replica_groups=mesh['grp'=2,'far'=4,'near'=8,'beam'=4,'dm'=2] {'beam'}, dimensions={0}, use_global_device_ids=true | all-gather | bytes 655360 | tf_op jit(solution)/shard_map/all_gather | solution.py:195
  153.6 0.0 collective-permute-done.other_any
  153.7 5.2 %dedisperse.1 = (f32[8,128,128]{2,1,0:T(8,128)S(1)}, f32[128,128]{1,0:T(8,128)S(1)}) custom-call(s32[2]{0:T(128)S(1)} %pad_add_fusion.place_ref, bf16[128,16,128]{2,1,0:T(8,128)(2,1)S(1)} %all_to_all.10.own_any, bf16[128,16,128]{2,1,0:T(8,128)(2,1)S(1)} %collective-permute-done.other_any, bf16[8,128,256]{2,1,0:T(8,128)(2,1)S(1)} %all-gather.lag_any), custom_call_target="tpu_custom_call" | custom-call | flops 2000000000 | bytes 4000000 | tf_op jit(solution)/shard_map/dedisperse/pallas_call | solution.py:198
  158.9 4.3 %collective-permute-start.3 = (bf16[128,128]{1,0:T(8,128)(2,1)S(1)}, bf16[128,128]{1,0:T(8,128)(2,1)S(1)}, u32[]{:S(2)}, u32[]{:S(2)}) collective-permute-start(bf16[128,128]{1,0:T(8,128)(2,1)S(1)} %convert_element_type.30), channel_id=1, source_target_pairs={{0,64},{1,65},{2,66},{3,67},{4,68},{5,69},{6,70},{7,71},{8,72},{9,... | collective-permute-start | bytes 98312 | tf_op jit(solution)/shard_map/ppermute | solution.py:220
  163.2 1.6 collective-permute-done.3
  164.8 0.7 collective-permute-start.4
  165.5 0.0 collective-permute-done.4
  165.5 0.7 collective-permute-start.5
  166.2 0.0 collective-permute-done.5
  166.3 17.0 %all_to_all.11.in_any = bf16[8,128,128]{2,1,0:T(8,128)(2,1)S(1)} all-to-all(bf16[8,128,128]{2,1,0:T(8,128)(2,1)S(1)} %add_convert_fusion), channel_id=1, replica_groups=mesh['grp'=2,'far'=4,'near'=8,'beam'=4,'dm'=2] {'near'}, dimensions={0} | all-to-all | bytes 524288 | tf_op jit(solution)/shard_map/all_to_all | solution.py:222
  183.3 1.3 spread.1
  (8 shorter events, 0.1 us)
Async XLA Ops:
  5.8 111.8 %copy-start = (s32[1,256,128]{2,1,0:T(8,128)S(1)}, s32[1,256,128]{2,1,0:T(8,128)}, u32[]{:S(2)}) copy-start(s32[1,256,128]{2,1,0:T(8,128)} %param.6) | copy-start | bytes 393220
  115.7 38.0 %collective-permute-start = (bf16[128,16,128]{2,1,0:T(8,128)(2,1)S(1)}, bf16[128,16,128]{2,1,0:T(8,128)(2,1)S(1)}, u32[]{:S(2)}, u32[]{:S(2)}) collective-permute-start(bf16[128,16,128]{2,1,0:T(8,128)(2,1)S(1)} %all_to_all.10.own_any), channel_id=1, source_target_pairs={{0,1},{1,0},{2,3},{3,2},{4,5},{5,4},{6,7},{7,6},{8,9},{9,8},{10,11... | collective-permute-start | bytes 1572872 | tf_op jit(solution)/shard_map/ppermute | solution.py:196
  117.8 9.4 %collective-permute-start.2 = (bf16[128,256]{1,0:T(8,128)(2,1)S(1)}, bf16[128,256]{1,0:T(8,128)(2,1)S(1)}, u32[]{:S(2)}, u32[]{:S(2)}) collective-permute-start(bf16[128,256]{1,0:T(8,128)(2,1)S(1)} %bitcast.19), channel_id=1, source_target_pairs={{8,0},{26,2},{44,4},{62,6},{16,8},{34,10},{52,12},{6,14},{24,16},{... | collective-permute-start | bytes 196616 | tf_op jit(solution)/shard_map/ppermute | solution.py:194
  124.9 2.3 %collective-permute-start.1 = (bf16[128,256]{1,0:T(8,128)(2,1)S(1)}, bf16[128,256]{1,0:T(8,128)(2,1)S(1)}, u32[]{:S(2)}, u32[]{:S(2)}) collective-permute-start(bf16[128,256]{1,0:T(8,128)(2,1)S(1)} %bitcast.20), channel_id=1, source_target_pairs={{0,0},{18,2},{36,4},{54,6},{8,8},{26,10},{44,12},{62,14},{16,16},{... | collective-permute-start | bytes 196616 | tf_op jit(solution)/shard_map/ppermute | solution.py:194
  158.9 5.9 %collective-permute-start.3 = (bf16[128,128]{1,0:T(8,128)(2,1)S(1)}, bf16[128,128]{1,0:T(8,128)(2,1)S(1)}, u32[]{:S(2)}, u32[]{:S(2)}) collective-permute-start(bf16[128,128]{1,0:T(8,128)(2,1)S(1)} %convert_element_type.30), channel_id=1, source_target_pairs={{0,64},{1,65},{2,66},{3,67},{4,68},{5,69},{6,70},{7,71},{8,72},{9,... | collective-permute-start | bytes 98312 | tf_op jit(solution)/shard_map/ppermute | solution.py:220
  164.8 0.7 collective-permute-start.4
  165.5 0.7 collective-permute-start.5

commit v5 on v4

--- a/solution.py
+++ b/solution.py
@@ -88,6 +88,7 @@
 
 
 def dedisperse_kernel(beams, place_ref, own_any, other_any, lag_any, out_ref, total_ref, own_ref, other_ref, lag_ref, level_ref, sems):
+    columns, share = lag_ref.shape[:2]
     pairs = ((own_any, own_ref), (other_any, other_ref), (lag_any, lag_ref))
     copies = [pltpu.make_async_copy(a, b, sems.at[i]) for i, (a, b) in enumerate(pairs)]
     for copy in copies:
@@ -125,7 +126,9 @@
             r = pl.ds(b * subs + s, sources, stride=tall)
             rows.append(jnp.concatenate([level_ref[0, r, :].astype(BF16), level_ref[1, r, :].astype(BF16)], axis=1))
         data = jnp.concatenate(rows, axis=0)
-        lags = lag_ref[lax.rem(b + bands - place_ref[1], bands)].astype(F32)
+        turn = lax.rem(b + bands - place_ref[1], bands)
+        column = lax.rem(lax.div(turn, share) + columns - place_ref[2], columns)
+        lags = lag_ref[column, lax.rem(turn, share)].astype(F32)
         chosen = [jnp.where(lags == float(v), 1.0, 0.0).astype(BF16) for v in range(LAGS)]
         for v in range(LAGS):
             picked = jnp.dot(chosen[v], data, preferred_element_type=F32)
@@ -192,9 +195,13 @@
         steps = [(n, x, (n + x * share + j) % near) for n in range(near) for x in range(columns)]
         pairs = [(source * columns + x, n * columns + x) for n, x, source in steps]
         fetched.append(lax.ppermute(lag_rows, ("near", "beam"), pairs))
-    lags = lax.all_gather(jnp.stack(fetched), "beam").reshape(near, trials, subs)
+    lags = [jnp.stack(fetched)]
+    for step in range(1, columns):
+        pairs = [((x + step) % columns, x) for x in range(columns)]
+        lags.append(lax.ppermute(lags[0], "beam", pairs))
+    lags = jnp.stack(lags)
     other = lax.ppermute(own, "dm", [(0, 1), (1, 0)])
-    place = jnp.stack([lax.axis_index("dm"), lax.axis_index("near")]).astype(jnp.int32)
+    place = jnp.stack([lax.axis_index(name) for name in ("dm", "near", "beam")]).astype(jnp.int32)
     local, total = pl.pallas_call(
         functools.partial(dedisperse_kernel, beams),
         out_shape=(

time: 185 us -> 189 us (1.022)
  blocking collectives: 153 us -> 129 us
  starting transfers between devices: 15.3 us -> 38.9 us
  waiting for transfers between devices: 3.15 us -> 7.48 us
    all_gather x1 -> x0, blocking collectives: 26.4 us -> none  [search(): lax.all_gather(jnp.stack(fetched), 'beam').reshape(near, trials, subs)]
    ppermute x0 -> x3, starting transfers between devices: none -> 23.5 us  [search(): lags.append(lax.ppermute(lags[0], 'beam', pairs))]
    ppermute x0 -> x3, waiting for transfers between devices: none -> 4.26 us  [search(): lags.append(lax.ppermute(lags[0], 'beam', pairs))]
    all_to_all x1, blocking collectives: 17 us -> 19 us  [search(): lax.all_to_all(cumulative, 'near', split_axis=0, concat_axis=0, tiled=True)]
  transfers between devices with their start and end apart: 6 -> 9, of which waited for: 2 -> 4; matrix products, arithmetic and copies ran while one was open for 0% -> 0% of each run, Pallas kernels for 0% -> 0%
where the time goes in v5:
time: 189 us; the launch traced here: 188 us
  blocking collectives  129 us (68%)
  starting transfers between devices  38.9 us (21%)
  Pallas kernels  12.3 us (7%)
  waiting for transfers between devices  7.48 us (4%)
    all_to_all x1, blocking collectives, search(): lax.all_to_all(sent, ('far', 'near', 'beam'), split_axis=0, concat_axis=0...  110 us
    ppermute x3, starting transfers between devices, search(): lags.append(lax.ppermute(lags[0], 'beam', pairs))  23.5 us
    all_to_all x1, blocking collectives, search(): lax.all_to_all(cumulative, 'near', split_axis=0, concat_axis=0, tiled=True)  19 us
    ppermute x2, starting transfers between devices, search(): fetched.append(lax.ppermute(lag_rows, ('near', 'beam'), pairs))  7.75 us
    pallas_call x1, Pallas kernels, search(): pl.pallas_call(functools.partial(front_kernel, times, blocks, near, beams...  5.83 us
    ppermute x3, starting transfers between devices, search(): base = base + lax.ppermute(message, 'far', [(k, k + 1)]).astype(F32)  5.66 us
    pallas_call x1, Pallas kernels, search(): pl.pallas_call(functools.partial(dedisperse_kernel, beams), out_shape=(ja...  5.18 us
    ppermute x3, waiting for transfers between devices, search(): lags.append(lax.ppermute(lags[0], 'beam', pairs))  4.26 us
  transfers between devices with their start and end apart: 9, of which 4 were waited for; matrix products, arithmetic and copies ran while one was open for 0% of the time, Pallas kernels for 0%

profile of v5, /device:TPU:40, one launch (start us, length us, event | category | flops | bytes accessed | tf_op | source)
XLA Modules:
  0.0 188.1 jit_solution(2534088626243434124)
XLA Ops:
  0.0 5.8 %front.1 = bf16[128,16,128]{2,1,0:T(8,128)(2,1)} custom-call(bf16[256,2,1024]{2,1,0:T(2,128)(2,1)} %bitcast.32, s32[1,1024]{1,0:T(1,128)} %bitcast.33, bf16[512,512]{1,0:T(8,128)(2,1)} %constant.14.clone.table_any), custom_call_target="tpu_custom_call" | custom-call | flops 2000000000 | bytes 4000000 | tf_op jit(solution)/shard_map/front/pallas_call | solution.py:177
  5.8 0.0 copy-start
  5.8 109.8 %all_to_all.10.own_any = bf16[128,16,128]{2,1,0:T(8,128)(2,1)S(1)} all-to-all(bf16[128,16,128]{2,1,0:T(8,128)(2,1)} %front.1), channel_id=1, replica_groups=mesh['grp'=2,'far'=4,'near'=8,'beam'=4,'dm'=2] {'far','near','beam'}, dimensions={0} | all-to-all | bytes 1048576 | tf_op jit(solution)/shard_map/all_to_all | solution.py:191
  115.7 1.9 %collective-permute-start = (bf16[128,16,128]{2,1,0:T(8,128)(2,1)S(1)}, bf16[128,16,128]{2,1,0:T(8,128)(2,1)S(1)}, u32[]{:S(2)}, u32[]{:S(2)}) collective-permute-start(bf16[128,16,128]{2,1,0:T(8,128)(2,1)S(1)} %all_to_all.10.own_any), channel_id=1, source_target_pairs={{0,1},{1,0},{2,3},{3,2},{4,5},{5,4},{6,7},{7,6},{8,9},{9,8},{10,11... | collective-permute-start | bytes 1572872 | tf_op jit(solution)/shard_map/ppermute | solution.py:203
  117.6 0.1 copy.5
  117.8 7.1 %collective-permute-start.2 = (bf16[128,256]{1,0:T(8,128)(2,1)S(1)}, bf16[128,256]{1,0:T(8,128)(2,1)S(1)}, u32[]{:S(2)}, u32[]{:S(2)}) collective-permute-start(bf16[128,256]{1,0:T(8,128)(2,1)S(1)} %bitcast.28), channel_id=1, source_target_pairs={{8,0},{26,2},{44,4},{62,6},{16,8},{34,10},{52,12},{6,14},{24,16},{... | collective-permute-start | bytes 196616 | tf_op jit(solution)/shard_map/ppermute | solution.py:197
  124.9 0.7 collective-permute-start.1
  125.5 1.6 collective-permute-done.2
  127.2 17.6 %collective-permute-start.4 = (bf16[2,128,256]{2,1,0:T(8,128)(2,1)S(1)}, bf16[2,128,256]{2,1,0:T(8,128)(2,1)S(1)}, u32[]{:S(2)}, u32[]{:S(2)}) collective-permute-start(bf16[2,128,256]{2,1,0:T(8,128)(2,1)S(1)} %get-tuple-element.10), channel_id=1, source_target_pairs={{4,0},{6,2},{0,4},{2,6},{5,1},{7,3},{1,5},{3,7},{12,8},{14,10},{8,... | collective-permute-start | bytes 393224 | tf_op jit(solution)/shard_map/ppermute | solution.py:201
  144.8 2.0 %collective-permute-start.3 = (bf16[2,128,256]{2,1,0:T(8,128)(2,1)S(1)}, bf16[2,128,256]{2,1,0:T(8,128)(2,1)S(1)}, u32[]{:S(2)}, u32[]{:S(2)}) collective-permute-start(bf16[2,128,256]{2,1,0:T(8,128)(2,1)S(1)} %get-tuple-element.10), channel_id=1, source_target_pairs={{2,0},{4,2},{6,4},{0,6},{3,1},{5,3},{7,5},{1,7},{10,8},{12,10},{14... | collective-permute-start | bytes 393224 | tf_op jit(solution)/shard_map/ppermute | solution.py:201
  146.8 4.0 %collective-permute-start.5 = (bf16[2,128,256]{2,1,0:T(8,128)(2,1)S(1)}, bf16[2,128,256]{2,1,0:T(8,128)(2,1)S(1)}, u32[]{:S(2)}, u32[]{:S(2)}) collective-permute-start(bf16[2,128,256]{2,1,0:T(8,128)(2,1)S(1)} %get-tuple-element.10), channel_id=1, source_target_pairs={{6,0},{0,2},{2,4},{4,6},{7,1},{1,3},{3,5},{5,7},{14,8},{8,10},{10,... | collective-permute-start | bytes 393224 | tf_op jit(solution)/shard_map/ppermute | solution.py:201
  150.8 0.1 pad_add_fusion.place_ref
  150.8 0.0 collective-permute-done.4
  150.9 1.1 collective-permute-done.3
  151.9 3.2 %collective-permute-done.5 = bf16[2,128,256]{2,1,0:T(8,128)(2,1)S(1)} collective-permute-done((bf16[2,128,256]{2,1,0:T(8,128)(2,1)S(1)}, bf16[2,128,256]{2,1,0:T(8,128)(2,1)S(1)}, u32[]{:S(2)}, u32[]{:S(2)}) %collective-permute-start.5) | collective-permute-done | bytes 131104 | tf_op jit(solution)/shard_map/ppermute | solution.py:201
  155.1 0.1 pad_maximum_fusion.lag_any
  155.2 5.2 %dedisperse.1 = (f32[8,128,128]{2,1,0:T(8,128)S(1)}, f32[128,128]{1,0:T(8,128)S(1)}) custom-call(s32[3]{0:T(128)S(1)} %pad_add_fusion.place_ref, bf16[128,16,128]{2,1,0:T(8,128)(2,1)S(1)} %all_to_all.10.own_any, bf16[128,16,128]{2,1,0:T(8,128)(2,1)S(1)} %collective-permute-done.other_any, bf16[4,2,128,256]{3,2,1,0:T(8,128)(2,1)S(1)} %pad_maximum_fusion.lag_any), custom_call_target="tpu_custom_call" | custom-call | flops 2000000000 | bytes 4000000 | tf_op jit(solution)/shard_map/dedisperse/pallas_call | solution.py:205
  160.4 4.3 %collective-permute-start.6 = (bf16[128,128]{1,0:T(8,128)(2,1)S(1)}, bf16[128,128]{1,0:T(8,128)(2,1)S(1)}, u32[]{:S(2)}, u32[]{:S(2)}) collective-permute-start(bf16[128,128]{1,0:T(8,128)(2,1)S(1)} %convert_element_type.30), channel_id=1, source_target_pairs={{0,64},{1,65},{2,66},{3,67},{4,68},{5,69},{6,70},{7,71},{8,72},{9,... | collective-permute-start | bytes 98312 | tf_op jit(solution)/shard_map/ppermute | solution.py:227
  164.7 1.6 collective-permute-done.6
  166.3 0.7 collective-permute-start.7
  167.0 0.7 collective-permute-start.8
  167.7 0.0 collective-permute-done.8
  167.8 19.0 %all_to_all.11.in_any = bf16[8,128,128]{2,1,0:T(8,128)(2,1)S(1)} all-to-all(bf16[8,128,128]{2,1,0:T(8,128)(2,1)S(1)} %add_convert_fusion), channel_id=1, replica_groups=mesh['grp'=2,'far'=4,'near'=8,'beam'=4,'dm'=2] {'near'}, dimensions={0} | all-to-all | bytes 524288 | tf_op jit(solution)/shard_map/all_to_all | solution.py:229
  186.8 1.3 spread.1
  (12 shorter events, 0.1 us)
Async XLA Ops:
  5.8 111.8 %copy-start = (s32[1,256,128]{2,1,0:T(8,128)S(1)}, s32[1,256,128]{2,1,0:T(8,128)}, u32[]{:S(2)}) copy-start(s32[1,256,128]{2,1,0:T(8,128)} %param.6) | copy-start | bytes 393220
  115.7 39.5 %collective-permute-start = (bf16[128,16,128]{2,1,0:T(8,128)(2,1)S(1)}, bf16[128,16,128]{2,1,0:T(8,128)(2,1)S(1)}, u32[]{:S(2)}, u32[]{:S(2)}) collective-permute-start(bf16[128,16,128]{2,1,0:T(8,128)(2,1)S(1)} %all_to_all.10.own_any), channel_id=1, source_target_pairs={{0,1},{1,0},{2,3},{3,2},{4,5},{5,4},{6,7},{7,6},{8,9},{9,8},{10,11... | collective-permute-start | bytes 1572872 | tf_op jit(solution)/shard_map/ppermute | solution.py:203
  117.8 9.4 %collective-permute-start.2 = (bf16[128,256]{1,0:T(8,128)(2,1)S(1)}, bf16[128,256]{1,0:T(8,128)(2,1)S(1)}, u32[]{:S(2)}, u32[]{:S(2)}) collective-permute-start(bf16[128,256]{1,0:T(8,128)(2,1)S(1)} %bitcast.28), channel_id=1, source_target_pairs={{8,0},{26,2},{44,4},{62,6},{16,8},{34,10},{52,12},{6,14},{24,16},{... | collective-permute-start | bytes 196616 | tf_op jit(solution)/shard_map/ppermute | solution.py:197
  124.9 2.3 %collective-permute-start.1 = (bf16[128,256]{1,0:T(8,128)(2,1)S(1)}, bf16[128,256]{1,0:T(8,128)(2,1)S(1)}, u32[]{:S(2)}, u32[]{:S(2)}) collective-permute-start(bf16[128,256]{1,0:T(8,128)(2,1)S(1)} %bitcast.29), channel_id=1, source_target_pairs={{0,0},{18,2},{36,4},{54,6},{8,8},{26,10},{44,12},{62,14},{16,16},{... | collective-permute-start | bytes 196616 | tf_op jit(solution)/shard_map/ppermute | solution.py:197
  127.2 23.6 %collective-permute-start.4 = (bf16[2,128,256]{2,1,0:T(8,128)(2,1)S(1)}, bf16[2,128,256]{2,1,0:T(8,128)(2,1)S(1)}, u32[]{:S(2)}, u32[]{:S(2)}) collective-permute-start(bf16[2,128,256]{2,1,0:T(8,128)(2,1)S(1)} %get-tuple-element.10), channel_id=1, source_target_pairs={{4,0},{6,2},{0,4},{2,6},{5,1},{7,3},{1,5},{3,7},{12,8},{14,10},{8,... | collective-permute-start | bytes 393224 | tf_op jit(solution)/shard_map/ppermute | solution.py:201
  144.8 7.1 %collective-permute-start.3 = (bf16[2,128,256]{2,1,0:T(8,128)(2,1)S(1)}, bf16[2,128,256]{2,1,0:T(8,128)(2,1)S(1)}, u32[]{:S(2)}, u32[]{:S(2)}) collective-permute-start(bf16[2,128,256]{2,1,0:T(8,128)(2,1)S(1)} %get-tuple-element.10), channel_id=1, source_target_pairs={{2,0},{4,2},{6,4},{0,6},{3,1},{5,3},{7,5},{1,7},{10,8},{12,10},{14... | collective-permute-start | bytes 393224 | tf_op jit(solution)/shard_map/ppermute | solution.py:201
  146.8 8.3 %collective-permute-start.5 = (bf16[2,128,256]{2,1,0:T(8,128)(2,1)S(1)}, bf16[2,128,256]{2,1,0:T(8,128)(2,1)S(1)}, u32[]{:S(2)}, u32[]{:S(2)}) collective-permute-start(bf16[2,128,256]{2,1,0:T(8,128)(2,1)S(1)} %get-tuple-element.10), channel_id=1, source_target_pairs={{6,0},{0,2},{2,4},{4,6},{7,1},{1,3},{3,5},{5,7},{14,8},{8,10},{10,... | collective-permute-start | bytes 393224 | tf_op jit(solution)/shard_map/ppermute | solution.py:201
  160.4 5.9 %collective-permute-start.6 = (bf16[128,128]{1,0:T(8,128)(2,1)S(1)}, bf16[128,128]{1,0:T(8,128)(2,1)S(1)}, u32[]{:S(2)}, u32[]{:S(2)}) collective-permute-start(bf16[128,128]{1,0:T(8,128)(2,1)S(1)} %convert_element_type.30), channel_id=1, source_target_pairs={{0,64},{1,65},{2,66},{3,67},{4,68},{5,69},{6,70},{7,71},{8,72},{9,... | collective-permute-start | bytes 98312 | tf_op jit(solution)/shard_map/ppermute | solution.py:227
  166.3 0.7 collective-permute-start.7
  167.0 0.7 collective-permute-start.8

commit v6 on v4

--- a/solution.py
+++ b/solution.py
@@ -68,11 +68,12 @@
         along = jnp.dot(paired, table_ref[...], preferred_element_type=F32)
         along_ref[gx] = along.astype(BF16)
     per_tile = LANES // beams
-    for block in range(blocks):
+    group = max(tall, 16)
+    for first in range(0, chans, group):
         for tile in range(GY // LANES):
             power = [[] for _ in range(GX)]
             for t in range(times):
-                r = pl.ds(t * chans + block * tall, tall)
+                r = pl.ds(t * chans + first, group)
                 re = [along_ref[gx, r, pl.ds(tile * LANES, LANES)].astype(F32) for gx in range(GX)]
                 im = [along_ref[gx, r, pl.ds(GY + tile * LANES, LANES)].astype(F32) for gx in range(GX)]
                 er, ei, orr, oi = re[0] + re[2], im[0] + im[2], re[1] + re[3], im[1] + im[3]
@@ -83,8 +84,12 @@
                     power[bx].append(0.5 * (fr * fr + fi * fi))
             for bx in range(GX):
                 for part in range(per_tile):
-                    peer = (block * near + tile * per_tile + part) * GX + bx
-                    out_ref[peer] = lane_blocks(power[bx], beams, part).astype(BF16)
+                    slab = tile * per_tile + part
+                    for u in range(times // per_tile):
+                        packed = lane_blocks(power[bx][u * per_tile : (u + 1) * per_tile], beams, part)
+                        for row in range(0, group, tall):
+                            peer = ((first + row) // tall * near + slab) * GX + bx
+                            out_ref[peer, :, pl.ds(u * LANES, LANES)] = packed[row : row + tall].astype(BF16)
 
 
 def dedisperse_kernel(beams, place_ref, own_any, other_any, lag_any, out_ref, total_ref, own_ref, other_ref, lag_ref, level_ref, sems):
@@ -100,47 +105,50 @@
     chunk = 8
     low = place_ref[0] == 0
 
+    tiles = width // LANES
+
     def center(i, carry):
         mine = own_ref[pl.ds(i * chunk, chunk)].astype(F32).reshape(chunk * tall, width)
         theirs = other_ref[pl.ds(i * chunk, chunk)].astype(F32).reshape(chunk * tall, width)
-        early = jnp.where(low, mine, theirs)
-        late = jnp.where(low, theirs, mine)
-        total = early + late
-        amount = width // 2
+        levels = []
+        for half in (jnp.where(low, mine, theirs), jnp.where(low, theirs, mine)):
+            levels += [half[:, u * LANES : (u + 1) * LANES] for u in range(tiles)]
+        total = sum(levels[1:], levels[0])
+        amount = LANES // 2
         while amount >= beams:
             total = total + pltpu.roll(total, amount, 1)
             amount //= 2
         mean = total * (0.5 * beams / width)
         r = pl.ds(pl.multiple_of(i * (chunk * tall), chunk * tall), chunk * tall)
-        level_ref[0, r, :] = early - mean
-        level_ref[1, r, :] = late - mean
+        for u, level in enumerate(levels):
+            level_ref[u, r, :] = level - mean
         return carry
 
     lax.fori_loop(0, sources // chunk, center, 0)
-    lane = iota((out_ref.shape[1], width), 1)
-    running = None
+    lane = iota((out_ref.shape[1], LANES), 1)
+    running = [None] * tiles
     for b in range(bands):
         rows = []
         for s in range(subs):
             r = pl.ds(b * subs + s, sources, stride=tall)
-            rows.append(jnp.concatenate([level_ref[0, r, :].astype(BF16), level_ref[1, r, :].astype(BF16)], axis=1))
+            rows.append(jnp.concatenate([level_ref[u, r, :].astype(BF16) for u in range(2 * tiles)], axis=1))
         data = jnp.concatenate(rows, axis=0)
         lags = lag_ref[lax.rem(b + bands - place_ref[1], bands)].astype(F32)
-        chosen = [jnp.where(lags == float(v), 1.0, 0.0).astype(BF16) for v in range(LAGS)]
         for v in range(LAGS):
-            picked = jnp.dot(chosen[v], data, preferred_element_type=F32)
-            first, second = picked[:, :width], picked[:, width:]
-            offset = v * beams
-            if offset == 0:
-                part = first
-            elif offset == width:
-                part = second
-            else:
-                back = width - offset
-                part = jnp.where(lane < back, pltpu.roll(first, back, 1), pltpu.roll(second, back, 1))
-            running = part if running is None else running + part
-        out_ref[b] = running
-    total_ref[...] = running
+            chosen = jnp.where(lags == float(v), 1.0, 0.0).astype(BF16)
+            picked = jnp.dot(chosen, data, preferred_element_type=F32)
+            for u in range(tiles):
+                whole, rest = divmod(v * beams + u * LANES, LANES)
+                part = picked[:, whole * LANES : (whole + 1) * LANES]
+                if rest:
+                    after = picked[:, (whole + 1) * LANES : (whole + 2) * LANES]
+                    back = LANES - rest
+                    part = jnp.where(lane < back, pltpu.roll(part, back, 1), pltpu.roll(after, back, 1))
+                running[u] = part if running[u] is None else running[u] + part
+        for u in range(tiles):
+            out_ref[b, :, pl.ds(u * LANES, LANES)] = running[u]
+    for u in range(tiles):
+        total_ref[:, pl.ds(u * LANES, LANES)] = running[u]
 
 
 def spread_kernel(beams, scale, in_any, out_ref, in_ref, sem):
@@ -148,11 +156,15 @@
     copy.start()
     copy.wait()
     slabs, trials, width = in_ref.shape
-    count = width // beams
+    times = width // beams
+    count = LANES // beams
+    stride = slabs // count * times
     for tile in range(slabs // count):
-        parts = [in_ref[tile * count + i].astype(F32) * scale for i in range(count)]
-        for t in range(count):
-            out_ref[pl.ds(tile * count + t, trials, stride=slabs), :] = lane_blocks(parts, beams, t)
+        for t in range(times):
+            source, shift = t * beams // LANES, t * beams % LANES // beams
+            cut = pl.ds(source * LANES, LANES)
+            parts = [in_ref[tile * count + i, :, cut].astype(F32) * scale for i in range(count)]
+            out_ref[pl.ds(tile * times + t, trials, stride=stride), :] = lane_blocks(parts, beams, shift)
 
 
 def search(voltages, grid_feed, delays):
@@ -207,34 +219,37 @@
             pltpu.VMEM(own.shape, BF16),
             pltpu.VMEM(own.shape, BF16),
             pltpu.VMEM(lags.shape, BF16),
-            pltpu.VMEM((2, peers * tall, times * beams), F32),
+            pltpu.VMEM((2 * times * beams // LANES, peers * tall, LANES), F32),
             pltpu.SemaphoreType.DMA((3,)),
         ],
         compiler_params=pltpu.CompilerParams(vmem_limit_bytes=24 * 2**20),
         cost_estimate=pl.CostEstimate(flops=2 * 10**9, bytes_accessed=4 * 10**6, transcendentals=0),
         name="dedisperse",
     )(place, own, other, lags)
-    base = jnp.zeros_like(total)
-    for k in range(blocks - 1):
-        message = (base + total).astype(BF16)
-        base = base + lax.ppermute(message, "far", [(k, k + 1)]).astype(F32)
+    inner = lax.ppermute(total.astype(BF16), "far", [(k, k + 1) for k in range(0, blocks, 2)]).astype(F32)
+    through = total + inner
+    before = jnp.zeros_like(total)
+    for k in range(1, blocks - 2, 2):
+        before = before + lax.ppermute((before + through).astype(BF16), "far", [(k, k + 2)]).astype(F32)
+    handed = lax.ppermute((before + through).astype(BF16), "far", [(k, k + 1) for k in range(1, blocks - 1, 2)])
+    base = inner + before + handed.astype(F32)
     cumulative = (local + base).astype(BF16)
     slabs = lax.all_to_all(cumulative, "near", split_axis=0, concat_axis=0, tiled=True)
     spread = pl.pallas_call(
         functools.partial(spread_kernel, beams, 1.0 / math.sqrt(FREQS)),
-        out_shape=jax.ShapeDtypeStruct((trials * near, LANES), F32),
+        out_shape=jax.ShapeDtypeStruct((trials * times * near * beams // LANES, LANES), F32),
         in_specs=[anywhere],
         out_specs=vmem,
         scratch_shapes=[pltpu.VMEM(slabs.shape, BF16), pltpu.SemaphoreType.DMA],
         compiler_params=pltpu.CompilerParams(vmem_limit_bytes=24 * 2**20),
         name="spread",
     )(slabs)
-    spread = jnp.transpose(spread.reshape(trials, near // times, times, LANES), (0, 2, 1, 3))
+    spread = jnp.transpose(spread.reshape(trials, near * beams // LANES, times, LANES), (0, 2, 1, 3))
     return spread.reshape(1, trials, times, near * beams)
 
 
 def solution(mesh):
-    near = 8
+    near = 4
     sizes = mesh.shape
     devices = mesh.devices.reshape(sizes["grp"], sizes["freq"] // near, near, sizes["beam"], sizes["dm"])
     split = Mesh(devices, ("grp", "far", "near", "beam", "dm"))

time: 185 us -> 170 us (0.919)
  the two profiles are of different devices: /device:TPU:40 before, /device:TPU:296 now
where the time goes in v6:
time: 170 us
  blocking collectives  137 us (81%)
  waiting for transfers between devices  12.9 us (8%)
  Pallas kernels  9.85 us (6%)
  starting transfers between devices  9.58 us (6%)
    all_to_all x1, blocking collectives, search(): lax.all_to_all(sent, ('far', 'near', 'beam'), split_axis=0, concat_axis=0...  104 us
    all_gather x1, blocking collectives, search(): lax.all_gather(jnp.stack(fetched), 'beam').reshape(near, trials, subs)  20.6 us
    all_to_all x1, blocking collectives, search(): lax.all_to_all(cumulative, 'near', split_axis=0, concat_axis=0, tiled=True)  12.1 us
    ppermute x1, waiting for transfers between devices, search(): lax.ppermute(total.astype(BF16), 'far', [(k, k + 1) for k in range(0, blo...  8.78 us
    pallas_call x1, Pallas kernels, search(): pl.pallas_call(functools.partial(front_kernel, times, blocks, near, beams...  5.67 us
    ppermute x3, starting transfers between devices, search(): lax.ppermute((before + through).astype(BF16), 'far', [(k, k + 2)])  4.36 us
  transfers between devices with their start and end apart: 7, of which 3 were waited for; matrix products, arithmetic and copies ran while one was open for 0% of the time, Pallas kernels for 0%

profile of v6, /device:TPU:296, one launch (start us, length us, event | category | flops | bytes accessed | tf_op | source)
XLA Modules:
  0.0 169.6 jit_solution(16825156199921885084)
XLA Ops:
  0.0 5.7 %front.1 = bf16[128,8,256]{2,1,0:T(8,128)(2,1)} custom-call(bf16[256,2,1024]{2,1,0:T(2,128)(2,1)} %bitcast.21, s32[1,1024]{1,0:T(1,128)} %bitcast.22, bf16[512,512]{1,0:T(8,128)(2,1)} %constant.11.clone.table_any), custom_call_target="tpu_custom_call" | custom-call | flops 2000000000 | bytes 4000000 | tf_op jit(solution)/shard_map/front/pallas_call | solution.py:186
  5.7 0.0 copy-start
  5.7 104.0 %all_to_all.10.own_any = bf16[128,8,256]{2,1,0:T(8,128)(2,1)S(1)} all-to-all(bf16[128,8,256]{2,1,0:T(8,128)(2,1)} %front.1), channel_id=1, replica_groups=mesh['grp'=2,'far'=8,'near'=4,'beam'=4,'dm'=2] {'far','near','beam'}, dimensions={0} | all-to-all | bytes 1048576 | tf_op jit(solution)/shard_map/all_to_all | solution.py:200
  109.7 1.9 %collective-permute-start = (bf16[128,8,256]{2,1,0:T(8,128)(2,1)S(1)}, bf16[128,8,256]{2,1,0:T(8,128)(2,1)S(1)}, u32[]{:S(2)}, u32[]{:S(2)}) collective-permute-start(bf16[128,8,256]{2,1,0:T(8,128)(2,1)S(1)} %all_to_all.10.own_any), channel_id=1, source_target_pairs={{0,1},{1,0},{2,3},{3,2},{4,5},{5,4},{6,7},{7,6},{8,9},{9,8},{10,11... | collective-permute-start | bytes 1572872 | tf_op jit(solution)/shard_map/ppermute | solution.py:208
  111.7 0.1 copy.5
  111.8 0.7 collective-permute-start.1
  112.5 0.1 pad_add_fusion.place_ref
  112.6 0.0 collective-permute-done.1
  112.6 20.6 %all-gather = bf16[512,256]{1,0:T(8,128)(2,1)S(1)} all-gather(bf16[128,256]{1,0:T(8,128)(2,1)S(1)} %collective-permute-done.1), channel_id=2, replica_groups=mesh['grp'=2,'far'=8,'near'=4,'beam'=4,'dm'=2] {'beam'}, dimensions={0}, use_global_device_ids=true | all-gather | bytes 327680 | tf_op jit(solution)/shard_map/all_gather | solution.py:207
  133.2 0.0 collective-permute-done.other_any
  133.2 3.1 %dedisperse.1 = (f32[4,128,256]{2,1,0:T(8,128)S(1)}, f32[128,256]{1,0:T(8,128)S(1)}) custom-call(s32[2]{0:T(128)S(1)} %pad_add_fusion.place_ref, bf16[128,8,256]{2,1,0:T(8,128)(2,1)S(1)} %all_to_all.10.own_any, bf16[128,8,256]{2,1,0:T(8,128)(2,1)S(1)} %collective-permute-done.other_any, bf16[4,128,256]{2,1,0:T(8,128)(2,1)S(1)} %bitcast.17), custom_call_target="tpu_custom_call" | custom-call | flops 2000000000 | bytes 4000000 | tf_op jit(solution)/shard_map/dedisperse/pallas_call | solution.py:210
  136.3 1.3 collective-permute-start.2
  137.6 8.8 %collective-permute-done.2 = bf16[128,256]{1,0:T(8,128)(2,1)S(1)} collective-permute-done((bf16[128,256]{1,0:T(8,128)(2,1)S(1)}, bf16[128,256]{1,0:T(8,128)(2,1)S(1)}, u32[]{:S(2)}, u32[]{:S(2)}) %collective-permute-start.2) | collective-permute-done | bytes 65568 | tf_op jit(solution)/shard_map/ppermute | solution.py:229
  146.4 3.0 %collective-permute-start.3 = (bf16[128,256]{1,0:T(8,128)(2,1)S(1)}, bf16[128,256]{1,0:T(8,128)(2,1)S(1)}, u32[]{:S(2)}, u32[]{:S(2)}) collective-permute-start(bf16[128,256]{1,0:T(8,128)(2,1)S(1)} %fusion.2), channel_id=1, source_target_pairs={{32,96},{33,97},{34,98},{35,99},{36,100},{37,101},{38,102},{39,103... | collective-permute-start | bytes 196616 | tf_op jit(solution)/shard_map/ppermute | solution.py:233
  149.5 1.9 %collective-permute-done.3 = bf16[128,256]{1,0:T(8,128)(2,1)S(1)} collective-permute-done((bf16[128,256]{1,0:T(8,128)(2,1)S(1)}, bf16[128,256]{1,0:T(8,128)(2,1)S(1)}, u32[]{:S(2)}, u32[]{:S(2)}) %collective-permute-start.3) | collective-permute-done | bytes 65568 | tf_op jit(solution)/shard_map/ppermute | solution.py:233
  151.4 0.7 collective-permute-start.4
  152.1 0.0 collective-permute-done.4
  152.1 0.7 collective-permute-start.5
  152.8 0.0 collective-permute-done.5
  152.9 1.3 collective-permute-start.6
  154.2 2.2 %collective-permute-done.6 = bf16[128,256]{1,0:T(8,128)(2,1)S(1)} collective-permute-done((bf16[128,256]{1,0:T(8,128)(2,1)S(1)}, bf16[128,256]{1,0:T(8,128)(2,1)S(1)}, u32[]{:S(2)}, u32[]{:S(2)}) %collective-permute-start.6) | collective-permute-done | bytes 65568 | tf_op jit(solution)/shard_map/ppermute | solution.py:234
  156.4 0.1 add_convert_fusion
  156.5 12.1 %all_to_all.11.in_any = bf16[4,128,256]{2,1,0:T(8,128)(2,1)S(1)} all-to-all(bf16[4,128,256]{2,1,0:T(8,128)(2,1)S(1)} %add_convert_fusion), channel_id=1, replica_groups=mesh['grp'=2,'far'=8,'near'=4,'beam'=4,'dm'=2] {'near'}, dimensions={0} | all-to-all | bytes 524288 | tf_op jit(solution)/shard_map/all_to_all | solution.py:237
  168.5 1.0 spread.1
  (9 shorter events, 0.2 us)
Async XLA Ops:
  5.7 106.0 %copy-start = (s32[1,256,128]{2,1,0:T(8,128)S(1)}, s32[1,256,128]{2,1,0:T(8,128)}, u32[]{:S(2)}) copy-start(s32[1,256,128]{2,1,0:T(8,128)} %param.6) | copy-start | bytes 393220
  109.7 23.5 %collective-permute-start = (bf16[128,8,256]{2,1,0:T(8,128)(2,1)S(1)}, bf16[128,8,256]{2,1,0:T(8,128)(2,1)S(1)}, u32[]{:S(2)}, u32[]{:S(2)}) collective-permute-start(bf16[128,8,256]{2,1,0:T(8,128)(2,1)S(1)} %all_to_all.10.own_any), channel_id=1, source_target_pairs={{0,1},{1,0},{2,3},{3,2},{4,5},{5,4},{6,7},{7,6},{8,9},{9,8},{10,11... | collective-permute-start | bytes 1572872 | tf_op jit(solution)/shard_map/ppermute | solution.py:208
  111.8 0.8 collective-permute-start.1
  136.3 10.1 %collective-permute-start.2 = (bf16[128,256]{1,0:T(8,128)(2,1)S(1)}, bf16[128,256]{1,0:T(8,128)(2,1)S(1)}, u32[]{:S(2)}, u32[]{:S(2)}) collective-permute-start(bf16[128,256]{1,0:T(8,128)(2,1)S(1)} %convert_element_type.42), channel_id=1, source_target_pairs={{0,32},{64,96},{128,160},{192,224},{1,33},{65,97},{129,161},{193,2... | collective-permute-start | bytes 196616 | tf_op jit(solution)/shard_map/ppermute | solution.py:229
  146.4 4.9 %collective-permute-start.3 = (bf16[128,256]{1,0:T(8,128)(2,1)S(1)}, bf16[128,256]{1,0:T(8,128)(2,1)S(1)}, u32[]{:S(2)}, u32[]{:S(2)}) collective-permute-start(bf16[128,256]{1,0:T(8,128)(2,1)S(1)} %fusion.2), channel_id=1, source_target_pairs={{32,96},{33,97},{34,98},{35,99},{36,100},{37,101},{38,102},{39,103... | collective-permute-start | bytes 196616 | tf_op jit(solution)/shard_map/ppermute | solution.py:233
  151.4 0.7 collective-permute-start.4
  152.1 0.7 collective-permute-start.5
  152.9 3.5 %collective-permute-start.6 = (bf16[128,256]{1,0:T(8,128)(2,1)S(1)}, bf16[128,256]{1,0:T(8,128)(2,1)S(1)}, u32[]{:S(2)}, u32[]{:S(2)}) collective-permute-start(bf16[128,256]{1,0:T(8,128)(2,1)S(1)} %add_convert_fusion.1), channel_id=1, source_target_pairs={{32,64},{96,128},{160,192},{33,65},{97,129},{161,193},{34,66},{98,... | collective-permute-start | bytes 196616 | tf_op jit(solution)/shard_map/ppermute | solution.py:234

commit v7 on v6

--- a/solution.py
+++ b/solution.py
@@ -45,11 +45,7 @@
     return result
 
 
-def front_kernel(times, blocks, near, beams, volt_any, feed_ref, table_any, out_ref, volt_ref, table_ref, along_ref, sems):
-    load = pltpu.make_async_copy(volt_any, volt_ref, sems.at[0])
-    load_table = pltpu.make_async_copy(table_any, table_ref, sems.at[1])
-    load.start()
-    load_table.start()
+def front_kernel(times, blocks, near, beams, volt_ref, feed_ref, table_ref, out_ref, along_ref):
     rows, feeds = 2 * volt_ref.shape[0], volt_ref.shape[2]
     half = rows // 2
     chans = half // times
@@ -58,8 +54,6 @@
     source = i % chans * (2 * times) + i // chans % times * 2 + i // half
     order = jnp.where(iota((rows, rows), 1) == source, 1.0, 0.0).astype(BF16)
     pick = jnp.where(iota((feeds, feeds), 0) == feed_ref[...], 1.0, 0.0).astype(BF16)
-    load.wait()
-    load_table.wait()
     planes = jnp.dot(order, volt_ref[...].reshape(rows, feeds), preferred_element_type=F32).astype(BF16)
     grid = jnp.dot(planes, pick, preferred_element_type=F32).astype(BF16)
     for gx in range(GX):
@@ -180,20 +174,12 @@
     vmem = pl.BlockSpec(memory_space=pltpu.VMEM)
     anywhere = pl.BlockSpec(memory_space=pl.ANY)
 
-    lag_rows = delays[0].astype(BF16).reshape(peers, sub_local, trials)
-    lag_rows = jnp.transpose(lag_rows, (2, 1, 0)).reshape(trials, subs)
-
     sent = pl.pallas_call(
         functools.partial(front_kernel, times, blocks, near, beams),
         out_shape=jax.ShapeDtypeStruct((peers, tall, times * beams), BF16),
-        in_specs=[anywhere, vmem, anywhere],
+        in_specs=[vmem] * 3,
         out_specs=vmem,
-        scratch_shapes=[
-            pltpu.VMEM((rows // 2, 2, feeds), BF16),
-            pltpu.VMEM((2 * GY, 2 * GY), BF16),
-            pltpu.VMEM((GX, rows // 2, 2 * GY), BF16),
-            pltpu.SemaphoreType.DMA((2,)),
-        ],
+        scratch_shapes=[pltpu.VMEM((GX, rows // 2, 2 * GY), BF16)],
         cost_estimate=pl.CostEstimate(flops=2 * 10**9, bytes_accessed=4 * 10**6, transcendentals=0),
         name="front",
     )(voltages.reshape(rows // 2, 2, feeds), grid_feed.reshape(1, feeds), jnp.asarray(steering_table(GY)))
@@ -203,8 +189,10 @@
     for j in range(share):
         steps = [(n, x, (n + x * share + j) % near) for n in range(near) for x in range(columns)]
         pairs = [(source * columns + x, n * columns + x) for n, x, source in steps]
-        fetched.append(lax.ppermute(lag_rows, ("near", "beam"), pairs))
-    lags = lax.all_gather(jnp.stack(fetched), "beam").reshape(near, trials, subs)
+        fetched.append(lax.ppermute(delays, ("near", "beam"), pairs))
+    lags = jnp.concatenate(fetched).astype(BF16).reshape(share, peers, sub_local, trials)
+    lags = jnp.transpose(lags, (0, 3, 2, 1)).reshape(share, trials, subs)
+    lags = lax.all_gather(lags, "beam").reshape(near, trials, subs)
     other = lax.ppermute(own, "dm", [(0, 1), (1, 0)])
     place = jnp.stack([lax.axis_index("dm"), lax.axis_index("near")]).astype(jnp.int32)
     local, total = pl.pallas_call(
@@ -226,13 +214,14 @@
         cost_estimate=pl.CostEstimate(flops=2 * 10**9, bytes_accessed=4 * 10**6, transcendentals=0),
         name="dedisperse",
     )(place, own, other, lags)
-    inner = lax.ppermute(total.astype(BF16), "far", [(k, k + 1) for k in range(0, blocks, 2)]).astype(F32)
+    mine = total.astype(BF16)
+    inner = lax.ppermute(mine, "far", [(k, k + 1) for k in range(blocks - 1)]).astype(F32)
+    before = lax.ppermute(mine, "far", [(0, 2)]).astype(F32)
     through = total + inner
-    before = jnp.zeros_like(total)
     for k in range(1, blocks - 2, 2):
-        before = before + lax.ppermute((before + through).astype(BF16), "far", [(k, k + 2)]).astype(F32)
-    handed = lax.ppermute((before + through).astype(BF16), "far", [(k, k + 1) for k in range(1, blocks - 1, 2)])
-    base = inner + before + handed.astype(F32)
+        pairs = [(k, k + 2)] if k == 1 else [(k - 1, k + 1), (k, k + 2)]
+        before = before + lax.ppermute((before + through).astype(BF16), "far", pairs).astype(F32)
+    base = inner + before
     cumulative = (local + base).astype(BF16)
     slabs = lax.all_to_all(cumulative, "near", split_axis=0, concat_axis=0, tiled=True)
     spread = pl.pallas_call(

time: 170 us -> 173 us (1.018)
  the two profiles are of different devices: /device:TPU:296 before, /device:TPU:40 now
where the time goes in v7:
time: 173 us; the launch traced here: 172 us
  blocking collectives  150 us (87%)
  starting transfers between devices  11.1 us (6%)
  Pallas kernels  9.24 us (5%)
  waiting for transfers between devices  1.9 us (1%)
    all_to_all x1, blocking collectives, search(): lax.all_to_all(sent, ('far', 'near', 'beam'), split_axis=0, concat_axis=0...  110 us
    all_gather x1, blocking collectives, search(): lags = lax.all_gather(lags, 'beam').reshape(near, trials, subs)  25.2 us
    all_to_all x1, blocking collectives, search(): lax.all_to_all(cumulative, 'near', split_axis=0, concat_axis=0, tiled=True)  14.6 us
    ppermute x1, starting transfers between devices, search(): before = lax.ppermute(mine, 'far', [(0, 2)]).astype(F32)  5.18 us
    pallas_call x1, Pallas kernels, search(): pl.pallas_call(functools.partial(front_kernel, times, blocks, near, beams...  5.07 us
  transfers between devices with their start and end apart: 7, of which 2 were waited for; matrix products, arithmetic and copies ran while one was open for 0% of the time, Pallas kernels for 0%

profile of v7, /device:TPU:40, one launch (start us, length us, event | category | flops | bytes accessed | tf_op | source)
XLA Modules:
  0.0 172.4 jit_solution(3454127587262471454)
XLA Ops:
  0.0 5.1 %front.1 = bf16[128,8,256]{2,1,0:T(8,128)(2,1)} custom-call(bf16[256,2,1024]{2,1,0:T(2,128)(2,1)} %bitcast.15, s32[1,1024]{1,0:T(1,128)} %bitcast.16, bf16[512,512]{1,0:T(8,128)(2,1)} %constant.11.clone.table_ref), custom_call_target="tpu_custom_call" | custom-call | flops 2000000000 | bytes 4000000 | tf_op jit(solution)/shard_map/front/pallas_call | solution.py:177
  5.1 109.8 %all_to_all.10.own_any = bf16[128,8,256]{2,1,0:T(8,128)(2,1)S(1)} all-to-all(bf16[128,8,256]{2,1,0:T(8,128)(2,1)} %front.1), channel_id=1, replica_groups=mesh['grp'=2,'far'=8,'near'=4,'beam'=4,'dm'=2] {'far','near','beam'}, dimensions={0} | all-to-all | bytes 1048576 | tf_op jit(solution)/shard_map/all_to_all | solution.py:186
  114.9 1.9 %collective-permute-start = (bf16[128,8,256]{2,1,0:T(8,128)(2,1)S(1)}, bf16[128,8,256]{2,1,0:T(8,128)(2,1)S(1)}, u32[]{:S(2)}, u32[]{:S(2)}) collective-permute-start(bf16[128,8,256]{2,1,0:T(8,128)(2,1)S(1)} %all_to_all.10.own_any), channel_id=1, source_target_pairs={{0,1},{1,0},{2,3},{3,2},{4,5},{5,4},{6,7},{7,6},{8,9},{9,8},{10,11... | collective-permute-start | bytes 1572872 | tf_op jit(solution)/shard_map/ppermute | solution.py:196
  116.8 0.0 copy-done
  116.8 0.7 collective-permute-start.1
  117.5 0.1 pad_add_fusion.place_ref
  117.6 0.0 collective-permute-done.1
  117.6 0.1 copy.7
  117.8 25.2 %all_gather.3 = bf16[4,1,128,256]{3,2,1,0:T(8,128)(2,1)S(1)} all-gather(bf16[1,1,128,256]{3,2,1,0:T(8,128)(2,1)S(1)} %all_gather_reshape.3), channel_id=1, replica_groups=mesh['grp'=2,'far'=8,'near'=4,'beam'=4,'dm'=2] {'beam'}, dimensions={0}, use_global_device_ids=true | all-gather | bytes 327680 | tf_op jit(solution)/shard_map/all_gather | solution.py:195
  143.0 0.0 collective-permute-done.other_any
  143.0 3.1 %dedisperse.1 = (f32[4,128,256]{2,1,0:T(8,128)S(1)}, f32[128,256]{1,0:T(8,128)S(1)}) custom-call(s32[2]{0:T(128)S(1)} %pad_add_fusion.place_ref, bf16[128,8,256]{2,1,0:T(8,128)(2,1)S(1)} %all_to_all.10.own_any, bf16[128,8,256]{2,1,0:T(8,128)(2,1)S(1)} %collective-permute-done.other_any, bf16[4,128,256]{2,1,0:T(8,128)(2,1)S(1)} %bitcast.12), custom_call_target="tpu_custom_call" | custom-call | flops 2000000000 | bytes 4000000 | tf_op jit(solution)/shard_map/dedisperse/pallas_call | solution.py:198
  146.1 5.2 %collective-permute-start.3 = (bf16[128,256]{1,0:T(8,128)(2,1)S(1)}, bf16[128,256]{1,0:T(8,128)(2,1)S(1)}, u32[]{:S(2)}, u32[]{:S(2)}) collective-permute-start(bf16[128,256]{1,0:T(8,128)(2,1)S(1)} %convert_element_type.34), channel_id=1, source_target_pairs={{0,64},{1,65},{2,66},{3,67},{4,68},{5,69},{6,70},{7,71},{8,72},{9,... | collective-permute-start | bytes 196616 | tf_op jit(solution)/shard_map/ppermute | solution.py:219
  151.3 1.3 collective-permute-start.2
  152.6 0.6 collective-permute-done.3
  153.2 1.3 collective-permute-done.2
  154.5 0.7 collective-permute-start.4
  155.2 0.0 collective-permute-done.4
  155.3 0.7 collective-permute-start.5
  155.9 0.0 collective-permute-done.5
  156.0 0.7 collective-permute-start.6
  156.7 0.0 collective-permute-done.6
  156.7 0.1 add_convert_fusion
  156.8 14.6 %all_to_all.11.in_any = bf16[4,128,256]{2,1,0:T(8,128)(2,1)S(1)} all-to-all(bf16[4,128,256]{2,1,0:T(8,128)(2,1)S(1)} %add_convert_fusion), channel_id=1, replica_groups=mesh['grp'=2,'far'=8,'near'=4,'beam'=4,'dm'=2] {'near'}, dimensions={0} | all-to-all | bytes 524288 | tf_op jit(solution)/shard_map/all_to_all | solution.py:226
  171.4 1.0 spread.1
  (8 shorter events, 0.2 us)
Async XLA Ops:
  5.1 111.8 %copy-start = (s32[1,256,128]{2,1,0:T(8,128)S(1)}, s32[1,256,128]{2,1,0:T(8,128)}, u32[]{:S(2)}) copy-start(s32[1,256,128]{2,1,0:T(8,128)} %param.6) | copy-start | bytes 393220
  114.9 28.1 %collective-permute-start = (bf16[128,8,256]{2,1,0:T(8,128)(2,1)S(1)}, bf16[128,8,256]{2,1,0:T(8,128)(2,1)S(1)}, u32[]{:S(2)}, u32[]{:S(2)}) collective-permute-start(bf16[128,8,256]{2,1,0:T(8,128)(2,1)S(1)} %all_to_all.10.own_any), channel_id=1, source_target_pairs={{0,1},{1,0},{2,3},{3,2},{4,5},{5,4},{6,7},{7,6},{8,9},{9,8},{10,11... | collective-permute-start | bytes 1572872 | tf_op jit(solution)/shard_map/ppermute | solution.py:196
  116.8 0.8 collective-permute-start.1
  146.1 7.1 %collective-permute-start.3 = (bf16[128,256]{1,0:T(8,128)(2,1)S(1)}, bf16[128,256]{1,0:T(8,128)(2,1)S(1)}, u32[]{:S(2)}, u32[]{:S(2)}) collective-permute-start(bf16[128,256]{1,0:T(8,128)(2,1)S(1)} %convert_element_type.34), channel_id=1, source_target_pairs={{0,64},{1,65},{2,66},{3,67},{4,68},{5,69},{6,70},{7,71},{8,72},{9,... | collective-permute-start | bytes 196616 | tf_op jit(solution)/shard_map/ppermute | solution.py:219
  151.3 3.2 %collective-permute-start.2 = (bf16[128,256]{1,0:T(8,128)(2,1)S(1)}, bf16[128,256]{1,0:T(8,128)(2,1)S(1)}, u32[]{:S(2)}, u32[]{:S(2)}) collective-permute-start(bf16[128,256]{1,0:T(8,128)(2,1)S(1)} %convert_element_type.34), channel_id=1, source_target_pairs={{0,32},{32,64},{64,96},{96,128},{128,160},{160,192},{192,224},{1,3... | collective-permute-start | bytes 196616 | tf_op jit(solution)/shard_map/ppermute | solution.py:218
  154.5 0.7 collective-permute-start.4
  155.3 0.7 collective-permute-start.5
  156.0 0.7 collective-permute-start.6

commit v8 on v7

--- a/solution.py
+++ b/solution.py
@@ -214,14 +214,15 @@
         cost_estimate=pl.CostEstimate(flops=2 * 10**9, bytes_accessed=4 * 10**6, transcendentals=0),
         name="dedisperse",
     )(place, own, other, lags)
-    mine = total.astype(BF16)
-    inner = lax.ppermute(mine, "far", [(k, k + 1) for k in range(blocks - 1)]).astype(F32)
-    before = lax.ppermute(mine, "far", [(0, 2)]).astype(F32)
+    inner = lax.ppermute(total.astype(BF16), "far", [(k, k + 1) for k in range(0, blocks, 2)]).astype(F32)
     through = total + inner
-    for k in range(1, blocks - 2, 2):
-        pairs = [(k, k + 2)] if k == 1 else [(k - 1, k + 1), (k, k + 2)]
-        before = before + lax.ppermute((before + through).astype(BF16), "far", pairs).astype(F32)
-    base = inner + before
+    known = through.astype(BF16)
+    before = lax.ppermute(known, "far", [(1, 3)]).astype(F32)
+    handed = lax.ppermute(known, "far", [(1, 2)]).astype(F32)
+    for k in range(3, blocks - 2, 2):
+        before = before + lax.ppermute((before + through).astype(BF16), "far", [(k, k + 2)]).astype(F32)
+    later = lax.ppermute((before + through).astype(BF16), "far", [(k, k + 1) for k in range(3, blocks - 1, 2)])
+    base = inner + before + handed + later.astype(F32)
     cumulative = (local + base).astype(BF16)
     slabs = lax.all_to_all(cumulative, "near", split_axis=0, concat_axis=0, tiled=True)
     spread = pl.pallas_call(

time: 173 us -> 172 us (level)
  the two profiles are of different devices: /device:TPU:40 before, /device:TPU:296 now
where the time goes in v8:
time: 172 us
  blocking collectives  140 us (81%)
  waiting for transfers between devices  11.8 us (7%)
  starting transfers between devices  10.4 us (6%)
  Pallas kernels  9.24 us (5%)
    all_to_all x1, blocking collectives, search(): lax.all_to_all(sent, ('far', 'near', 'beam'), split_axis=0, concat_axis=0...  104 us
    all_gather x1, blocking collectives, search(): lags = lax.all_gather(lags, 'beam').reshape(near, trials, subs)  23.5 us
    all_to_all x1, blocking collectives, search(): lax.all_to_all(cumulative, 'near', split_axis=0, concat_axis=0, tiled=True)  12.1 us
    ppermute x1, waiting for transfers between devices, search(): lax.ppermute(total.astype(BF16), 'far', [(k, k + 1) for k in range(0, blo...  8.78 us
    pallas_call x1, Pallas kernels, search(): pl.pallas_call(functools.partial(front_kernel, times, blocks, near, beams...  5.07 us
  transfers between devices with their start and end apart: 8, of which 3 were waited for; matrix products, arithmetic and copies ran while one was open for 0% of the time, Pallas kernels for 0%

profile of v8, /device:TPU:296, one launch (start us, length us, event | category | flops | bytes accessed | tf_op | source)
XLA Modules:
  0.0 171.7 jit_solution(2652216176695155972)
XLA Ops:
  0.0 5.1 %front.1 = bf16[128,8,256]{2,1,0:T(8,128)(2,1)} custom-call(bf16[256,2,1024]{2,1,0:T(2,128)(2,1)} %bitcast.15, s32[1,1024]{1,0:T(1,128)} %bitcast.16, bf16[512,512]{1,0:T(8,128)(2,1)} %constant.11.clone.table_ref), custom_call_target="tpu_custom_call" | custom-call | flops 2000000000 | bytes 4000000 | tf_op jit(solution)/shard_map/front/pallas_call | solution.py:177
  5.1 104.0 %all_to_all.10.own_any = bf16[128,8,256]{2,1,0:T(8,128)(2,1)S(1)} all-to-all(bf16[128,8,256]{2,1,0:T(8,128)(2,1)} %front.1), channel_id=1, replica_groups=mesh['grp'=2,'far'=8,'near'=4,'beam'=4,'dm'=2] {'far','near','beam'}, dimensions={0} | all-to-all | bytes 1048576 | tf_op jit(solution)/shard_map/all_to_all | solution.py:186
  109.1 1.9 %collective-permute-start = (bf16[128,8,256]{2,1,0:T(8,128)(2,1)S(1)}, bf16[128,8,256]{2,1,0:T(8,128)(2,1)S(1)}, u32[]{:S(2)}, u32[]{:S(2)}) collective-permute-start(bf16[128,8,256]{2,1,0:T(8,128)(2,1)S(1)} %all_to_all.10.own_any), channel_id=1, source_target_pairs={{0,1},{1,0},{2,3},{3,2},{4,5},{5,4},{6,7},{7,6},{8,9},{9,8},{10,11... | collective-permute-start | bytes 1572872 | tf_op jit(solution)/shard_map/ppermute | solution.py:196
  111.0 0.7 collective-permute-start.1
  111.7 0.1 pad_add_fusion.place_ref
  111.8 0.0 collective-permute-done.1
  111.8 0.1 copy.7
  112.0 23.5 %all_gather.3 = bf16[4,1,128,256]{3,2,1,0:T(8,128)(2,1)S(1)} all-gather(bf16[1,1,128,256]{3,2,1,0:T(8,128)(2,1)S(1)} %all_gather_reshape.3), channel_id=1, replica_groups=mesh['grp'=2,'far'=8,'near'=4,'beam'=4,'dm'=2] {'beam'}, dimensions={0}, use_global_device_ids=true | all-gather | bytes 327680 | tf_op jit(solution)/shard_map/all_gather | solution.py:195
  135.4 0.0 collective-permute-done.other_any
  135.4 3.1 %dedisperse.1 = (f32[4,128,256]{2,1,0:T(8,128)S(1)}, f32[128,256]{1,0:T(8,128)S(1)}) custom-call(s32[2]{0:T(128)S(1)} %pad_add_fusion.place_ref, bf16[128,8,256]{2,1,0:T(8,128)(2,1)S(1)} %all_to_all.10.own_any, bf16[128,8,256]{2,1,0:T(8,128)(2,1)S(1)} %collective-permute-done.other_any, bf16[4,128,256]{2,1,0:T(8,128)(2,1)S(1)} %bitcast.12), custom_call_target="tpu_custom_call" | custom-call | flops 2000000000 | bytes 4000000 | tf_op jit(solution)/shard_map/dedisperse/pallas_call | solution.py:198
  138.6 1.3 collective-permute-start.2
  139.9 8.8 %collective-permute-done.2 = bf16[128,256]{1,0:T(8,128)(2,1)S(1)} collective-permute-done((bf16[128,256]{1,0:T(8,128)(2,1)S(1)}, bf16[128,256]{1,0:T(8,128)(2,1)S(1)}, u32[]{:S(2)}, u32[]{:S(2)}) %collective-permute-start.2) | collective-permute-done | bytes 65568 | tf_op jit(solution)/shard_map/ppermute | solution.py:217
  148.7 3.1 %collective-permute-start.3 = (bf16[128,256]{1,0:T(8,128)(2,1)S(1)}, bf16[128,256]{1,0:T(8,128)(2,1)S(1)}, u32[]{:S(2)}, u32[]{:S(2)}) collective-permute-start(bf16[128,256]{1,0:T(8,128)(2,1)S(1)} %fusion.3), channel_id=1, source_target_pairs={{32,96},{33,97},{34,98},{35,99},{36,100},{37,101},{38,102},{39,103... | collective-permute-start | bytes 196616 | tf_op jit(solution)/shard_map/ppermute | solution.py:220
  151.9 1.9 %collective-permute-done.3 = bf16[128,256]{1,0:T(8,128)(2,1)S(1)} collective-permute-done((bf16[128,256]{1,0:T(8,128)(2,1)S(1)}, bf16[128,256]{1,0:T(8,128)(2,1)S(1)}, u32[]{:S(2)}, u32[]{:S(2)}) %collective-permute-start.3) | collective-permute-done | bytes 65568 | tf_op jit(solution)/shard_map/ppermute | solution.py:220
  153.8 0.7 collective-permute-start.4
  154.5 0.7 collective-permute-start.5
  155.2 1.3 collective-permute-start.6
  156.6 0.7 collective-permute-start.7
  157.2 1.2 collective-permute-done.6
  158.4 0.0 collective-permute-done.7
  158.4 0.1 fusion.1
  158.4 0.1 add_convert_fusion
  158.5 12.1 %all_to_all.11.in_any = bf16[4,128,256]{2,1,0:T(8,128)(2,1)S(1)} all-to-all(bf16[4,128,256]{2,1,0:T(8,128)(2,1)S(1)} %add_convert_fusion), channel_id=1, replica_groups=mesh['grp'=2,'far'=8,'near'=4,'beam'=4,'dm'=2] {'near'}, dimensions={0} | all-to-all | bytes 524288 | tf_op jit(solution)/shard_map/all_to_all | solution.py:227
  170.6 1.0 spread.1
  (11 shorter events, 0.2 us)
Async XLA Ops:
  5.1 105.9 %copy-start = (s32[1,256,128]{2,1,0:T(8,128)S(1)}, s32[1,256,128]{2,1,0:T(8,128)}, u32[]{:S(2)}) copy-start(s32[1,256,128]{2,1,0:T(8,128)} %param.6) | copy-start | bytes 393220
  109.1 26.4 %collective-permute-start = (bf16[128,8,256]{2,1,0:T(8,128)(2,1)S(1)}, bf16[128,8,256]{2,1,0:T(8,128)(2,1)S(1)}, u32[]{:S(2)}, u32[]{:S(2)}) collective-permute-start(bf16[128,8,256]{2,1,0:T(8,128)(2,1)S(1)} %all_to_all.10.own_any), channel_id=1, source_target_pairs={{0,1},{1,0},{2,3},{3,2},{4,5},{5,4},{6,7},{7,6},{8,9},{9,8},{10,11... | collective-permute-start | bytes 1572872 | tf_op jit(solution)/shard_map/ppermute | solution.py:196
  111.0 0.8 collective-permute-start.1
  138.6 10.1 %collective-permute-start.2 = (bf16[128,256]{1,0:T(8,128)(2,1)S(1)}, bf16[128,256]{1,0:T(8,128)(2,1)S(1)}, u32[]{:S(2)}, u32[]{:S(2)}) collective-permute-start(bf16[128,256]{1,0:T(8,128)(2,1)S(1)} %convert_element_type.40), channel_id=1, source_target_pairs={{0,32},{64,96},{128,160},{192,224},{1,33},{65,97},{129,161},{193,2... | collective-permute-start | bytes 196616 | tf_op jit(solution)/shard_map/ppermute | solution.py:217
  148.7 5.0 %collective-permute-start.3 = (bf16[128,256]{1,0:T(8,128)(2,1)S(1)}, bf16[128,256]{1,0:T(8,128)(2,1)S(1)}, u32[]{:S(2)}, u32[]{:S(2)}) collective-permute-start(bf16[128,256]{1,0:T(8,128)(2,1)S(1)} %fusion.3), channel_id=1, source_target_pairs={{32,96},{33,97},{34,98},{35,99},{36,100},{37,101},{38,102},{39,103... | collective-permute-start | bytes 196616 | tf_op jit(solution)/shard_map/ppermute | solution.py:220
  153.8 0.7 collective-permute-start.4
  154.5 2.0 %collective-permute-start.5 = (bf16[128,256]{1,0:T(8,128)(2,1)S(1)}, bf16[128,256]{1,0:T(8,128)(2,1)S(1)}, u32[]{:S(2)}, u32[]{:S(2)}) collective-permute-start(bf16[128,256]{1,0:T(8,128)(2,1)S(1)} %add_convert_fusion.2), channel_id=1, source_target_pairs={{160,224},{161,225},{162,226},{163,227},{164,228},{165,229},{166,2... | collective-permute-start | bytes 196616 | tf_op jit(solution)/shard_map/ppermute | solution.py:223
  155.2 3.2 %collective-permute-start.6 = (bf16[128,256]{1,0:T(8,128)(2,1)S(1)}, bf16[128,256]{1,0:T(8,128)(2,1)S(1)}, u32[]{:S(2)}, u32[]{:S(2)}) collective-permute-start(bf16[128,256]{1,0:T(8,128)(2,1)S(1)} %fusion.3), channel_id=1, source_target_pairs={{32,64},{33,65},{34,66},{35,67},{36,68},{37,69},{38,70},{39,71},{4... | collective-permute-start | bytes 196616 | tf_op jit(solution)/shard_map/ppermute | solution.py:221
  156.6 1.8 %collective-permute-start.7 = (bf16[128,256]{1,0:T(8,128)(2,1)S(1)}, bf16[128,256]{1,0:T(8,128)(2,1)S(1)}, u32[]{:S(2)}, u32[]{:S(2)}) collective-permute-start(bf16[128,256]{1,0:T(8,128)(2,1)S(1)} %add_convert_fusion.1), channel_id=1, source_target_pairs={{96,128},{160,192},{97,129},{161,193},{98,130},{162,194},{99,131},... | collective-permute-start | bytes 196616 | tf_op jit(solution)/shard_map/ppermute | solution.py:224

commit v9 on v8

--- a/solution.py
+++ b/solution.py
@@ -145,10 +145,17 @@
         total_ref[:, pl.ds(u * LANES, LANES)] = running[u]
 
 
-def spread_kernel(beams, scale, in_any, out_ref, in_ref, sem):
-    copy = pltpu.make_async_copy(in_any, in_ref, sem)
-    copy.start()
-    copy.wait()
+def spread_kernel(beams, scale, place_ref, *refs):
+    pieces, (out_ref, in_ref, sems) = refs[:-3], refs[-3:]
+    near = len(pieces)
+    copies = []
+    for d, piece in enumerate(pieces):
+        slab = lax.rem(place_ref[1] + near - d, near)
+        copies.append(pltpu.make_async_copy(piece, in_ref.at[slab], sems.at[d]))
+    for copy in copies:
+        copy.start()
+    for copy in copies:
+        copy.wait()
     slabs, trials, width = in_ref.shape
     times = width // beams
     count = LANES // beams
@@ -223,17 +230,22 @@
         before = before + lax.ppermute((before + through).astype(BF16), "far", [(k, k + 2)]).astype(F32)
     later = lax.ppermute((before + through).astype(BF16), "far", [(k, k + 1) for k in range(3, blocks - 1, 2)])
     base = inner + before + handed + later.astype(F32)
-    cumulative = (local + base).astype(BF16)
-    slabs = lax.all_to_all(cumulative, "near", split_axis=0, concat_axis=0, tiled=True)
+    pieces = []
+    for d in range(near):
+        band = lax.rem(lax.axis_index("near") + d, near)
+        mine = (lax.dynamic_index_in_dim(local, band, 0, keepdims=False) + base).astype(BF16)
+        if d:
+            mine = lax.ppermute(mine, "near", [(n, (n + d) % near) for n in range(near)])
+        pieces.append(mine)
     spread = pl.pallas_call(
         functools.partial(spread_kernel, beams, 1.0 / math.sqrt(FREQS)),
         out_shape=jax.ShapeDtypeStruct((trials * times * near * beams // LANES, LANES), F32),
-        in_specs=[anywhere],
+        in_specs=[pl.BlockSpec(memory_space=pltpu.SMEM)] + [anywhere] * near,
         out_specs=vmem,
-        scratch_shapes=[pltpu.VMEM(slabs.shape, BF16), pltpu.SemaphoreType.DMA],
+        scratch_shapes=[pltpu.VMEM((near, *base.shape), BF16), pltpu.SemaphoreType.DMA((near,))],
         compiler_params=pltpu.CompilerParams(vmem_limit_bytes=24 * 2**20),
         name="spread",
-    )(slabs)
+    )(place, *pieces)
     spread = jnp.transpose(spread.reshape(trials, near * beams // LANES, times, LANES), (0, 2, 1, 3))
     return spread.reshape(1, trials, times, near * beams)
 

time: 172 us -> 175 us (1.017)
  blocking collectives: 140 us -> 127 us
  starting transfers between devices: 10.4 us -> 20.7 us
  waiting for transfers between devices: 11.8 us -> 16 us
    all_to_all x1 -> x0, blocking collectives: 12.1 us -> none  [search(): lax.all_to_all(cumulative, 'near', split_axis=0, concat_axis=0, tiled=True)]
    ppermute x0 -> x3, starting transfers between devices: none -> 10.3 us  [search(): lax.ppermute(mine, 'near', [(n, (n + d) % near) for n in range(near)])]
    ppermute x0 -> x3, waiting for transfers between devices: none -> 4.22 us  [search(): lax.ppermute(mine, 'near', [(n, (n + d) % near) for n in range(near)])]
  transfers between devices with their start and end apart: 8 -> 11, of which waited for: 3 -> 5; matrix products, arithmetic and copies ran while one was open for 0% -> 0% of each run, Pallas kernels for 0% -> 0%
where the time goes in v9:
time: 175 us
  blocking collectives  127 us (73%)
  starting transfers between devices  20.7 us (12%)
  waiting for transfers between devices  16 us (9%)
  Pallas kernels  10.2 us (6%)
    all_to_all x1, blocking collectives, search(): lax.all_to_all(sent, ('far', 'near', 'beam'), split_axis=0, concat_axis=0...  104 us
    all_gather x1, blocking collectives, search(): lags = lax.all_gather(lags, 'beam').reshape(near, trials, subs)  23.5 us
    ppermute x3, starting transfers between devices, search(): lax.ppermute(mine, 'near', [(n, (n + d) % near) for n in range(near)])  10.3 us
    ppermute x1, waiting for transfers between devices, search(): lax.ppermute(total.astype(BF16), 'far', [(k, k + 1) for k in range(0, blo...  8.78 us
    pallas_call x1, Pallas kernels, search(): pl.pallas_call(functools.partial(front_kernel, times, blocks, near, beams...  5.07 us
    ppermute x3, waiting for transfers between devices, search(): lax.ppermute(mine, 'near', [(n, (n + d) % near) for n in range(near)])  4.22 us
  transfers between devices with their start and end apart: 11, of which 5 were waited for; matrix products, arithmetic and copies ran while one was open for 0% of the time, Pallas kernels for 0%

profile of v9, /device:TPU:296, one launch (start us, length us, event | category | flops | bytes accessed | tf_op | source)
XLA Modules:
  0.0 175.0 jit_solution(16904281139295549191)
XLA Ops:
  0.0 5.1 %front.1 = bf16[128,8,256]{2,1,0:T(8,128)(2,1)} custom-call(bf16[256,2,1024]{2,1,0:T(2,128)(2,1)} %bitcast.31, s32[1,1024]{1,0:T(1,128)} %bitcast.32, bf16[512,512]{1,0:T(8,128)(2,1)} %constant.38.clone.table_ref), custom_call_target="tpu_custom_call" | custom-call | flops 2000000000 | bytes 4000000 | tf_op jit(solution)/shard_map/front/pallas_call | solution.py:184
  5.1 104.0 %all_to_all.5.own_any = bf16[128,8,256]{2,1,0:T(8,128)(2,1)S(1)} all-to-all(bf16[128,8,256]{2,1,0:T(8,128)(2,1)} %front.1), channel_id=1, replica_groups=mesh['grp'=2,'far'=8,'near'=4,'beam'=4,'dm'=2] {'far','near','beam'}, dimensions={0} | all-to-all | bytes 1048576 | tf_op jit(solution)/shard_map/all_to_all | solution.py:193
  109.1 1.9 %collective-permute-start = (bf16[128,8,256]{2,1,0:T(8,128)(2,1)S(1)}, bf16[128,8,256]{2,1,0:T(8,128)(2,1)S(1)}, u32[]{:S(2)}, u32[]{:S(2)}) collective-permute-start(bf16[128,8,256]{2,1,0:T(8,128)(2,1)S(1)} %all_to_all.5.own_any), channel_id=1, source_target_pairs={{0,1},{1,0},{2,3},{3,2},{4,5},{5,4},{6,7},{7,6},{8,9},{9,8},{10,11... | collective-permute-start | bytes 1572872 | tf_op jit(solution)/shard_map/ppermute | solution.py:203
  111.0 0.7 collective-permute-start.1
  111.7 0.1 pad_add_fusion.place_ref
  111.8 0.1 copy.7
  112.0 23.5 %all_gather.3 = bf16[4,1,128,256]{3,2,1,0:T(8,128)(2,1)S(1)} all-gather(bf16[1,1,128,256]{3,2,1,0:T(8,128)(2,1)S(1)} %all_gather_reshape.3), channel_id=1, replica_groups=mesh['grp'=2,'far'=8,'near'=4,'beam'=4,'dm'=2] {'beam'}, dimensions={0}, use_global_device_ids=true | all-gather | bytes 327680 | tf_op jit(solution)/shard_map/all_gather | solution.py:202
  135.4 3.1 %dedisperse.1 = (f32[4,128,256]{2,1,0:T(8,128)S(1)}, f32[128,256]{1,0:T(8,128)S(1)}) custom-call(s32[2]{0:T(128)S(1)} %pad_add_fusion.place_ref, bf16[128,8,256]{2,1,0:T(8,128)(2,1)S(1)} %all_to_all.5.own_any, bf16[128,8,256]{2,1,0:T(8,128)(2,1)S(1)} %collective-permute-done.other_any, bf16[4,128,256]{2,1,0:T(8,128)(2,1)S(1)} %bitcast.28), custom_call_target="tpu_custom_call" | custom-call | flops 2000000000 | bytes 4000000 | tf_op jit(solution)/shard_map/dedisperse/pallas_call | solution.py:205
  138.6 1.3 collective-permute-start.2
  139.9 8.8 %collective-permute-done.2 = bf16[128,256]{1,0:T(8,128)(2,1)S(1)} collective-permute-done((bf16[128,256]{1,0:T(8,128)(2,1)S(1)}, bf16[128,256]{1,0:T(8,128)(2,1)S(1)}, u32[]{:S(2)}, u32[]{:S(2)}) %collective-permute-start.2) | collective-permute-done | bytes 65568 | tf_op jit(solution)/shard_map/ppermute | solution.py:224
  148.7 3.1 %collective-permute-start.3 = (bf16[128,256]{1,0:T(8,128)(2,1)S(1)}, bf16[128,256]{1,0:T(8,128)(2,1)S(1)}, u32[]{:S(2)}, u32[]{:S(2)}) collective-permute-start(bf16[128,256]{1,0:T(8,128)(2,1)S(1)} %fusion.7), channel_id=1, source_target_pairs={{32,96},{33,97},{34,98},{35,99},{36,100},{37,101},{38,102},{39,103... | collective-permute-start | bytes 196616 | tf_op jit(solution)/shard_map/ppermute | solution.py:227
  151.9 1.9 %collective-permute-done.3 = bf16[128,256]{1,0:T(8,128)(2,1)S(1)} collective-permute-done((bf16[128,256]{1,0:T(8,128)(2,1)S(1)}, bf16[128,256]{1,0:T(8,128)(2,1)S(1)}, u32[]{:S(2)}, u32[]{:S(2)}) %collective-permute-start.3) | collective-permute-done | bytes 65568 | tf_op jit(solution)/shard_map/ppermute | solution.py:227
  153.8 0.7 collective-permute-start.4
  154.5 0.7 collective-permute-start.5
  155.2 1.3 collective-permute-start.6
  156.6 0.7 collective-permute-start.7
  157.3 1.1 collective-permute-done.6
  158.4 0.1 fusion.3
  158.5 2.0 %collective-permute-start.8 = (bf16[128,256]{1,0:T(8,128)(2,1)S(1)}, bf16[128,256]{1,0:T(8,128)(2,1)S(1)}, u32[]{:S(2)}, u32[]{:S(2)}) collective-permute-start(bf16[128,256]{1,0:T(8,128)(2,1)S(1)} %get-tuple-element.12), channel_id=1, source_target_pairs={{0,8},{8,16},{16,24},{24,0},{1,9},{9,17},{17,25},{25,1},{2,10},{10... | collective-permute-start | bytes 196616 | tf_op jit(solution)/shard_map/ppermute | solution.py:238
  160.5 6.4 %collective-permute-start.9 = (bf16[128,256]{1,0:T(8,128)(2,1)S(1)}, bf16[128,256]{1,0:T(8,128)(2,1)S(1)}, u32[]{:S(2)}, u32[]{:S(2)}) collective-permute-start(bf16[128,256]{1,0:T(8,128)(2,1)S(1)} %get-tuple-element.11), channel_id=1, source_target_pairs={{0,16},{8,24},{16,0},{24,8},{1,17},{9,25},{17,1},{25,9},{2,18},{10... | collective-permute-start | bytes 196616 | tf_op jit(solution)/shard_map/ppermute | solution.py:238
  166.9 2.0 %collective-permute-start.10 = (bf16[128,256]{1,0:T(8,128)(2,1)S(1)}, bf16[128,256]{1,0:T(8,128)(2,1)S(1)}, u32[]{:S(2)}, u32[]{:S(2)}) collective-permute-start(bf16[128,256]{1,0:T(8,128)(2,1)S(1)} %get-tuple-element.9), channel_id=1, source_target_pairs={{0,24},{8,0},{16,8},{24,16},{1,25},{9,1},{17,9},{25,17},{2,26},{10... | collective-permute-start | bytes 196616 | tf_op jit(solution)/shard_map/ppermute | solution.py:238
  168.9 0.4 collective-permute-done.9.refs_2_
  169.3 3.8 %collective-permute-done.10.refs_3_ = bf16[128,256]{1,0:T(8,128)(2,1)S(1)} collective-permute-done((bf16[128,256]{1,0:T(8,128)(2,1)S(1)}, bf16[128,256]{1,0:T(8,128)(2,1)S(1)}, u32[]{:S(2)}, u32[]{:S(2)}) %collective-permute-start.10) | collective-permute-done | bytes 65568 | tf_op jit(solution)/shard_map/ppermute | solution.py:238
  173.1 1.9 %spread.1 = f32[1024,128]{1,0:T(8,128)} custom-call(s32[2]{0:T(128)S(1)} %pad_add_fusion.place_ref, bf16[128,256]{1,0:T(8,128)(2,1)S(1)} %get-tuple-element.13.refs_0_, bf16[128,256]{1,0:T(8,128)(2,1)S(1)} %collective-permute-done.8.refs_1_, bf16[128,256]{1,0:T(8,128)(2,1)S(1)} %collective-permute-done.9.refs_2_, ...), custom_call_target="tpu_custom_call" | custom-call | tf_op jit(solution)/shard_map/spread/pallas_call | solution.py:240
  (16 shorter events, 0.2 us)
Async XLA Ops:
  5.1 105.9 %copy-start = (s32[1,256,128]{2,1,0:T(8,128)S(1)}, s32[1,256,128]{2,1,0:T(8,128)}, u32[]{:S(2)}) copy-start(s32[1,256,128]{2,1,0:T(8,128)} %param.6) | copy-start | bytes 393220
  109.1 26.4 %collective-permute-start = (bf16[128,8,256]{2,1,0:T(8,128)(2,1)S(1)}, bf16[128,8,256]{2,1,0:T(8,128)(2,1)S(1)}, u32[]{:S(2)}, u32[]{:S(2)}) collective-permute-start(bf16[128,8,256]{2,1,0:T(8,128)(2,1)S(1)} %all_to_all.5.own_any), channel_id=1, source_target_pairs={{0,1},{1,0},{2,3},{3,2},{4,5},{5,4},{6,7},{7,6},{8,9},{9,8},{10,11... | collective-permute-start | bytes 1572872 | tf_op jit(solution)/shard_map/ppermute | solution.py:203
  111.0 0.8 collective-permute-start.1
  138.6 10.1 %collective-permute-start.2 = (bf16[128,256]{1,0:T(8,128)(2,1)S(1)}, bf16[128,256]{1,0:T(8,128)(2,1)S(1)}, u32[]{:S(2)}, u32[]{:S(2)}) collective-permute-start(bf16[128,256]{1,0:T(8,128)(2,1)S(1)} %convert_element_type.49), channel_id=1, source_target_pairs={{0,32},{64,96},{128,160},{192,224},{1,33},{65,97},{129,161},{193,2... | collective-permute-start | bytes 196616 | tf_op jit(solution)/shard_map/ppermute | solution.py:224
  148.7 5.0 %collective-permute-start.3 = (bf16[128,256]{1,0:T(8,128)(2,1)S(1)}, bf16[128,256]{1,0:T(8,128)(2,1)S(1)}, u32[]{:S(2)}, u32[]{:S(2)}) collective-permute-start(bf16[128,256]{1,0:T(8,128)(2,1)S(1)} %fusion.7), channel_id=1, source_target_pairs={{32,96},{33,97},{34,98},{35,99},{36,100},{37,101},{38,102},{39,103... | collective-permute-start | bytes 196616 | tf_op jit(solution)/shard_map/ppermute | solution.py:227
  153.8 0.7 collective-permute-start.4
  154.5 2.0 %collective-permute-start.5 = (bf16[128,256]{1,0:T(8,128)(2,1)S(1)}, bf16[128,256]{1,0:T(8,128)(2,1)S(1)}, u32[]{:S(2)}, u32[]{:S(2)}) collective-permute-start(bf16[128,256]{1,0:T(8,128)(2,1)S(1)} %add_convert_fusion.1), channel_id=1, source_target_pairs={{160,224},{161,225},{162,226},{163,227},{164,228},{165,229},{166,2... | collective-permute-start | bytes 196616 | tf_op jit(solution)/shard_map/ppermute | solution.py:230
  155.2 3.2 %collective-permute-start.6 = (bf16[128,256]{1,0:T(8,128)(2,1)S(1)}, bf16[128,256]{1,0:T(8,128)(2,1)S(1)}, u32[]{:S(2)}, u32[]{:S(2)}) collective-permute-start(bf16[128,256]{1,0:T(8,128)(2,1)S(1)} %fusion.7), channel_id=1, source_target_pairs={{32,64},{33,65},{34,66},{35,67},{36,68},{37,69},{38,70},{39,71},{4... | collective-permute-start | bytes 196616 | tf_op jit(solution)/shard_map/ppermute | solution.py:228
  156.6 1.8 %collective-permute-start.7 = (bf16[128,256]{1,0:T(8,128)(2,1)S(1)}, bf16[128,256]{1,0:T(8,128)(2,1)S(1)}, u32[]{:S(2)}, u32[]{:S(2)}) collective-permute-start(bf16[128,256]{1,0:T(8,128)(2,1)S(1)} %add_convert_fusion), channel_id=1, source_target_pairs={{96,128},{160,192},{97,129},{161,193},{98,130},{162,194},{99,131},... | collective-permute-start | bytes 196616 | tf_op jit(solution)/shard_map/ppermute | solution.py:231
  158.5 10.4 %collective-permute-start.8 = (bf16[128,256]{1,0:T(8,128)(2,1)S(1)}, bf16[128,256]{1,0:T(8,128)(2,1)S(1)}, u32[]{:S(2)}, u32[]{:S(2)}) collective-permute-start(bf16[128,256]{1,0:T(8,128)(2,1)S(1)} %get-tuple-element.12), channel_id=1, source_target_pairs={{0,8},{8,16},{16,24},{24,0},{1,9},{9,17},{17,25},{25,1},{2,10},{10... | collective-permute-start | bytes 196616 | tf_op jit(solution)/shard_map/ppermute | solution.py:238
  160.5 8.8 %collective-permute-start.9 = (bf16[128,256]{1,0:T(8,128)(2,1)S(1)}, bf16[128,256]{1,0:T(8,128)(2,1)S(1)}, u32[]{:S(2)}, u32[]{:S(2)}) collective-permute-start(bf16[128,256]{1,0:T(8,128)(2,1)S(1)} %get-tuple-element.11), channel_id=1, source_target_pairs={{0,16},{8,24},{16,0},{24,8},{1,17},{9,25},{17,1},{25,9},{2,18},{10... | collective-permute-start | bytes 196616 | tf_op jit(solution)/shard_map/ppermute | solution.py:238
  166.9 6.2 %collective-permute-start.10 = (bf16[128,256]{1,0:T(8,128)(2,1)S(1)}, bf16[128,256]{1,0:T(8,128)(2,1)S(1)}, u32[]{:S(2)}, u32[]{:S(2)}) collective-permute-start(bf16[128,256]{1,0:T(8,128)(2,1)S(1)} %get-tuple-element.9), channel_id=1, source_target_pairs={{0,24},{8,0},{16,8},{24,16},{1,25},{9,1},{17,9},{25,17},{2,26},{10... | collective-permute-start | bytes 196616 | tf_op jit(solution)/shard_map/ppermute | solution.py:238

commit v10 on v8

--- a/solution.py
+++ b/solution.py
@@ -86,7 +86,29 @@
                             out_ref[peer, :, pl.ds(u * LANES, LANES)] = packed[row : row + tall].astype(BF16)
 
 
-def dedisperse_kernel(beams, place_ref, own_any, other_any, lag_any, out_ref, total_ref, own_ref, other_ref, lag_ref, level_ref, sems):
+def dedisperse_kernel(beams, turn, place_ref, own_any, other_any, lag_any, *refs):
+    earlier, (out_ref, total_ref, *scratch) = refs[:-7], refs[-7:]
+    active = lax.rem(place_ref[2], 2) == turn
+
+    @pl.when(active)
+    def work():
+        dedisperse(beams, place_ref, own_any, other_any, lag_any, out_ref, total_ref, *scratch)
+
+    @pl.when(jnp.logical_not(active))
+    def pass_on():
+        if not earlier:
+            out_ref[...] = jnp.zeros_like(out_ref)
+            total_ref[...] = jnp.zeros_like(total_ref)
+        else:
+            sems = scratch[-1]
+            kept = [pltpu.make_async_copy(a, b, sems.at[i]) for i, (a, b) in enumerate(zip(earlier, (out_ref, total_ref)))]
+            for copy in kept:
+                copy.start()
+            for copy in kept:
+                copy.wait()
+
+
+def dedisperse(beams, place_ref, own_any, other_any, lag_any, out_ref, total_ref, own_ref, other_ref, lag_ref, level_ref, sems):
     pairs = ((own_any, own_ref), (other_any, other_ref), (lag_any, lag_ref))
     copies = [pltpu.make_async_copy(a, b, sems.at[i]) for i, (a, b) in enumerate(pairs)]
     for copy in copies:
@@ -194,27 +216,32 @@
     lags = jnp.transpose(lags, (0, 3, 2, 1)).reshape(share, trials, subs)
     lags = lax.all_gather(lags, "beam").reshape(near, trials, subs)
     other = lax.ppermute(own, "dm", [(0, 1), (1, 0)])
-    place = jnp.stack([lax.axis_index("dm"), lax.axis_index("near")]).astype(jnp.int32)
-    local, total = pl.pallas_call(
-        functools.partial(dedisperse_kernel, beams),
-        out_shape=(
-            jax.ShapeDtypeStruct((bands // blocks, trials, times * beams), F32),
-            jax.ShapeDtypeStruct((trials, times * beams), F32),
-        ),
-        in_specs=[pl.BlockSpec(memory_space=pltpu.SMEM)] + [anywhere] * 3,
-        out_specs=(vmem, vmem),
-        scratch_shapes=[
-            pltpu.VMEM(own.shape, BF16),
-            pltpu.VMEM(own.shape, BF16),
-            pltpu.VMEM(lags.shape, BF16),
-            pltpu.VMEM((2 * times * beams // LANES, peers * tall, LANES), F32),
-            pltpu.SemaphoreType.DMA((3,)),
-        ],
-        compiler_params=pltpu.CompilerParams(vmem_limit_bytes=24 * 2**20),
-        cost_estimate=pl.CostEstimate(flops=2 * 10**9, bytes_accessed=4 * 10**6, transcendentals=0),
-        name="dedisperse",
-    )(place, own, other, lags)
+    place = jnp.stack([lax.axis_index(name) for name in ("dm", "near", "far")]).astype(jnp.int32)
+
+    def dedispersed(turn, *earlier):
+        return pl.pallas_call(
+            functools.partial(dedisperse_kernel, beams, turn),
+            out_shape=(
+                jax.ShapeDtypeStruct((bands // blocks, trials, times * beams), F32),
+                jax.ShapeDtypeStruct((trials, times * beams), F32),
+            ),
+            in_specs=[pl.BlockSpec(memory_space=pltpu.SMEM)] + [anywhere] * (3 + len(earlier)),
+            out_specs=(vmem, vmem),
+            scratch_shapes=[
+                pltpu.VMEM(own.shape, BF16),
+                pltpu.VMEM(own.shape, BF16),
+                pltpu.VMEM(lags.shape, BF16),
+                pltpu.VMEM((2 * times * beams // LANES, peers * tall, LANES), F32),
+                pltpu.SemaphoreType.DMA((3,)),
+            ],
+            compiler_params=pltpu.CompilerParams(vmem_limit_bytes=24 * 2**20),
+            cost_estimate=pl.CostEstimate(flops=10**9, bytes_accessed=4 * 10**6, transcendentals=0),
+            name="dedisperse",
+        )(place, own, other, lags, *earlier)
+
+    local, total = dedispersed(0)
     inner = lax.ppermute(total.astype(BF16), "far", [(k, k + 1) for k in range(0, blocks, 2)]).astype(F32)
+    local, total = dedispersed(1, local, total)
     through = total + inner
     known = through.astype(BF16)
     before = lax.ppermute(known, "far", [(1, 3)]).astype(F32)

time: 172 us -> 172 us (level)
  the two profiles are of different devices: /device:TPU:296 before, /device:TPU:288 now
where the time goes in v10:
time: 172 us
  blocking collectives  141 us (82%)
  starting transfers between devices  11.2 us (7%)
  Pallas kernels  9.87 us (6%)
  waiting for transfers between devices  8.69 us (5%)
    all_to_all x1, blocking collectives, search(): lax.all_to_all(sent, ('far', 'near', 'beam'), split_axis=0, concat_axis=0...  104 us
    all_gather x1, blocking collectives, search(): lags = lax.all_gather(lags, 'beam').reshape(near, trials, subs)  23.5 us
    all_to_all x1, blocking collectives, search(): lax.all_to_all(cumulative, 'near', split_axis=0, concat_axis=0, tiled=True)  13.7 us
    ppermute x1, waiting for transfers between devices, search(): lax.ppermute(total.astype(BF16), 'far', [(k, k + 1) for k in range(0, blo...  5.64 us
    pallas_call x1, Pallas kernels, search(): pl.pallas_call(functools.partial(front_kernel, times, blocks, near, beams...  5.07 us
    ppermute x1, starting transfers between devices, search(): before = lax.ppermute(known, 'far', [(1, 3)]).astype(F32)  3.96 us
    pallas_call x2, Pallas kernels, dedispersed(): pl.pallas_call(functools.partial(dedisperse_kernel, beams, turn), out_sha...  3.76 us
  transfers between devices with their start and end apart: 8, of which 3 were waited for; matrix products, arithmetic and copies ran while one was open for 0% of the time, Pallas kernels for 2%

profile of v10, /device:TPU:288, one launch (start us, length us, event | category | flops | bytes accessed | tf_op | source)
XLA Modules:
  0.0 171.5 jit_solution(2828633405763946115)
XLA Ops:
  0.0 5.1 %front.1 = bf16[128,8,256]{2,1,0:T(8,128)(2,1)} custom-call(bf16[256,2,1024]{2,1,0:T(2,128)(2,1)} %bitcast.17, s32[1,1024]{1,0:T(1,128)} %bitcast.18, bf16[512,512]{1,0:T(8,128)(2,1)} %constant.16.clone.table_ref), custom_call_target="tpu_custom_call" | custom-call | flops 2000000000 | bytes 4000000 | tf_op jit(solution)/shard_map/front/pallas_call | solution.py:199
  5.1 104.0 %all_to_all.10.own_any = bf16[128,8,256]{2,1,0:T(8,128)(2,1)S(1)} all-to-all(bf16[128,8,256]{2,1,0:T(8,128)(2,1)} %front.1), channel_id=1, replica_groups=mesh['grp'=2,'far'=8,'near'=4,'beam'=4,'dm'=2] {'far','near','beam'}, dimensions={0} | all-to-all | bytes 1048576 | tf_op jit(solution)/shard_map/all_to_all | solution.py:208
  109.1 1.9 %collective-permute-start = (bf16[128,8,256]{2,1,0:T(8,128)(2,1)S(1)}, bf16[128,8,256]{2,1,0:T(8,128)(2,1)S(1)}, u32[]{:S(2)}, u32[]{:S(2)}) collective-permute-start(bf16[128,8,256]{2,1,0:T(8,128)(2,1)S(1)} %all_to_all.10.own_any), channel_id=1, source_target_pairs={{0,1},{1,0},{2,3},{3,2},{4,5},{5,4},{6,7},{7,6},{8,9},{9,8},{10,11... | collective-permute-start | bytes 1572872 | tf_op jit(solution)/shard_map/ppermute | solution.py:218
  111.0 0.7 collective-permute-start.1
  111.7 0.1 pad_add_fusion.place_ref
  111.8 0.0 collective-permute-done.1
  111.8 0.1 copy.7
  112.0 23.5 %all_gather.3 = bf16[4,1,128,256]{3,2,1,0:T(8,128)(2,1)S(1)} all-gather(bf16[1,1,128,256]{3,2,1,0:T(8,128)(2,1)S(1)} %all_gather_reshape.3), channel_id=1, replica_groups=mesh['grp'=2,'far'=8,'near'=4,'beam'=4,'dm'=2] {'beam'}, dimensions={0}, use_global_device_ids=true | all-gather | bytes 327680 | tf_op jit(solution)/shard_map/all_gather | solution.py:217
  135.4 0.0 collective-permute-done.other_any
  135.4 0.6 dedisperse.2
  136.1 1.3 collective-permute-start.2
  137.4 3.1 %dedisperse.3 = (f32[4,128,256]{2,1,0:T(8,128)S(1)}, f32[128,256]{1,0:T(8,128)S(1)}) custom-call(s32[3]{0:T(128)S(1)} %pad_add_fusion.place_ref, bf16[128,8,256]{2,1,0:T(8,128)(2,1)S(1)} %all_to_all.10.own_any, bf16[128,8,256]{2,1,0:T(8,128)(2,1)S(1)} %collective-permute-done.other_any, bf16[4,128,256]{2,1,0:T(8,128)(2,1)S(1)} %bitcast.14, ...), custom_call_target="tpu_custom_call" | custom-call | flops 1000000000 | bytes 4000000 | tf_op jit(solution)/shard_map/dedisperse/pallas_call | solution.py:222
  140.5 5.6 %collective-permute-done.2 = bf16[128,256]{1,0:T(8,128)(2,1)S(1)} collective-permute-done((bf16[128,256]{1,0:T(8,128)(2,1)S(1)}, bf16[128,256]{1,0:T(8,128)(2,1)S(1)}, u32[]{:S(2)}, u32[]{:S(2)}) %collective-permute-start.2) | collective-permute-done | bytes 65568 | tf_op jit(solution)/shard_map/ppermute | solution.py:243
  146.2 4.0 %collective-permute-start.3 = (bf16[128,256]{1,0:T(8,128)(2,1)S(1)}, bf16[128,256]{1,0:T(8,128)(2,1)S(1)}, u32[]{:S(2)}, u32[]{:S(2)}) collective-permute-start(bf16[128,256]{1,0:T(8,128)(2,1)S(1)} %fusion.3), channel_id=1, source_target_pairs={{32,96},{33,97},{34,98},{35,99},{36,100},{37,101},{38,102},{39,103... | collective-permute-start | bytes 196616 | tf_op jit(solution)/shard_map/ppermute | solution.py:247
  150.2 1.9 %collective-permute-done.3 = bf16[128,256]{1,0:T(8,128)(2,1)S(1)} collective-permute-done((bf16[128,256]{1,0:T(8,128)(2,1)S(1)}, bf16[128,256]{1,0:T(8,128)(2,1)S(1)}, u32[]{:S(2)}, u32[]{:S(2)}) %collective-permute-start.3) | collective-permute-done | bytes 65568 | tf_op jit(solution)/shard_map/ppermute | solution.py:247
  152.1 0.7 collective-permute-start.4
  152.8 0.7 collective-permute-start.5
  153.5 1.3 collective-permute-start.6
  154.9 0.7 collective-permute-start.7
  155.5 1.2 collective-permute-done.6
  156.7 0.1 fusion.1
  156.7 0.1 add_convert_fusion
  156.8 13.7 %all_to_all.11.in_any = bf16[4,128,256]{2,1,0:T(8,128)(2,1)S(1)} all-to-all(bf16[4,128,256]{2,1,0:T(8,128)(2,1)S(1)} %add_convert_fusion), channel_id=1, replica_groups=mesh['grp'=2,'far'=8,'near'=4,'beam'=4,'dm'=2] {'near'}, dimensions={0} | all-to-all | bytes 524288 | tf_op jit(solution)/shard_map/all_to_all | solution.py:254
  170.5 1.0 spread.1
  (12 shorter events, 0.2 us)
Async XLA Ops:
  5.1 105.9 %copy-start = (s32[1,256,128]{2,1,0:T(8,128)S(1)}, s32[1,256,128]{2,1,0:T(8,128)}, u32[]{:S(2)}) copy-start(s32[1,256,128]{2,1,0:T(8,128)} %param.6) | copy-start | bytes 393220
  109.1 26.4 %collective-permute-start = (bf16[128,8,256]{2,1,0:T(8,128)(2,1)S(1)}, bf16[128,8,256]{2,1,0:T(8,128)(2,1)S(1)}, u32[]{:S(2)}, u32[]{:S(2)}) collective-permute-start(bf16[128,8,256]{2,1,0:T(8,128)(2,1)S(1)} %all_to_all.10.own_any), channel_id=1, source_target_pairs={{0,1},{1,0},{2,3},{3,2},{4,5},{5,4},{6,7},{7,6},{8,9},{9,8},{10,11... | collective-permute-start | bytes 1572872 | tf_op jit(solution)/shard_map/ppermute | solution.py:218
  111.0 0.8 collective-permute-start.1
  136.1 10.1 %collective-permute-start.2 = (bf16[128,256]{1,0:T(8,128)(2,1)S(1)}, bf16[128,256]{1,0:T(8,128)(2,1)S(1)}, u32[]{:S(2)}, u32[]{:S(2)}) collective-permute-start(bf16[128,256]{1,0:T(8,128)(2,1)S(1)} %convert_element_type.40), channel_id=1, source_target_pairs={{0,32},{64,96},{128,160},{192,224},{1,33},{65,97},{129,161},{193,2... | collective-permute-start | bytes 196616 | tf_op jit(solution)/shard_map/ppermute | solution.py:243
  146.2 5.9 %collective-permute-start.3 = (bf16[128,256]{1,0:T(8,128)(2,1)S(1)}, bf16[128,256]{1,0:T(8,128)(2,1)S(1)}, u32[]{:S(2)}, u32[]{:S(2)}) collective-permute-start(bf16[128,256]{1,0:T(8,128)(2,1)S(1)} %fusion.3), channel_id=1, source_target_pairs={{32,96},{33,97},{34,98},{35,99},{36,100},{37,101},{38,102},{39,103... | collective-permute-start | bytes 196616 | tf_op jit(solution)/shard_map/ppermute | solution.py:247
  152.1 0.7 collective-permute-start.4
  152.8 2.0 %collective-permute-start.5 = (bf16[128,256]{1,0:T(8,128)(2,1)S(1)}, bf16[128,256]{1,0:T(8,128)(2,1)S(1)}, u32[]{:S(2)}, u32[]{:S(2)}) collective-permute-start(bf16[128,256]{1,0:T(8,128)(2,1)S(1)} %add_convert_fusion.2), channel_id=1, source_target_pairs={{160,224},{161,225},{162,226},{163,227},{164,228},{165,229},{166,2... | collective-permute-start | bytes 196616 | tf_op jit(solution)/shard_map/ppermute | solution.py:250
  153.5 3.2 %collective-permute-start.6 = (bf16[128,256]{1,0:T(8,128)(2,1)S(1)}, bf16[128,256]{1,0:T(8,128)(2,1)S(1)}, u32[]{:S(2)}, u32[]{:S(2)}) collective-permute-start(bf16[128,256]{1,0:T(8,128)(2,1)S(1)} %fusion.3), channel_id=1, source_target_pairs={{32,64},{33,65},{34,66},{35,67},{36,68},{37,69},{38,70},{39,71},{4... | collective-permute-start | bytes 196616 | tf_op jit(solution)/shard_map/ppermute | solution.py:248
  154.9 1.8 %collective-permute-start.7 = (bf16[128,256]{1,0:T(8,128)(2,1)S(1)}, bf16[128,256]{1,0:T(8,128)(2,1)S(1)}, u32[]{:S(2)}, u32[]{:S(2)}) collective-permute-start(bf16[128,256]{1,0:T(8,128)(2,1)S(1)} %add_convert_fusion.1), channel_id=1, source_target_pairs={{96,128},{160,192},{97,129},{161,193},{98,130},{162,194},{99,131},... | collective-permute-start | bytes 196616 | tf_op jit(solution)/shard_map/ppermute | solution.py:251

commit v11 on v8

--- a/solution.py
+++ b/solution.py
@@ -47,29 +47,29 @@
 
 def front_kernel(times, blocks, near, beams, volt_ref, feed_ref, table_ref, out_ref, along_ref):
     rows, feeds = 2 * volt_ref.shape[0], volt_ref.shape[2]
-    half = rows // 2
-    chans = half // times
+    chans = rows // (2 * times)
     tall = chans // blocks
-    i = iota((rows, rows), 0)
-    source = i % chans * (2 * times) + i // chans % times * 2 + i // half
-    order = jnp.where(iota((rows, rows), 1) == source, 1.0, 0.0).astype(BF16)
     pick = jnp.where(iota((feeds, feeds), 0) == feed_ref[...], 1.0, 0.0).astype(BF16)
-    planes = jnp.dot(order, volt_ref[...].reshape(rows, feeds), preferred_element_type=F32).astype(BF16)
-    grid = jnp.dot(planes, pick, preferred_element_type=F32).astype(BF16)
+    volts = volt_ref[...].reshape(rows, feeds)
+    grid = jnp.dot(volts, pick, preferred_element_type=F32).astype(BF16)
+    table = table_ref[pl.ds(GY, GY), :]
+    halves = GY // LANES
     for gx in range(GX):
-        cells = slice(gx * GY, (gx + 1) * GY)
-        paired = jnp.concatenate([grid[:half, cells], grid[half:, cells]], axis=1)
-        along = jnp.dot(paired, table_ref[...], preferred_element_type=F32)
-        along_ref[gx] = along.astype(BF16)
+        along = jnp.dot(grid[:, gx * GY : (gx + 1) * GY], table, preferred_element_type=F32)
+        for u in range(2 * halves):
+            along_ref[gx, u] = along[:, u * LANES : (u + 1) * LANES]
     per_tile = LANES // beams
     group = max(tall, 16)
     for first in range(0, chans, group):
         for tile in range(GY // LANES):
             power = [[] for _ in range(GX)]
             for t in range(times):
-                r = pl.ds(t * chans + first, group)
-                re = [along_ref[gx, r, pl.ds(tile * LANES, LANES)].astype(F32) for gx in range(GX)]
-                im = [along_ref[gx, r, pl.ds(GY + tile * LANES, LANES)].astype(F32) for gx in range(GX)]
+                r0, r1 = (pl.ds((first * times + t) * 2 + p, group, stride=2 * times) for p in range(2))
+                re, im = [], []
+                for gx in range(GX):
+                    sine, cosine = along_ref.at[gx, tile], along_ref.at[gx, halves + tile]
+                    re.append((cosine[r0, :] + sine[r1, :]).astype(BF16).astype(F32))
+                    im.append((cosine[r1, :] - sine[r0, :]).astype(BF16).astype(F32))
                 er, ei, orr, oi = re[0] + re[2], im[0] + im[2], re[1] + re[3], im[1] + im[3]
                 dr, di, ur, ui = re[0] - re[2], im[0] - im[2], re[1] - re[3], im[1] - im[3]
                 formed = [(er + orr, ei + oi), (dr + ui, di - ur), (er - orr, ei - oi), (dr - ui, di + ur)]
@@ -179,7 +179,7 @@
         out_shape=jax.ShapeDtypeStruct((peers, tall, times * beams), BF16),
         in_specs=[vmem] * 3,
         out_specs=vmem,
-        scratch_shapes=[pltpu.VMEM((GX, rows // 2, 2 * GY), BF16)],
+        scratch_shapes=[pltpu.VMEM((GX, 2 * GY // LANES, rows, LANES), F32)],
         cost_estimate=pl.CostEstimate(flops=2 * 10**9, bytes_accessed=4 * 10**6, transcendentals=0),
         name="front",
     )(voltages.reshape(rows // 2, 2, feeds), grid_feed.reshape(1, feeds), jnp.asarray(steering_table(GY)))

time: 172 us -> 172 us (level)
  the two profiles are of different devices: /device:TPU:296 before, /device:TPU:288 now
where the time goes in v11:
time: 172 us; the launch traced here: 171 us
  blocking collectives  140 us (81%)
  waiting for transfers between devices  11.8 us (7%)
  starting transfers between devices  10.4 us (6%)
  Pallas kernels  9.05 us (5%)
    all_to_all x1, blocking collectives, search(): lax.all_to_all(sent, ('far', 'near', 'beam'), split_axis=0, concat_axis=0...  104 us
    all_gather x1, blocking collectives, search(): lags = lax.all_gather(lags, 'beam').reshape(near, trials, subs)  23.5 us
    all_to_all x1, blocking collectives, search(): lax.all_to_all(cumulative, 'near', split_axis=0, concat_axis=0, tiled=True)  12.1 us
    ppermute x1, waiting for transfers between devices, search(): lax.ppermute(total.astype(BF16), 'far', [(k, k + 1) for k in range(0, blo...  8.78 us
    pallas_call x1, Pallas kernels, search(): pl.pallas_call(functools.partial(front_kernel, times, blocks, near, beams...  4.88 us
  transfers between devices with their start and end apart: 8, of which 3 were waited for; matrix products, arithmetic and copies ran while one was open for 0% of the time, Pallas kernels for 0%

profile of v11, /device:TPU:288, one launch (start us, length us, event | category | flops | bytes accessed | tf_op | source)
XLA Modules:
  0.0 171.5 jit_solution(13618363691570547421)
XLA Ops:
  0.0 4.9 %front.1 = bf16[128,8,256]{2,1,0:T(8,128)(2,1)} custom-call(bf16[256,2,1024]{2,1,0:T(2,128)(2,1)} %bitcast.15, s32[1,1024]{1,0:T(1,128)} %bitcast.16, bf16[512,512]{1,0:T(8,128)(2,1)} %constant.11.clone.table_ref), custom_call_target="tpu_custom_call" | custom-call | flops 2000000000 | bytes 4000000 | tf_op jit(solution)/shard_map/front/pallas_call | solution.py:177
  4.9 104.0 %all_to_all.10.own_any = bf16[128,8,256]{2,1,0:T(8,128)(2,1)S(1)} all-to-all(bf16[128,8,256]{2,1,0:T(8,128)(2,1)} %front.1), channel_id=1, replica_groups=mesh['grp'=2,'far'=8,'near'=4,'beam'=4,'dm'=2] {'far','near','beam'}, dimensions={0} | all-to-all | bytes 1048576 | tf_op jit(solution)/shard_map/all_to_all | solution.py:186
  108.9 1.9 %collective-permute-start = (bf16[128,8,256]{2,1,0:T(8,128)(2,1)S(1)}, bf16[128,8,256]{2,1,0:T(8,128)(2,1)S(1)}, u32[]{:S(2)}, u32[]{:S(2)}) collective-permute-start(bf16[128,8,256]{2,1,0:T(8,128)(2,1)S(1)} %all_to_all.10.own_any), channel_id=1, source_target_pairs={{0,1},{1,0},{2,3},{3,2},{4,5},{5,4},{6,7},{7,6},{8,9},{9,8},{10,11... | collective-permute-start | bytes 1572872 | tf_op jit(solution)/shard_map/ppermute | solution.py:196
  110.8 0.7 collective-permute-start.1
  111.5 0.1 pad_add_fusion.place_ref
  111.6 0.0 collective-permute-done.1
  111.6 0.1 copy.7
  111.8 23.5 %all_gather.3 = bf16[4,1,128,256]{3,2,1,0:T(8,128)(2,1)S(1)} all-gather(bf16[1,1,128,256]{3,2,1,0:T(8,128)(2,1)S(1)} %all_gather_reshape.3), channel_id=1, replica_groups=mesh['grp'=2,'far'=8,'near'=4,'beam'=4,'dm'=2] {'beam'}, dimensions={0}, use_global_device_ids=true | all-gather | bytes 327680 | tf_op jit(solution)/shard_map/all_gather | solution.py:195
  135.2 0.0 collective-permute-done.other_any
  135.2 3.1 %dedisperse.1 = (f32[4,128,256]{2,1,0:T(8,128)S(1)}, f32[128,256]{1,0:T(8,128)S(1)}) custom-call(s32[2]{0:T(128)S(1)} %pad_add_fusion.place_ref, bf16[128,8,256]{2,1,0:T(8,128)(2,1)S(1)} %all_to_all.10.own_any, bf16[128,8,256]{2,1,0:T(8,128)(2,1)S(1)} %collective-permute-done.other_any, bf16[4,128,256]{2,1,0:T(8,128)(2,1)S(1)} %bitcast.12), custom_call_target="tpu_custom_call" | custom-call | flops 2000000000 | bytes 4000000 | tf_op jit(solution)/shard_map/dedisperse/pallas_call | solution.py:198
  138.4 1.3 collective-permute-start.2
  139.7 8.8 %collective-permute-done.2 = bf16[128,256]{1,0:T(8,128)(2,1)S(1)} collective-permute-done((bf16[128,256]{1,0:T(8,128)(2,1)S(1)}, bf16[128,256]{1,0:T(8,128)(2,1)S(1)}, u32[]{:S(2)}, u32[]{:S(2)}) %collective-permute-start.2) | collective-permute-done | bytes 65568 | tf_op jit(solution)/shard_map/ppermute | solution.py:217
  148.5 3.1 %collective-permute-start.3 = (bf16[128,256]{1,0:T(8,128)(2,1)S(1)}, bf16[128,256]{1,0:T(8,128)(2,1)S(1)}, u32[]{:S(2)}, u32[]{:S(2)}) collective-permute-start(bf16[128,256]{1,0:T(8,128)(2,1)S(1)} %fusion.3), channel_id=1, source_target_pairs={{32,96},{33,97},{34,98},{35,99},{36,100},{37,101},{38,102},{39,103... | collective-permute-start | bytes 196616 | tf_op jit(solution)/shard_map/ppermute | solution.py:220
  151.7 1.9 %collective-permute-done.3 = bf16[128,256]{1,0:T(8,128)(2,1)S(1)} collective-permute-done((bf16[128,256]{1,0:T(8,128)(2,1)S(1)}, bf16[128,256]{1,0:T(8,128)(2,1)S(1)}, u32[]{:S(2)}, u32[]{:S(2)}) %collective-permute-start.3) | collective-permute-done | bytes 65568 | tf_op jit(solution)/shard_map/ppermute | solution.py:220
  153.6 0.7 collective-permute-start.4
  154.3 0.0 collective-permute-done.4
  154.3 0.7 collective-permute-start.5
  155.0 1.3 collective-permute-start.6
  156.4 0.7 collective-permute-start.7
  157.0 1.2 collective-permute-done.6
  158.2 0.1 fusion.1
  158.2 0.1 add_convert_fusion
  158.3 12.1 %all_to_all.11.in_any = bf16[4,128,256]{2,1,0:T(8,128)(2,1)S(1)} all-to-all(bf16[4,128,256]{2,1,0:T(8,128)(2,1)S(1)} %add_convert_fusion), channel_id=1, replica_groups=mesh['grp'=2,'far'=8,'near'=4,'beam'=4,'dm'=2] {'near'}, dimensions={0} | all-to-all | bytes 524288 | tf_op jit(solution)/shard_map/all_to_all | solution.py:227
  170.4 1.0 spread.1
  (11 shorter events, 0.2 us)
Async XLA Ops:
  4.9 105.9 %copy-start = (s32[1,256,128]{2,1,0:T(8,128)S(1)}, s32[1,256,128]{2,1,0:T(8,128)}, u32[]{:S(2)}) copy-start(s32[1,256,128]{2,1,0:T(8,128)} %param.6) | copy-start | bytes 393220
  108.9 26.4 %collective-permute-start = (bf16[128,8,256]{2,1,0:T(8,128)(2,1)S(1)}, bf16[128,8,256]{2,1,0:T(8,128)(2,1)S(1)}, u32[]{:S(2)}, u32[]{:S(2)}) collective-permute-start(bf16[128,8,256]{2,1,0:T(8,128)(2,1)S(1)} %all_to_all.10.own_any), channel_id=1, source_target_pairs={{0,1},{1,0},{2,3},{3,2},{4,5},{5,4},{6,7},{7,6},{8,9},{9,8},{10,11... | collective-permute-start | bytes 1572872 | tf_op jit(solution)/shard_map/ppermute | solution.py:196
  110.8 0.8 collective-permute-start.1
  138.4 10.1 %collective-permute-start.2 = (bf16[128,256]{1,0:T(8,128)(2,1)S(1)}, bf16[128,256]{1,0:T(8,128)(2,1)S(1)}, u32[]{:S(2)}, u32[]{:S(2)}) collective-permute-start(bf16[128,256]{1,0:T(8,128)(2,1)S(1)} %convert_element_type.40), channel_id=1, source_target_pairs={{0,32},{64,96},{128,160},{192,224},{1,33},{65,97},{129,161},{193,2... | collective-permute-start | bytes 196616 | tf_op jit(solution)/shard_map/ppermute | solution.py:217
  148.5 5.0 %collective-permute-start.3 = (bf16[128,256]{1,0:T(8,128)(2,1)S(1)}, bf16[128,256]{1,0:T(8,128)(2,1)S(1)}, u32[]{:S(2)}, u32[]{:S(2)}) collective-permute-start(bf16[128,256]{1,0:T(8,128)(2,1)S(1)} %fusion.3), channel_id=1, source_target_pairs={{32,96},{33,97},{34,98},{35,99},{36,100},{37,101},{38,102},{39,103... | collective-permute-start | bytes 196616 | tf_op jit(solution)/shard_map/ppermute | solution.py:220
  153.6 0.7 collective-permute-start.4
  154.3 2.0 %collective-permute-start.5 = (bf16[128,256]{1,0:T(8,128)(2,1)S(1)}, bf16[128,256]{1,0:T(8,128)(2,1)S(1)}, u32[]{:S(2)}, u32[]{:S(2)}) collective-permute-start(bf16[128,256]{1,0:T(8,128)(2,1)S(1)} %add_convert_fusion.2), channel_id=1, source_target_pairs={{160,224},{161,225},{162,226},{163,227},{164,228},{165,229},{166,2... | collective-permute-start | bytes 196616 | tf_op jit(solution)/shard_map/ppermute | solution.py:223
  155.0 3.2 %collective-permute-start.6 = (bf16[128,256]{1,0:T(8,128)(2,1)S(1)}, bf16[128,256]{1,0:T(8,128)(2,1)S(1)}, u32[]{:S(2)}, u32[]{:S(2)}) collective-permute-start(bf16[128,256]{1,0:T(8,128)(2,1)S(1)} %fusion.3), channel_id=1, source_target_pairs={{32,64},{33,65},{34,66},{35,67},{36,68},{37,69},{38,70},{39,71},{4... | collective-permute-start | bytes 196616 | tf_op jit(solution)/shard_map/ppermute | solution.py:221
  156.4 1.8 %collective-permute-start.7 = (bf16[128,256]{1,0:T(8,128)(2,1)S(1)}, bf16[128,256]{1,0:T(8,128)(2,1)S(1)}, u32[]{:S(2)}, u32[]{:S(2)}) collective-permute-start(bf16[128,256]{1,0:T(8,128)(2,1)S(1)} %add_convert_fusion.1), channel_id=1, source_target_pairs={{96,128},{160,192},{97,129},{161,193},{98,130},{162,194},{99,131},... | collective-permute-start | bytes 196616 | tf_op jit(solution)/shard_map/ppermute | solution.py:224

commit v12 on v11

--- a/solution.py
+++ b/solution.py
@@ -86,13 +86,7 @@
                             out_ref[peer, :, pl.ds(u * LANES, LANES)] = packed[row : row + tall].astype(BF16)
 
 
-def dedisperse_kernel(beams, place_ref, own_any, other_any, lag_any, out_ref, total_ref, own_ref, other_ref, lag_ref, level_ref, sems):
-    pairs = ((own_any, own_ref), (other_any, other_ref), (lag_any, lag_ref))
-    copies = [pltpu.make_async_copy(a, b, sems.at[i]) for i, (a, b) in enumerate(pairs)]
-    for copy in copies:
-        copy.start()
-    for copy in copies:
-        copy.wait()
+def dedisperse_kernel(beams, place_ref, own_ref, other_ref, lag_ref, out_ref, total_ref, level_ref):
     sources, tall, width = own_ref.shape
     bands = out_ref.shape[0]
     subs = tall // bands
@@ -145,10 +139,7 @@
         total_ref[:, pl.ds(u * LANES, LANES)] = running[u]
 
 
-def spread_kernel(beams, scale, in_any, out_ref, in_ref, sem):
-    copy = pltpu.make_async_copy(in_any, in_ref, sem)
-    copy.start()
-    copy.wait()
+def spread_kernel(beams, scale, in_ref, out_ref):
     slabs, trials, width = in_ref.shape
     times = width // beams
     count = LANES // beams
@@ -201,14 +192,10 @@
             jax.ShapeDtypeStruct((bands // blocks, trials, times * beams), F32),
             jax.ShapeDtypeStruct((trials, times * beams), F32),
         ),
-        in_specs=[pl.BlockSpec(memory_space=pltpu.SMEM)] + [anywhere] * 3,
+        in_specs=[pl.BlockSpec(memory_space=pltpu.SMEM)] + [vmem] * 3,
         out_specs=(vmem, vmem),
         scratch_shapes=[
-            pltpu.VMEM(own.shape, BF16),
-            pltpu.VMEM(own.shape, BF16),
-            pltpu.VMEM(lags.shape, BF16),
             pltpu.VMEM((2 * times * beams // LANES, peers * tall, LANES), F32),
-            pltpu.SemaphoreType.DMA((3,)),
         ],
         compiler_params=pltpu.CompilerParams(vmem_limit_bytes=24 * 2**20),
         cost_estimate=pl.CostEstimate(flops=2 * 10**9, bytes_accessed=4 * 10**6, transcendentals=0),
@@ -228,9 +215,8 @@
     spread = pl.pallas_call(
         functools.partial(spread_kernel, beams, 1.0 / math.sqrt(FREQS)),
         out_shape=jax.ShapeDtypeStruct((trials * times * near * beams // LANES, LANES), F32),
-        in_specs=[anywhere],
+        in_specs=[vmem],
         out_specs=vmem,
-        scratch_shapes=[pltpu.VMEM(slabs.shape, BF16), pltpu.SemaphoreType.DMA],
         compiler_params=pltpu.CompilerParams(vmem_limit_bytes=24 * 2**20),
         name="spread",
     )(slabs)

time: 172 us -> 172 us (level)
  no operation moved by 1% of the time
where the time goes in v12:
time: 172 us; the launch traced here: 171 us
  blocking collectives  140 us (81%)
  waiting for transfers between devices  11.8 us (7%)
  starting transfers between devices  10.4 us (6%)
  Pallas kernels  8.9 us (5%)
    all_to_all x1, blocking collectives, search(): lax.all_to_all(sent, ('far', 'near', 'beam'), split_axis=0, concat_axis=0...  104 us
    all_gather x1, blocking collectives, search(): lags = lax.all_gather(lags, 'beam').reshape(near, trials, subs)  23.5 us
    all_to_all x1, blocking collectives, search(): lax.all_to_all(cumulative, 'near', split_axis=0, concat_axis=0, tiled=True)  12.1 us
    ppermute x1, waiting for transfers between devices, search(): lax.ppermute(total.astype(BF16), 'far', [(k, k + 1) for k in range(0, blo...  8.78 us
    pallas_call x1, Pallas kernels, search(): pl.pallas_call(functools.partial(front_kernel, times, blocks, near, beams...  4.88 us
  transfers between devices with their start and end apart: 8, of which 3 were waited for; matrix products, arithmetic and copies ran while one was open for 0% of the time, Pallas kernels for 0%

profile of v12, /device:TPU:288, one launch (start us, length us, event | category | flops | bytes accessed | tf_op | source)
XLA Modules:
  0.0 171.3 jit_solution(2140081211035372552)
XLA Ops:
  0.0 4.9 %front.1 = bf16[128,8,256]{2,1,0:T(8,128)(2,1)} custom-call(bf16[256,2,1024]{2,1,0:T(2,128)(2,1)} %bitcast.15, s32[1,1024]{1,0:T(1,128)} %bitcast.16, bf16[512,512]{1,0:T(8,128)(2,1)} %constant.11.clone.table_ref), custom_call_target="tpu_custom_call" | custom-call | flops 2000000000 | bytes 4000000 | tf_op jit(solution)/shard_map/front/pallas_call | solution.py:168
  4.9 104.0 %all_to_all.10.own_ref = bf16[128,8,256]{2,1,0:T(8,128)(2,1)S(1)} all-to-all(bf16[128,8,256]{2,1,0:T(8,128)(2,1)} %front.1), channel_id=1, replica_groups=mesh['grp'=2,'far'=8,'near'=4,'beam'=4,'dm'=2] {'far','near','beam'}, dimensions={0} | all-to-all | bytes 1048576 | tf_op jit(solution)/shard_map/all_to_all | solution.py:177
  108.9 1.9 %collective-permute-start = (bf16[128,8,256]{2,1,0:T(8,128)(2,1)S(1)}, bf16[128,8,256]{2,1,0:T(8,128)(2,1)S(1)}, u32[]{:S(2)}, u32[]{:S(2)}) collective-permute-start(bf16[128,8,256]{2,1,0:T(8,128)(2,1)S(1)} %all_to_all.10.own_ref), channel_id=1, source_target_pairs={{0,1},{1,0},{2,3},{3,2},{4,5},{5,4},{6,7},{7,6},{8,9},{9,8},{10,11... | collective-permute-start | bytes 1572872 | tf_op jit(solution)/shard_map/ppermute | solution.py:187
  110.8 0.7 collective-permute-start.1
  111.5 0.1 pad_add_fusion.place_ref
  111.6 0.0 collective-permute-done.1
  111.6 0.1 copy.7
  111.8 23.5 %all_gather.3 = bf16[4,1,128,256]{3,2,1,0:T(8,128)(2,1)S(1)} all-gather(bf16[1,1,128,256]{3,2,1,0:T(8,128)(2,1)S(1)} %all_gather_reshape.3), channel_id=1, replica_groups=mesh['grp'=2,'far'=8,'near'=4,'beam'=4,'dm'=2] {'beam'}, dimensions={0}, use_global_device_ids=true | all-gather | bytes 327680 | tf_op jit(solution)/shard_map/all_gather | solution.py:186
  135.2 0.0 collective-permute-done.other_ref
  135.2 3.0 %dedisperse.1 = (f32[4,128,256]{2,1,0:T(8,128)S(1)}, f32[128,256]{1,0:T(8,128)S(1)}) custom-call(s32[2]{0:T(128)S(1)} %pad_add_fusion.place_ref, bf16[128,8,256]{2,1,0:T(8,128)(2,1)S(1)} %all_to_all.10.own_ref, bf16[128,8,256]{2,1,0:T(8,128)(2,1)S(1)} %collective-permute-done.other_ref, bf16[4,128,256]{2,1,0:T(8,128)(2,1)S(1)} %bitcast.12), custom_call_target="tpu_custom_call" | custom-call | flops 2000000000 | bytes 4000000 | tf_op jit(solution)/shard_map/dedisperse/pallas_call | solution.py:189
  138.3 1.3 collective-permute-start.2
  139.6 8.8 %collective-permute-done.2 = bf16[128,256]{1,0:T(8,128)(2,1)S(1)} collective-permute-done((bf16[128,256]{1,0:T(8,128)(2,1)S(1)}, bf16[128,256]{1,0:T(8,128)(2,1)S(1)}, u32[]{:S(2)}, u32[]{:S(2)}) %collective-permute-start.2) | collective-permute-done | bytes 65568 | tf_op jit(solution)/shard_map/ppermute | solution.py:204
  148.4 3.1 %collective-permute-start.3 = (bf16[128,256]{1,0:T(8,128)(2,1)S(1)}, bf16[128,256]{1,0:T(8,128)(2,1)S(1)}, u32[]{:S(2)}, u32[]{:S(2)}) collective-permute-start(bf16[128,256]{1,0:T(8,128)(2,1)S(1)} %fusion.3), channel_id=1, source_target_pairs={{32,96},{33,97},{34,98},{35,99},{36,100},{37,101},{38,102},{39,103... | collective-permute-start | bytes 196616 | tf_op jit(solution)/shard_map/ppermute | solution.py:207
  151.6 1.9 %collective-permute-done.3 = bf16[128,256]{1,0:T(8,128)(2,1)S(1)} collective-permute-done((bf16[128,256]{1,0:T(8,128)(2,1)S(1)}, bf16[128,256]{1,0:T(8,128)(2,1)S(1)}, u32[]{:S(2)}, u32[]{:S(2)}) %collective-permute-start.3) | collective-permute-done | bytes 65568 | tf_op jit(solution)/shard_map/ppermute | solution.py:207
  153.5 0.7 collective-permute-start.4
  154.1 0.0 collective-permute-done.4
  154.2 0.7 collective-permute-start.5
  154.9 1.3 collective-permute-start.6
  156.2 0.7 collective-permute-start.7
  156.9 1.2 collective-permute-done.6
  158.1 0.1 fusion.1
  158.1 0.1 add_convert_fusion
  158.2 12.1 %all_to_all.11.in_ref = bf16[4,128,256]{2,1,0:T(8,128)(2,1)S(1)} all-to-all(bf16[4,128,256]{2,1,0:T(8,128)(2,1)S(1)} %add_convert_fusion), channel_id=1, replica_groups=mesh['grp'=2,'far'=8,'near'=4,'beam'=4,'dm'=2] {'near'}, dimensions={0} | all-to-all | bytes 524288 | tf_op jit(solution)/shard_map/all_to_all | solution.py:214
  170.3 1.0 spread.1
  (11 shorter events, 0.2 us)
Async XLA Ops:
  4.9 105.9 %copy-start = (s32[1,256,128]{2,1,0:T(8,128)S(1)}, s32[1,256,128]{2,1,0:T(8,128)}, u32[]{:S(2)}) copy-start(s32[1,256,128]{2,1,0:T(8,128)} %param.6) | copy-start | bytes 393220
  108.9 26.4 %collective-permute-start = (bf16[128,8,256]{2,1,0:T(8,128)(2,1)S(1)}, bf16[128,8,256]{2,1,0:T(8,128)(2,1)S(1)}, u32[]{:S(2)}, u32[]{:S(2)}) collective-permute-start(bf16[128,8,256]{2,1,0:T(8,128)(2,1)S(1)} %all_to_all.10.own_ref), channel_id=1, source_target_pairs={{0,1},{1,0},{2,3},{3,2},{4,5},{5,4},{6,7},{7,6},{8,9},{9,8},{10,11... | collective-permute-start | bytes 1572872 | tf_op jit(solution)/shard_map/ppermute | solution.py:187
  110.8 0.8 collective-permute-start.1
  138.3 10.1 %collective-permute-start.2 = (bf16[128,256]{1,0:T(8,128)(2,1)S(1)}, bf16[128,256]{1,0:T(8,128)(2,1)S(1)}, u32[]{:S(2)}, u32[]{:S(2)}) collective-permute-start(bf16[128,256]{1,0:T(8,128)(2,1)S(1)} %convert_element_type.40), channel_id=1, source_target_pairs={{0,32},{64,96},{128,160},{192,224},{1,33},{65,97},{129,161},{193,2... | collective-permute-start | bytes 196616 | tf_op jit(solution)/shard_map/ppermute | solution.py:204
  148.4 5.0 %collective-permute-start.3 = (bf16[128,256]{1,0:T(8,128)(2,1)S(1)}, bf16[128,256]{1,0:T(8,128)(2,1)S(1)}, u32[]{:S(2)}, u32[]{:S(2)}) collective-permute-start(bf16[128,256]{1,0:T(8,128)(2,1)S(1)} %fusion.3), channel_id=1, source_target_pairs={{32,96},{33,97},{34,98},{35,99},{36,100},{37,101},{38,102},{39,103... | collective-permute-start | bytes 196616 | tf_op jit(solution)/shard_map/ppermute | solution.py:207
  153.5 0.7 collective-permute-start.4
  154.2 2.0 %collective-permute-start.5 = (bf16[128,256]{1,0:T(8,128)(2,1)S(1)}, bf16[128,256]{1,0:T(8,128)(2,1)S(1)}, u32[]{:S(2)}, u32[]{:S(2)}) collective-permute-start(bf16[128,256]{1,0:T(8,128)(2,1)S(1)} %add_convert_fusion.2), channel_id=1, source_target_pairs={{160,224},{161,225},{162,226},{163,227},{164,228},{165,229},{166,2... | collective-permute-start | bytes 196616 | tf_op jit(solution)/shard_map/ppermute | solution.py:210
  154.9 3.2 %collective-permute-start.6 = (bf16[128,256]{1,0:T(8,128)(2,1)S(1)}, bf16[128,256]{1,0:T(8,128)(2,1)S(1)}, u32[]{:S(2)}, u32[]{:S(2)}) collective-permute-start(bf16[128,256]{1,0:T(8,128)(2,1)S(1)} %fusion.3), channel_id=1, source_target_pairs={{32,64},{33,65},{34,66},{35,67},{36,68},{37,69},{38,70},{39,71},{4... | collective-permute-start | bytes 196616 | tf_op jit(solution)/shard_map/ppermute | solution.py:208
  156.2 1.8 %collective-permute-start.7 = (bf16[128,256]{1,0:T(8,128)(2,1)S(1)}, bf16[128,256]{1,0:T(8,128)(2,1)S(1)}, u32[]{:S(2)}, u32[]{:S(2)}) collective-permute-start(bf16[128,256]{1,0:T(8,128)(2,1)S(1)} %add_convert_fusion.1), channel_id=1, source_target_pairs={{96,128},{160,192},{97,129},{161,193},{98,130},{162,194},{99,131},... | collective-permute-start | bytes 196616 | tf_op jit(solution)/shard_map/ppermute | solution.py:211

commit v13 on v12

--- a/solution.py
+++ b/solution.py
@@ -175,15 +175,11 @@
         name="front",
     )(voltages.reshape(rows // 2, 2, feeds), grid_feed.reshape(1, feeds), jnp.asarray(steering_table(GY)))
     own = lax.all_to_all(sent, ("far", "near", "beam"), split_axis=0, concat_axis=0, tiled=True)
-    share = near // columns
-    fetched = []
-    for j in range(share):
-        steps = [(n, x, (n + x * share + j) % near) for n in range(near) for x in range(columns)]
-        pairs = [(source * columns + x, n * columns + x) for n, x, source in steps]
-        fetched.append(lax.ppermute(delays, ("near", "beam"), pairs))
-    lags = jnp.concatenate(fetched).astype(BF16).reshape(share, peers, sub_local, trials)
-    lags = jnp.transpose(lags, (0, 3, 2, 1)).reshape(share, trials, subs)
-    lags = lax.all_gather(lags, "beam").reshape(near, trials, subs)
+    lags = delays.astype(BF16).reshape(peers, sub_local, trials)
+    lags = [jnp.transpose(lags, (2, 1, 0)).reshape(trials, subs)]
+    for j in range(1, near):
+        lags.append(lax.ppermute(lags[0], "near", [((n + j) % near, n) for n in range(near)]))
+    lags = jnp.stack(lags)
     other = lax.ppermute(own, "dm", [(0, 1), (1, 0)])
     place = jnp.stack([lax.axis_index("dm"), lax.axis_index("near")]).astype(jnp.int32)
     local, total = pl.pallas_call(

time: 172 us -> 168 us (0.977)
  blocking collectives: 140 us -> 122 us
  starting transfers between devices: 10.4 us -> 21.4 us
  waiting for transfers between devices: 11.8 us -> 13.7 us
    all_gather x1 -> x0, blocking collectives: 23.5 us -> none  [search(): lags = lax.all_gather(lags, 'beam').reshape(near, trials, subs)]
    ppermute x1 -> x3, starting transfers between devices: 0.67 us -> 10.7 us  [search(): lax.ppermute(lags[0], 'near', [((n + j) % near, n) for n in range(near)])]
    all_to_all x1, blocking collectives: 12.1 us -> 18.4 us  [search(): lax.all_to_all(cumulative, 'near', split_axis=0, concat_axis=0, tiled=True)]
    ppermute x1 -> x3, waiting for transfers between devices: 0.01 us -> 1.76 us  [search(): lax.ppermute(lags[0], 'near', [((n + j) % near, n) for n in range(near)])]
  transfers between devices with their start and end apart: 8 -> 10, of which waited for: 3 -> 5; matrix products, arithmetic and copies ran while one was open for 0% -> 0% of each run, Pallas kernels for 0% -> 0%
where the time goes in v13:
time: 168 us; the launch traced here: 167 us
  blocking collectives  122 us (73%)
  starting transfers between devices  21.4 us (13%)
  waiting for transfers between devices  13.7 us (8%)
  Pallas kernels  8.91 us (5%)
    all_to_all x1, blocking collectives, search(): lax.all_to_all(sent, ('far', 'near', 'beam'), split_axis=0, concat_axis=0...  104 us
    all_to_all x1, blocking collectives, search(): lax.all_to_all(cumulative, 'near', split_axis=0, concat_axis=0, tiled=True)  18.4 us
    ppermute x3, starting transfers between devices, search(): lax.ppermute(lags[0], 'near', [((n + j) % near, n) for n in range(near)])  10.7 us
    ppermute x1, waiting for transfers between devices, search(): lax.ppermute(total.astype(BF16), 'far', [(k, k + 1) for k in range(0, blo...  8.91 us
    pallas_call x1, Pallas kernels, search(): pl.pallas_call(functools.partial(front_kernel, times, blocks, near, beams...  4.88 us
    ppermute x1, starting transfers between devices, search(): before = lax.ppermute(known, 'far', [(1, 3)]).astype(F32)  4.2 us
  transfers between devices with their start and end apart: 10, of which 5 were waited for; matrix products, arithmetic and copies ran while one was open for 0% of the time, Pallas kernels for 0%

profile of v13, /device:TPU:288, one launch (start us, length us, event | category | flops | bytes accessed | tf_op | source)
XLA Modules:
  0.0 167.2 jit_solution(6818459339643169377)
XLA Ops:
  0.0 4.9 %front.1 = bf16[128,8,256]{2,1,0:T(8,128)(2,1)} custom-call(bf16[256,2,1024]{2,1,0:T(2,128)(2,1)} %bitcast.27, s32[1,1024]{1,0:T(1,128)} %bitcast.28, bf16[512,512]{1,0:T(8,128)(2,1)} %constant.11.clone.table_ref), custom_call_target="tpu_custom_call" | custom-call | flops 2000000000 | bytes 4000000 | tf_op jit(solution)/shard_map/front/pallas_call | solution.py:168
  4.9 104.0 %all_to_all.10.own_ref = bf16[128,8,256]{2,1,0:T(8,128)(2,1)S(1)} all-to-all(bf16[128,8,256]{2,1,0:T(8,128)(2,1)} %front.1), channel_id=1, replica_groups=mesh['grp'=2,'far'=8,'near'=4,'beam'=4,'dm'=2] {'far','near','beam'}, dimensions={0} | all-to-all | bytes 1048576 | tf_op jit(solution)/shard_map/all_to_all | solution.py:177
  108.9 1.9 %collective-permute-start = (bf16[128,8,256]{2,1,0:T(8,128)(2,1)S(1)}, bf16[128,8,256]{2,1,0:T(8,128)(2,1)S(1)}, u32[]{:S(2)}, u32[]{:S(2)}) collective-permute-start(bf16[128,8,256]{2,1,0:T(8,128)(2,1)S(1)} %all_to_all.10.own_ref), channel_id=1, source_target_pairs={{0,1},{1,0},{2,3},{3,2},{4,5},{5,4},{6,7},{7,6},{8,9},{9,8},{10,11... | collective-permute-start | bytes 1572872 | tf_op jit(solution)/shard_map/ppermute | solution.py:183
  110.8 0.1 copy.5
  111.0 2.7 %collective-permute-start.3 = (bf16[128,256]{1,0:T(8,128)(2,1)S(1)}, bf16[128,256]{1,0:T(8,128)(2,1)S(1)}, u32[]{:S(2)}, u32[]{:S(2)}) collective-permute-start(bf16[128,256]{1,0:T(8,128)(2,1)S(1)} %bitcast.21), channel_id=1, source_target_pairs={{24,0},{0,8},{8,16},{16,24},{25,1},{1,9},{9,17},{17,25},{26,2},{2,... | collective-permute-start | bytes 196616 | tf_op jit(solution)/shard_map/ppermute | solution.py:181
  113.7 3.1 %collective-permute-start.2 = (bf16[128,256]{1,0:T(8,128)(2,1)S(1)}, bf16[128,256]{1,0:T(8,128)(2,1)S(1)}, u32[]{:S(2)}, u32[]{:S(2)}) collective-permute-start(bf16[128,256]{1,0:T(8,128)(2,1)S(1)} %bitcast.22), channel_id=1, source_target_pairs={{16,0},{24,8},{0,16},{8,24},{17,1},{25,9},{1,17},{9,25},{18,2},{26... | collective-permute-start | bytes 196616 | tf_op jit(solution)/shard_map/ppermute | solution.py:181
  116.8 4.9 %collective-permute-start.1 = (bf16[128,256]{1,0:T(8,128)(2,1)S(1)}, bf16[128,256]{1,0:T(8,128)(2,1)S(1)}, u32[]{:S(2)}, u32[]{:S(2)}) collective-permute-start(bf16[128,256]{1,0:T(8,128)(2,1)S(1)} %bitcast.23), channel_id=1, source_target_pairs={{8,0},{16,8},{24,16},{0,24},{9,1},{17,9},{25,17},{1,25},{10,2},{18... | collective-permute-start | bytes 196616 | tf_op jit(solution)/shard_map/ppermute | solution.py:181
  121.7 0.1 pad_add_fusion.place_ref
  121.8 0.5 collective-permute-done.2
  122.3 1.3 collective-permute-done.1
  123.6 3.0 %dedisperse.1 = (f32[4,128,256]{2,1,0:T(8,128)S(1)}, f32[128,256]{1,0:T(8,128)S(1)}) custom-call(s32[2]{0:T(128)S(1)} %pad_add_fusion.place_ref, bf16[128,8,256]{2,1,0:T(8,128)(2,1)S(1)} %all_to_all.10.own_ref, bf16[128,8,256]{2,1,0:T(8,128)(2,1)S(1)} %collective-permute-done.other_ref, bf16[4,128,256]{2,1,0:T(8,128)(2,1)S(1)} %pad_maximum_fusion.lag_ref), custom_call_target="tpu_custom_call" | custom-call | flops 2000000000 | bytes 4000000 | tf_op jit(solution)/shard_map/dedisperse/pallas_call | solution.py:185
  126.7 1.3 collective-permute-start.4
  128.0 8.9 %collective-permute-done.4 = bf16[128,256]{1,0:T(8,128)(2,1)S(1)} collective-permute-done((bf16[128,256]{1,0:T(8,128)(2,1)S(1)}, bf16[128,256]{1,0:T(8,128)(2,1)S(1)}, u32[]{:S(2)}, u32[]{:S(2)}) %collective-permute-start.4) | collective-permute-done | bytes 65568 | tf_op jit(solution)/shard_map/ppermute | solution.py:200
  136.9 4.2 %collective-permute-start.5 = (bf16[128,256]{1,0:T(8,128)(2,1)S(1)}, bf16[128,256]{1,0:T(8,128)(2,1)S(1)}, u32[]{:S(2)}, u32[]{:S(2)}) collective-permute-start(bf16[128,256]{1,0:T(8,128)(2,1)S(1)} %fusion.3), channel_id=1, source_target_pairs={{32,96},{33,97},{34,98},{35,99},{36,100},{37,101},{38,102},{39,103... | collective-permute-start | bytes 196616 | tf_op jit(solution)/shard_map/ppermute | solution.py:203
  141.1 1.9 %collective-permute-done.5 = bf16[128,256]{1,0:T(8,128)(2,1)S(1)} collective-permute-done((bf16[128,256]{1,0:T(8,128)(2,1)S(1)}, bf16[128,256]{1,0:T(8,128)(2,1)S(1)}, u32[]{:S(2)}, u32[]{:S(2)}) %collective-permute-start.5) | collective-permute-done | bytes 65568 | tf_op jit(solution)/shard_map/ppermute | solution.py:203
  143.0 0.7 collective-permute-start.6
  143.8 0.7 collective-permute-start.7
  144.4 1.3 collective-permute-start.8
  145.8 0.7 collective-permute-start.9
  146.5 1.2 collective-permute-done.8
  147.6 0.1 fusion.1
  147.7 0.1 add_convert_fusion
  147.8 18.4 %all_to_all.11.in_ref = bf16[4,128,256]{2,1,0:T(8,128)(2,1)S(1)} all-to-all(bf16[4,128,256]{2,1,0:T(8,128)(2,1)S(1)} %add_convert_fusion), channel_id=1, replica_groups=mesh['grp'=2,'far'=8,'near'=4,'beam'=4,'dm'=2] {'near'}, dimensions={0} | all-to-all | bytes 524288 | tf_op jit(solution)/shard_map/all_to_all | solution.py:210
  166.1 1.0 spread.1
  (16 shorter events, 0.3 us)
Async XLA Ops:
  4.9 105.9 %copy-start = (s32[1,256,128]{2,1,0:T(8,128)S(1)}, s32[1,256,128]{2,1,0:T(8,128)}, u32[]{:S(2)}) copy-start(s32[1,256,128]{2,1,0:T(8,128)} %param.6) | copy-start | bytes 393220
  108.9 14.8 %collective-permute-start = (bf16[128,8,256]{2,1,0:T(8,128)(2,1)S(1)}, bf16[128,8,256]{2,1,0:T(8,128)(2,1)S(1)}, u32[]{:S(2)}, u32[]{:S(2)}) collective-permute-start(bf16[128,8,256]{2,1,0:T(8,128)(2,1)S(1)} %all_to_all.10.own_ref), channel_id=1, source_target_pairs={{0,1},{1,0},{2,3},{3,2},{4,5},{5,4},{6,7},{7,6},{8,9},{9,8},{10,11... | collective-permute-start | bytes 1572872 | tf_op jit(solution)/shard_map/ppermute | solution.py:183
  111.0 10.8 %collective-permute-start.3 = (bf16[128,256]{1,0:T(8,128)(2,1)S(1)}, bf16[128,256]{1,0:T(8,128)(2,1)S(1)}, u32[]{:S(2)}, u32[]{:S(2)}) collective-permute-start(bf16[128,256]{1,0:T(8,128)(2,1)S(1)} %bitcast.21), channel_id=1, source_target_pairs={{24,0},{0,8},{8,16},{16,24},{25,1},{1,9},{9,17},{17,25},{26,2},{2,... | collective-permute-start | bytes 196616 | tf_op jit(solution)/shard_map/ppermute | solution.py:181
  113.7 8.6 %collective-permute-start.2 = (bf16[128,256]{1,0:T(8,128)(2,1)S(1)}, bf16[128,256]{1,0:T(8,128)(2,1)S(1)}, u32[]{:S(2)}, u32[]{:S(2)}) collective-permute-start(bf16[128,256]{1,0:T(8,128)(2,1)S(1)} %bitcast.22), channel_id=1, source_target_pairs={{16,0},{24,8},{0,16},{8,24},{17,1},{25,9},{1,17},{9,25},{18,2},{26... | collective-permute-start | bytes 196616 | tf_op jit(solution)/shard_map/ppermute | solution.py:181
  116.8 6.8 %collective-permute-start.1 = (bf16[128,256]{1,0:T(8,128)(2,1)S(1)}, bf16[128,256]{1,0:T(8,128)(2,1)S(1)}, u32[]{:S(2)}, u32[]{:S(2)}) collective-permute-start(bf16[128,256]{1,0:T(8,128)(2,1)S(1)} %bitcast.23), channel_id=1, source_target_pairs={{8,0},{16,8},{24,16},{0,24},{9,1},{17,9},{25,17},{1,25},{10,2},{18... | collective-permute-start | bytes 196616 | tf_op jit(solution)/shard_map/ppermute | solution.py:181
  126.7 10.2 %collective-permute-start.4 = (bf16[128,256]{1,0:T(8,128)(2,1)S(1)}, bf16[128,256]{1,0:T(8,128)(2,1)S(1)}, u32[]{:S(2)}, u32[]{:S(2)}) collective-permute-start(bf16[128,256]{1,0:T(8,128)(2,1)S(1)} %convert_element_type.40), channel_id=1, source_target_pairs={{0,32},{64,96},{128,160},{192,224},{1,33},{65,97},{129,161},{193,2... | collective-permute-start | bytes 196616 | tf_op jit(solution)/shard_map/ppermute | solution.py:200
  136.9 6.1 %collective-permute-start.5 = (bf16[128,256]{1,0:T(8,128)(2,1)S(1)}, bf16[128,256]{1,0:T(8,128)(2,1)S(1)}, u32[]{:S(2)}, u32[]{:S(2)}) collective-permute-start(bf16[128,256]{1,0:T(8,128)(2,1)S(1)} %fusion.3), channel_id=1, source_target_pairs={{32,96},{33,97},{34,98},{35,99},{36,100},{37,101},{38,102},{39,103... | collective-permute-start | bytes 196616 | tf_op jit(solution)/shard_map/ppermute | solution.py:203
  143.0 0.7 collective-permute-start.6
  143.8 2.0 %collective-permute-start.7 = (bf16[128,256]{1,0:T(8,128)(2,1)S(1)}, bf16[128,256]{1,0:T(8,128)(2,1)S(1)}, u32[]{:S(2)}, u32[]{:S(2)}) collective-permute-start(bf16[128,256]{1,0:T(8,128)(2,1)S(1)} %add_convert_fusion.2), channel_id=1, source_target_pairs={{160,224},{161,225},{162,226},{163,227},{164,228},{165,229},{166,2... | collective-permute-start | bytes 196616 | tf_op jit(solution)/shard_map/ppermute | solution.py:206
  144.4 3.2 %collective-permute-start.8 = (bf16[128,256]{1,0:T(8,128)(2,1)S(1)}, bf16[128,256]{1,0:T(8,128)(2,1)S(1)}, u32[]{:S(2)}, u32[]{:S(2)}) collective-permute-start(bf16[128,256]{1,0:T(8,128)(2,1)S(1)} %fusion.3), channel_id=1, source_target_pairs={{32,64},{33,65},{34,66},{35,67},{36,68},{37,69},{38,70},{39,71},{4... | collective-permute-start | bytes 196616 | tf_op jit(solution)/shard_map/ppermute | solution.py:204
  145.8 1.8 %collective-permute-start.9 = (bf16[128,256]{1,0:T(8,128)(2,1)S(1)}, bf16[128,256]{1,0:T(8,128)(2,1)S(1)}, u32[]{:S(2)}, u32[]{:S(2)}) collective-permute-start(bf16[128,256]{1,0:T(8,128)(2,1)S(1)} %add_convert_fusion.1), channel_id=1, source_target_pairs={{96,128},{160,192},{97,129},{161,193},{98,130},{162,194},{99,131},... | collective-permute-start | bytes 196616 | tf_op jit(solution)/shard_map/ppermute | solution.py:207
